TPU v7x, 32 devices: a whole 2x2x4 slice. The times are simulated.
32 devices in a mesh: row: 8 (over z, y), col: 4 (over x, core).
Axes of the slice: x: 2, y: 2, z: 4, core: 2. Of those that a mesh axis runs over, the one named last changes fastest.
Arguments:
- object_slab: float32 [2, 2560, 1280], P(None, 'row', 'col'), may hold values from -5 to 5
- probe_field: float32 [2, 512, 512], replicated, may hold values from -5 to 5
- offsets: int32 [8, 4, 1, 2], P('row', 'col'), may hold values from 0 to 64
- counts: int32 [8, 4, 1, 512, 512], P('row', 'col'), may hold values from 0 to 399
Outputs:
- updated: float32 [2, 2560, 1280], P(None, 'row', 'col')
Inputs may be any that keep to these rules, and one draw needn't show every extreme that they name: Window offsets inside the widened tile of 576 cells a side; the window never leaves it.
All inputs are finite; a program needn't handle non-finite values.
Results may differ from a plain program's by a relative error of at most 0.0003.
Values sent between devices are 32-bit elements; how exact they have to be, the bound alone decides.
No kernel may reach another device: no remote copies, remote signals or barrier semaphores. Data moves between devices by JAX's collectives and lax.ppermute only.
A program may use at most 128 MiB of HBM per device.

v0:
```python
import functools
import math

import jax
import jax.numpy as jnp
import ml_dtypes
import numpy as np
from jax import lax
from jax.experimental import pallas as pl
from jax.experimental.pallas import tpu as pltpu
from jax.sharding import PartitionSpec as P

OVL = 128
HALF = 64
LANES = 128

EPSILON = 0.01
PHOTON_SCALE = 0.01
STEP_SIZE = 0.5
REGULAR = 1.0

F32 = jnp.float32
BF16 = jnp.bfloat16


def call(kernel, name, out_shapes, n_smem, args, scratch=(), flops=0):
    specs = [
        pl.BlockSpec(memory_space=pltpu.SMEM if i < n_smem else pltpu.VMEM)
        for i in range(len(args))
    ]
    return pl.pallas_call(
        kernel,
        name=name,
        out_shape=[jax.ShapeDtypeStruct(s, d) for s, d in out_shapes],
        in_specs=specs,
        out_specs=[pl.BlockSpec(memory_space=pltpu.VMEM) for _ in out_shapes],
        scratch_shapes=list(scratch),
        compiler_params=pltpu.CompilerParams(vmem_limit_bytes=56 * 1024 * 1024),
        cost_estimate=pl.CostEstimate(flops=flops, bytes_accessed=0, transcendentals=0)
        if flops
        else None,
    )(*args)


@functools.lru_cache(maxsize=None)
def tables(length):
    quarter = length // 4
    n = np.arange(quarter)[:, None]
    k = np.arange(quarter)[None, :]
    blocks = []
    for p in range(4):
        angle = 2.0 * np.pi * ((n * (4 * k + p)) % length) / length
        c = np.cos(angle) / math.sqrt(length)
        s = np.sin(angle) / math.sqrt(length)
        blocks.append(np.block([[c, -s], [s, c]]))
    blocks += [b.T for b in blocks]
    full = np.stack(blocks)
    high = full.astype(np.float32).astype(ml_dtypes.bfloat16)
    low = (full - high.astype(np.float64)).astype(np.float32).astype(ml_dtypes.bfloat16)
    return high, low


def split(x):
    high = x.astype(BF16)
    return high, (x - high.astype(F32)).astype(BF16)


def dot(a, b):
    return lax.dot_general(a, b, (((1,), (0,)), ((), ())), preferred_element_type=F32)


def mix_forward(x):
    (x0r, x0i), (x1r, x1i), (x2r, x2i), (x3r, x3i) = x
    ar, ai, br, bi = x0r + x2r, x0i + x2i, x0r - x2r, x0i - x2i
    cr, ci, dr, di = x1r + x3r, x1i + x3i, x1r - x3r, x1i - x3i
    return [(ar + cr, ai + ci), (br + di, bi - dr), (ar - cr, ai - ci), (br - di, bi + dr)]


def mix_inverse(x):
    (x0r, x0i), (x1r, x1i), (x2r, x2i), (x3r, x3i) = x
    ar, ai, br, bi = x0r + x2r, x0i + x2i, x0r - x2r, x0i - x2i
    cr, ci, dr, di = x1r + x3r, x1i + x3i, x1r - x3r, x1i - x3i
    return [(ar + cr, ai + ci), (br - di, bi + dr), (ar - cr, ai - ci), (br + di, bi - dr)]


def lane_iota(shape):
    return lax.broadcasted_iota(jnp.int32, shape, len(shape) - 1)


def row_iota(shape):
    return lax.broadcasted_iota(jnp.int32, shape, len(shape) - 2)


def turn(x):
    return pltpu.roll(x, HALF, len(x.shape) - 1)


def pack_kernel(obj, north, south, west, east):
    rows, cols = obj.shape[1:]
    first = lane_iota((OVL, LANES)) < HALF
    for out, base in ((north, 0), (south, rows - OVL)):
        for c in range(2):
            out[:, c * 256 : c * 256 + 256] = obj[c, base : base + OVL, 0:256]
        out[:, 512 + 0 : 512 + HALF] = obj[0, base : base + OVL, 256:cols]
        out[:, 512 + HALF : 640] = obj[1, base : base + OVL, 256:cols]
    for c in range(2):
        west[c] = turn(obj[c, :, 0:128])
        east[c] = obj[c, :, cols - OVL : cols]


def corner_kernel(north, south, west, east):
    for base, halo in ((0, north), (OVL, south)):
        for c in range(2):
            west[c, base : base + OVL, :] = turn(halo[:, c * 256 : c * 256 + 128])
            tail = halo[:, 512 + c * HALF : 512 + c * HALF + HALF]
            east[c, base : base + OVL, 0:HALF] = halo[:, c * 256 + 192 : c * 256 + 256]
            east[c, base : base + OVL, HALF:128] = tail


def ready_kernel(offs, probe, counts, rolled, measured, wide):
    size = probe.shape[-1]
    quarter = size // 4
    u = offs[0]
    v = offs[1]
    for c in range(2):
        for t in range(4):
            cols = slice(t * quarter, (t + 1) * quarter)
            wide[c, t, 0:HALF, :] = probe[c, size - HALF : size, cols]
            wide[c, t, HALF : HALF + size, :] = probe[c, :, cols]
        for base in range(0, size, HALF):
            rows = pl.ds(HALF - u + base, HALF)
            piece = jnp.concatenate([wide[c, t, rows, :] for t in range(4)], axis=1)
            rolled[c, base : base + HALF, :] = pltpu.roll(piece, v, 1)
    r = row_iota((size, size))
    k = lane_iota((size, size))
    order = jnp.where(r == 4 * (k % quarter) + k // quarter, 1.0, 0.0).astype(BF16)
    for t in range(4):
        wide[0, t, 0:size, :] = counts[:, t * quarter : (t + 1) * quarter].astype(F32)
    for p in range(4):
        rows = jnp.concatenate([wide[0, t, pl.ds(p, quarter, stride=4), :] for t in range(4)], axis=1)
        high = jnp.floor(rows * (1.0 / 256.0))
        low = rows - 256.0 * high
        moved = 256.0 * dot(high.astype(BF16), order) + dot(low.astype(BF16), order)
        measured[p * quarter : (p + 1) * quarter, :] = jnp.sqrt(moved * PHOTON_SCALE)


def main_kernel(
    offs, obj, north, south, west, east, wcorner, ecorner, rolled, measured, high, low,
    own, nblock, sblock, wedge, eedge, wcorn, ecorn, fr, fi,
):
    size = rolled.shape[-1]
    quarter = size // 4
    cells = obj.shape[1]
    u = offs[0]
    v = offs[1]

    def pieces(c, part, base, count):
        lane = lane_iota((count, LANES))
        if part == "own":
            tiles = [obj[c, base : base + count, 0:128], obj[c, base : base + count, 128:256]]
            last = obj[c, base : base + count, 256:cells]
            last = jnp.concatenate([last, last], axis=1)
            w = west[c, base : base + count, :]
            e = east[c, base : base + count, :]
        else:
            ref, start = (north, base) if part == "n" else (south, base)
            tiles = [ref[start : start + count, c * 256 + 128 * t : c * 256 + 128 * t + 128] for t in range(2)]
            last = ref[start : start + count, 512:640]
            if c == 1:
                last = turn(last)
            start = start + (0 if part == "n" else OVL)
            w = wcorner[c, start : start + count, :]
            e = ecorner[c, start : start + count, :]
        return [jnp.where(lane < v, e, w), tiles[0], tiles[1], jnp.where(lane < HALF, last, e)]

    def patch(c, slot, count):
        if slot < HALF:
            row = row_iota((count, LANES)) + slot
            a = pieces(c, "n", slot, count)
            b = pieces(c, "s", slot + HALF, count)
            return [jnp.where(row < u, y, x) for x, y in zip(a, b)]
        if slot < OVL:
            return pieces(c, "n", slot, count)
        if slot < OVL + cells:
            return pieces(c, "own", slot - OVL, count)
        return pieces(c, "s", slot - OVL - cells, count)

    step = 64
    for base in range(0, size, step):
        rows = slice(base, base + step)
        orr, oi = patch(0, base, step), patch(1, base, step)
        exits = []
        for q in range(4):
            cols = slice(q * quarter, (q + 1) * quarter)
            pr, pi = rolled[0, rows, cols], rolled[1, rows, cols]
            exits.append((pr * orr[q] - pi * oi[q], pr * oi[q] + pi * orr[q]))
        for p, (yr, yi) in enumerate(mix_forward(exits)):
            a, b = split(jnp.concatenate([yr, yi], axis=1))
            z = dot(a, high[p]) + dot(a, low[p]) + dot(b, high[p])
            cols = slice(p * quarter, (p + 1) * quarter)
            fr[rows, cols] = z[:, :quarter]
            fi[rows, cols] = z[:, quarter:]

    for cb in range(4):
        cols = slice(cb * quarter, (cb + 1) * quarter)
        quads = [
            (fr[q * quarter : (q + 1) * quarter, cols], fi[q * quarter : (q + 1) * quarter, cols])
            for q in range(4)
        ]
        backs = []
        for p, (yr, yi) in enumerate(mix_forward(quads)):
            a, b = split(jnp.concatenate([yr, yi], axis=0))
            z = dot(high[4 + p], a) + dot(low[4 + p], a) + dot(high[4 + p], b)
            zr, zi = z[:quarter], z[quarter:]
            m = measured[p * quarter : (p + 1) * quarter, cols]
            factor = 1.0 - m * lax.rsqrt(zr * zr + zi * zi + EPSILON)
            a, b = split(jnp.concatenate([factor * zr, factor * zi], axis=0))
            z = dot(high[p], a) + dot(low[p], a) + dot(high[p], b)
            backs.append((z[:quarter], z[quarter:]))
        for q, (xr, xi) in enumerate(mix_inverse(backs)):
            fr[q * quarter : (q + 1) * quarter, cols] = xr
            fi[q * quarter : (q + 1) * quarter, cols] = xi

    for base in range(0, size, step):
        rows = slice(base, base + step)
        outs = []
        for p in range(4):
            cols = slice(p * quarter, (p + 1) * quarter)
            a, b = split(jnp.concatenate([fr[rows, cols], fi[rows, cols]], axis=1))
            z = dot(a, high[4 + p]) + dot(a, low[4 + p]) + dot(b, high[4 + p])
            outs.append((z[:, :quarter], z[:, quarter:]))
        grads = ([], [])
        for q, (br, bi) in enumerate(mix_inverse(outs)):
            cols = slice(q * quarter, (q + 1) * quarter)
            pr, pi = rolled[0, rows, cols], rolled[1, rows, cols]
            grads[0].append(pr * br + pi * bi)
            grads[1].append(pr * bi - pi * br)
        lane = lane_iota((step, LANES))
        for c in range(2):
            g = grads[c]
            wout = turn(jnp.where(lane >= v, g[0], 0.0))
            eout = turn(jnp.where(lane < HALF, jnp.where(lane < v, g[0], 0.0), g[3]))
            if OVL <= base < OVL + cells:
                o = base - OVL
                own[c, o : o + step, 0:128] = g[1]
                own[c, o : o + step, 128:256] = g[2]
                own[c, o : o + step, 256:cells] = g[3][:, : cells - 256]
                wedge[c, o : o + step, :] = wout
                eedge[c, o : o + step, :] = eout
                continue
            row = row_iota((step, LANES)) + base
            sends = []
            if base < OVL:
                sends.append((nblock, 0, base, row >= u if base < HALF else None))
            if base < HALF:
                sends.append((sblock, OVL, base + HALF, row < u))
            if base >= OVL + cells:
                sends.append((sblock, OVL, base - OVL - cells, None))
            for block, off, o, keep in sends:
                put = (lambda x: x) if keep is None else (lambda x: jnp.where(keep, x, 0.0))
                block[c, o : o + step, 0:128] = put(g[1])
                block[c, o : o + step, 128:256] = put(g[2])
                block[c, o : o + step, 256:384] = put(g[3])
                wcorn[c, off + o : off + o + step, :] = put(wout)
                ecorn[c, off + o : off + o + step, :] = put(eout)


def send_kernel(nblock, sblock, fromw, frome, north, south):
    first = lane_iota((OVL, LANES)) < HALF
    for base, block, out in ((0, nblock, north), (OVL, sblock, south)):
        last = []
        for c in range(2):
            fw = fromw[c, base : base + OVL, :]
            fe = frome[c, base : base + OVL, :]
            out[:, c * 256 : c * 256 + 128] = block[c, :, 0:128] + fw
            out[:, c * 256 + 128 : c * 256 + 256] = block[c, :, 128:256] + jnp.where(first, 0.0, fe)
            last.append(block[c, :, 256:384] + fe)
        out[:, 512:640] = jnp.where(first, last[0], turn(last[1]))


def light_kernel(info, probe, obj, own, fromw, frome, total, weight, pad, acc):
    size = probe.shape[-1]
    cells = own.shape[1]
    pad[...] = jnp.zeros(pad.shape, F32)
    for t in range(4):
        cols = slice(t * LANES, (t + 1) * LANES)
        x = probe[0, :, cols]
        y = probe[1, :, cols]
        pad[1 + t, OVL : OVL + size, :] = x * x + y * y
    acc[...] = jnp.zeros(acc.shape, F32)
    first = lane_iota((HALF, LANES)) < HALF
    for di in (0, -1, 1):
        for dj in (0, -1, 1):
            at = (di + 1) * 3 + (dj + 1)
            there = info[at, 2]
            u = info[at, 0]
            v = info[at, 1]
            start, count, put = {
                0: (2 * OVL - u, cells, 0),
                1: (OVL - u, OVL, cells - OVL),
                -1: (size + HALF - u, OVL, 0),
            }[di]
            seen = there.astype(F32)
            for r in range(0, count, HALF):
                rows = pl.ds(start + r, HALF)
                to = slice(put + r, put + r + HALF)
                lo, hi, shift = {0: (1, 5, 384 + v), -1: (4, 6, lax.rem(192 + v, 256)), 1: (0, 2, 128 + v)}[dj]
                x = pltpu.roll(jnp.concatenate([pad[t, rows, :] for t in range(lo, hi)], axis=1), shift, 1)
                if dj == 0:
                    x = x[:, 0:384]
                    acc[to, :] += x * seen
                    continue
                if dj == -1:
                    x = x[:, 0:128]
                    acc[to, 0:128] += x * seen
                    continue
                x = turn(x[:, 0:128]) * seen
                acc[to, 128:256] += jnp.where(first, 0.0, x)
                acc[to, 256:384] += x
    for r in range(0, cells, HALF):
        rows = slice(r, r + HALF)
        for c in range(2):
            fe = frome[c, rows, :]
            total[c, rows, 0:128] = own[c, rows, 0:128] + fromw[c, rows, :]
            total[c, rows, 128:256] = own[c, rows, 128:256] + jnp.where(first, 0.0, fe)
            total[c, rows, 256:cells] = own[c, rows, 256:cells] + fe[:, : cells - 256]
        weight[rows, :] = STEP_SIZE / (acc[rows, 0:cells] + REGULAR)


def final_kernel(obj, total, weight, fromn, froms, updated):
    cells = obj.shape[1]
    for r in range(0, cells, HALF):
        rows = slice(r, r + HALF)
        for c in range(2):
            g = [total[c, rows, 0:128], total[c, rows, 128:256], total[c, rows, 256:cells]]
            adds = []
            if r < OVL:
                adds.append((fromn, r))
            if r >= cells - OVL:
                adds.append((froms, r - cells + OVL))
            for ref, o in adds:
                src = slice(o, o + HALF)
                g[0] = g[0] + ref[src, c * 256 : c * 256 + 128]
                g[1] = g[1] + ref[src, c * 256 + 128 : c * 256 + 256]
                g[2] = g[2] + ref[src, 512 + c * HALF : 512 + c * HALF + HALF]
            for t, x in enumerate(g):
                cols = slice(128 * t, min(128 * t + 128, cells))
                updated[c, rows, cols] = obj[c, rows, cols] - x * weight[rows, cols]


def routes(axis):
    count = lax.axis_size(axis)
    up = [(i, i - 1) for i in range(1, count)]
    down = [(i, i + 1) for i in range(count - 1)]
    return up, down


def local(object_slab, probe_field, offsets, counts):
    cells = object_slab.shape[1]
    size = probe_field.shape[-1]
    up, down = routes("row")
    left, right = routes("col")
    offs = offsets.reshape(2)
    table_high, table_low = tables(size)
    high, low = jnp.asarray(table_high), jnp.asarray(table_low)

    north, south, west, east = call(
        pack_kernel,
        "pack",
        [((OVL, 640), F32), ((OVL, 640), F32), ((2, cells, OVL), F32), ((2, cells, OVL), F32)],
        0,
        [object_slab],
    )
    from_south = lax.ppermute(north, "row", up)
    from_north = lax.ppermute(south, "row", down)
    from_east = lax.ppermute(west, "col", left)
    from_west = lax.ppermute(east, "col", right)

    mine = jnp.concatenate([offs, jnp.ones((1,), jnp.int32)])
    above = lax.ppermute(mine, "row", down)
    below = lax.ppermute(mine, "row", up)
    column = jnp.stack([above, mine, below])
    lefts = lax.ppermute(column, "col", right)
    rights = lax.ppermute(column, "col", left)
    info = jnp.stack([lefts, column, rights], axis=1).reshape(9, 3)

    rolled, measured = call(
        ready_kernel,
        "ready",
        [((2, size, size), F32), ((size, size), F32)],
        1,
        [offs, probe_field, counts.reshape(size, size)],
        scratch=[pltpu.VMEM((2, 4, size + HALF, LANES), F32)],
        flops=20_000_000_000,
    )
    wcorner_out, ecorner_out = call(
        corner_kernel,
        "corner",
        [((2, 2 * OVL, OVL), F32), ((2, 2 * OVL, OVL), F32)],
        0,
        [from_north, from_south],
    )
    ecorner = lax.ppermute(wcorner_out, "col", left)
    wcorner = lax.ppermute(ecorner_out, "col", right)

    own, nblock, sblock, wedge, eedge, wcorn, ecorn = call(
        main_kernel,
        "main",
        [
            ((2, cells, cells), F32),
            ((2, OVL, 384), F32),
            ((2, OVL, 384), F32),
            ((2, cells, OVL), F32),
            ((2, cells, OVL), F32),
            ((2, 2 * OVL, OVL), F32),
            ((2, 2 * OVL, OVL), F32),
        ],
        1,
        [
            offs,
            object_slab,
            from_north,
            from_south,
            from_west,
            from_east,
            wcorner,
            ecorner,
            rolled,
            measured,
            high,
            low,
        ],
        scratch=[pltpu.VMEM((size, size), F32), pltpu.VMEM((size, size), F32)],
        flops=5_000_000_000,
    )
    corner_e = lax.ppermute(wcorn, "col", left)
    corner_w = lax.ppermute(ecorn, "col", right)
    edge_e = lax.ppermute(wedge, "col", left)
    edge_w = lax.ppermute(eedge, "col", right)
    nsend, ssend = call(
        send_kernel,
        "send",
        [((OVL, 640), F32), ((OVL, 640), F32)],
        0,
        [nblock, sblock, corner_w, corner_e],
    )
    grad_s = lax.ppermute(nsend, "row", up)
    grad_n = lax.ppermute(ssend, "row", down)
    total, weight = call(
        light_kernel,
        "light",
        [((2, cells, cells), F32), ((cells, cells), F32)],
        1,
        [info, probe_field, object_slab, own, edge_w, edge_e],
        scratch=[pltpu.VMEM((6, size + 2 * OVL, LANES), F32), pltpu.VMEM((cells, 384), F32)],
        flops=10_000_000_000,
    )
    (updated,) = call(
        final_kernel,
        "final",
        [((2, cells, cells), F32)],
        0,
        [object_slab, total, weight, grad_n, grad_s],
    )
    return updated


def solution(mesh):
    return jax.shard_map(
        local,
        mesh=mesh,
        in_specs=(
            P(None, "row", "col"),
            P(),
            P("row", "col", None, None),
            P("row", "col", None, None, None),
        ),
        out_specs=P(None, "row", "col"),
        check_vma=False,
    )
```

profile of v0, /device:TPU:27, one launch (start us, length us, event | category | flops | bytes accessed | tf_op | source)
XLA Modules:
  0.0 110.0 jit_solution(16179290670322493354)
XLA Ops:
  0.0 2.5 %pack.1 = (f32[128,640]{1,0:T(8,128)}, f32[128,640]{1,0:T(8,128)}, f32[2,320,128]{2,1,0:T(8,128)}, f32[2,320,128]{2,1,0:T(8,128)}) custom-call(f32[2,320,320]{2,1,0:T(8,128)} %obj.7), custom_call_target="tpu_custom_call" | custom-call | tf_op jit(solution)/shard_map/pack/pallas_call | solution.py:31
  2.5 3.1 %collective-permute-start.4 = (f32[128,640]{1,0:T(8,128)}, f32[128,640]{1,0:T(8,128)S(1)}, u32[]{:S(2)}, u32[]{:S(2)}) collective-permute-start(f32[128,640]{1,0:T(8,128)} %get-tuple-element.24), channel_id=1, source_target_pairs={{0,4},{4,8},{8,12},{12,16},{16,20},{20,24},{24,28},{1,5},{5,9},{9,... | collective-permute-start | bytes 983048 | tf_op jit(solution)/shard_map/ppermute | solution.py:375
  5.7 3.0 %collective-permute-start.5 = (f32[128,640]{1,0:T(8,128)}, f32[128,640]{1,0:T(8,128)S(1)}, u32[]{:S(2)}, u32[]{:S(2)}) collective-permute-start(f32[128,640]{1,0:T(8,128)} %get-tuple-element.25), channel_id=1, source_target_pairs={{4,0},{8,4},{12,8},{16,12},{20,16},{24,20},{28,24},{5,1},{9,5},{13... | collective-permute-start | bytes 983048 | tf_op jit(solution)/shard_map/ppermute | solution.py:374
  8.7 1.3 %collective-permute-start.6 = (f32[2,320,128]{2,1,0:T(8,128)}, f32[2,320,128]{2,1,0:T(8,128)S(1)}, u32[]{:S(2)}, u32[]{:S(2)}) collective-permute-start(f32[2,320,128]{2,1,0:T(8,128)} %get-tuple-element.26), channel_id=1, source_target_pairs={{0,1},{1,2},{2,3},{4,5},{5,6},{6,7},{8,9},{9,10},{10,11},{12,13},{... | collective-permute-start | bytes 983048 | tf_op jit(solution)/shard_map/ppermute | solution.py:377
  10.0 3.8 %collective-permute-start.7 = (f32[2,320,128]{2,1,0:T(8,128)}, f32[2,320,128]{2,1,0:T(8,128)S(1)}, u32[]{:S(2)}, u32[]{:S(2)}) collective-permute-start(f32[2,320,128]{2,1,0:T(8,128)} %get-tuple-element.27), channel_id=1, source_target_pairs={{1,0},{2,1},{3,2},{5,4},{6,5},{7,6},{9,8},{10,9},{11,10},{13,12},{... | collective-permute-start | bytes 983048 | tf_op jit(solution)/shard_map/ppermute | solution.py:376
  13.8 0.3 collective-permute-done.4.north
  14.1 0.0 copy-start
  14.1 8.0 %collective-permute-done.5.south = f32[128,640]{1,0:T(8,128)S(1)} collective-permute-done((f32[128,640]{1,0:T(8,128)}, f32[128,640]{1,0:T(8,128)S(1)}, u32[]{:S(2)}, u32[]{:S(2)}) %collective-permute-start.5) | collective-permute-done | bytes 327712 | tf_op jit(solution)/shard_map/ppermute | solution.py:374
  22.2 0.0 copy-done
  22.2 0.0 copy-start.1
  22.2 0.7 copy-done.1
  22.9 2.1 %corner.1 = (f32[2,256,128]{2,1,0:T(8,128)}, f32[2,256,128]{2,1,0:T(8,128)}) custom-call(f32[128,640]{1,0:T(8,128)} %copy-done, f32[128,640]{1,0:T(8,128)} %copy-done.1), custom_call_target="tpu_custom_call" | custom-call | tf_op jit(solution)/shard_map/corner/pallas_call | solution.py:31
  25.0 1.3 %collective-permute-start.8 = (f32[2,256,128]{2,1,0:T(8,128)}, f32[2,256,128]{2,1,0:T(8,128)S(1)}, u32[]{:S(2)}, u32[]{:S(2)}) collective-permute-start(f32[2,256,128]{2,1,0:T(8,128)} %get-tuple-element.28), channel_id=1, source_target_pairs={{0,1},{1,2},{2,3},{4,5},{5,6},{6,7},{8,9},{9,10},{10,11},{12,13},{... | collective-permute-start | bytes 786440 | tf_op jit(solution)/shard_map/ppermute | solution.py:404
  26.3 3.0 %collective-permute-start.9 = (f32[2,256,128]{2,1,0:T(8,128)}, f32[2,256,128]{2,1,0:T(8,128)S(1)}, u32[]{:S(2)}, u32[]{:S(2)}) collective-permute-start(f32[2,256,128]{2,1,0:T(8,128)} %get-tuple-element.29), channel_id=1, source_target_pairs={{1,0},{2,1},{3,2},{5,4},{6,5},{7,6},{9,8},{10,9},{11,10},{13,12},{... | collective-permute-start | bytes 786440 | tf_op jit(solution)/shard_map/ppermute | solution.py:403
  29.3 5.2 %ready.1 = (f32[2,512,512]{2,1,0:T(8,128)}, f32[512,512]{1,0:T(8,128)}) custom-call(s32[2]{0:T(128)} %bitcast.12, f32[2,512,512]{2,1,0:T(8,128)} %probe.3, s32[512,512]{1,0:T(8,128)} %bitcast.17), custom_call_target="tpu_custom_call" | custom-call | flops 20000000000 | tf_op jit(solution)/shard_map/ready/pallas_call | solution.py:31
  34.6 0.0 collective-permute-done.6.west
  34.6 0.0 copy-start.9
  34.6 0.0 collective-permute-done.7.east
  34.6 0.0 copy-start.10
  34.6 0.0 collective-permute-done.8.wcorner
  34.6 0.0 copy-start.11
  34.6 0.0 collective-permute-done.9.ecorner
  34.6 0.0 copy-start.12
  34.6 0.7 copy-done.9
  35.3 0.1 copy-done.10
  35.4 0.1 copy-done.11
  35.5 0.1 copy-done.12
  35.6 0.0 copy-start.6
  35.6 15.1 %main.1 = (f32[2,320,320]{2,1,0:T(8,128)}, f32[2,128,384]{2,1,0:T(8,128)}, f32[2,128,384]{2,1,0:T(8,128)}, f32[2,320,128]{2,1,0:T(8,128)}, f32[2,320,128]{2,1,0:...) custom-call(s32[2]{0:T(128)} %bitcast.13, f32[2,320,320]{2,1,0:T(8,128)} %obj.7, f32[128,640]{1,0:T(8,128)} %copy-done, ...), custom_call_target="tpu_custom_call" | custom-call | flops 5000000000 | tf_op jit(solution)/shard_map/main/pallas_call | solution.py:31
  50.7 1.3 %collective-permute-start.12 = (f32[2,256,128]{2,1,0:T(8,128)}, f32[2,256,128]{2,1,0:T(8,128)S(1)}, u32[]{:S(2)}, u32[]{:S(2)}) collective-permute-start(f32[2,256,128]{2,1,0:T(8,128)} %get-tuple-element.39), channel_id=1, source_target_pairs={{0,1},{1,2},{2,3},{4,5},{5,6},{6,7},{8,9},{9,10},{10,11},{12,13},{... | collective-permute-start | bytes 786440 | tf_op jit(solution)/shard_map/ppermute | solution.py:437
  52.0 4.3 %collective-permute-start.13 = (f32[2,256,128]{2,1,0:T(8,128)}, f32[2,256,128]{2,1,0:T(8,128)S(1)}, u32[]{:S(2)}, u32[]{:S(2)}) collective-permute-start(f32[2,256,128]{2,1,0:T(8,128)} %get-tuple-element.40), channel_id=1, source_target_pairs={{1,0},{2,1},{3,2},{5,4},{6,5},{7,6},{9,8},{10,9},{11,10},{13,12},{... | collective-permute-start | bytes 786440 | tf_op jit(solution)/shard_map/ppermute | solution.py:436
  56.2 1.3 %collective-permute-start.10 = (f32[2,320,128]{2,1,0:T(8,128)}, f32[2,320,128]{2,1,0:T(8,128)S(1)}, u32[]{:S(2)}, u32[]{:S(2)}) collective-permute-start(f32[2,320,128]{2,1,0:T(8,128)} %get-tuple-element.33), channel_id=1, source_target_pairs={{0,1},{1,2},{2,3},{4,5},{5,6},{6,7},{8,9},{9,10},{10,11},{12,13},{... | collective-permute-start | bytes 983048 | tf_op jit(solution)/shard_map/ppermute | solution.py:439
  57.5 4.3 %collective-permute-start.11 = (f32[2,320,128]{2,1,0:T(8,128)}, f32[2,320,128]{2,1,0:T(8,128)S(1)}, u32[]{:S(2)}, u32[]{:S(2)}) collective-permute-start(f32[2,320,128]{2,1,0:T(8,128)} %get-tuple-element.34), channel_id=1, source_target_pairs={{1,0},{2,1},{3,2},{5,4},{6,5},{7,6},{9,8},{10,9},{11,10},{13,12},{... | collective-permute-start | bytes 983048 | tf_op jit(solution)/shard_map/ppermute | solution.py:438
  61.8 0.0 copy-done.6
  61.8 0.1 fusion
  61.9 1.9 %collective-permute-start = (s32[3]{0:T(128)S(1)}, s32[3]{0:T(128)S(1)}, u32[]{:S(2)}, u32[]{:S(2)}) collective-permute-start(s32[3]{0:T(128)S(1)} %get-tuple-element.46), channel_id=1, source_target_pairs={{0,4},{4,8},{8,12},{12,16},{16,20},{20,24},{24,28},{1,5},{5,9},{9,... | collective-permute-start | bytes 44 | tf_op jit(solution)/shard_map/ppermute | solution.py:380
  63.8 3.3 %collective-permute-done = s32[3]{0:T(128)S(1)} collective-permute-done((s32[3]{0:T(128)S(1)}, s32[3]{0:T(128)S(1)}, u32[]{:S(2)}, u32[]{:S(2)}) %collective-permute-start) | collective-permute-done | bytes 44 | tf_op jit(solution)/shard_map/ppermute | solution.py:380
  67.1 2.0 %collective-permute-start.1 = (s32[3]{0:T(128)S(1)}, s32[3]{0:T(128)S(1)}, u32[]{:S(2)}, u32[]{:S(2)}) collective-permute-start(s32[3]{0:T(128)S(1)} %get-tuple-element.46), channel_id=1, source_target_pairs={{4,0},{8,4},{12,8},{16,12},{20,16},{24,20},{28,24},{5,1},{9,5},{13... | collective-permute-start | bytes 44 | tf_op jit(solution)/shard_map/ppermute | solution.py:381
  69.1 2.3 %collective-permute-done.1 = s32[3]{0:T(128)S(1)} collective-permute-done((s32[3]{0:T(128)S(1)}, s32[3]{0:T(128)S(1)}, u32[]{:S(2)}, u32[]{:S(2)}) %collective-permute-start.1) | collective-permute-done | bytes 44 | tf_op jit(solution)/shard_map/ppermute | solution.py:381
  71.4 1.3 %collective-permute-start.2 = (s32[3,3]{1,0:T(4,128)S(1)}, s32[3,3]{1,0:T(4,128)S(1)}, u32[]{:S(2)}, u32[]{:S(2)}) collective-permute-start(s32[3,3]{1,0:T(4,128)S(1)} %get-tuple-element.44), channel_id=1, source_target_pairs={{0,1},{1,2},{2,3},{4,5},{5,6},{6,7},{8,9},{9,10},{10,11},{12,13},{... | collective-permute-start | bytes 116 | tf_op jit(solution)/shard_map/ppermute | solution.py:383
  72.7 5.3 %collective-permute-done.2 = s32[3,3]{1,0:T(4,128)S(1)} collective-permute-done((s32[3,3]{1,0:T(4,128)S(1)}, s32[3,3]{1,0:T(4,128)S(1)}, u32[]{:S(2)}, u32[]{:S(2)}) %collective-permute-start.2) | collective-permute-done | bytes 68 | tf_op jit(solution)/shard_map/ppermute | solution.py:383
  78.0 4.2 %collective-permute-start.3 = (s32[3,3]{1,0:T(4,128)S(1)}, s32[3,3]{1,0:T(4,128)S(1)}, u32[]{:S(2)}, u32[]{:S(2)}) collective-permute-start(s32[3,3]{1,0:T(4,128)S(1)} %get-tuple-element.44), channel_id=1, source_target_pairs={{1,0},{2,1},{3,2},{5,4},{6,5},{7,6},{9,8},{10,9},{11,10},{13,12},{... | collective-permute-start | bytes 116 | tf_op jit(solution)/shard_map/ppermute | solution.py:384
  82.2 0.8 collective-permute-done.3
  83.0 0.6 reshape.12.info
  83.7 0.0 collective-permute-done.12.fromw
  83.7 0.0 collective-permute-done.13.frome
  83.7 0.0 copy-start.5
  83.7 0.7 copy-done.4
  84.4 0.1 copy-done.5
  84.5 2.2 %send.1 = (f32[128,640]{1,0:T(8,128)}, f32[128,640]{1,0:T(8,128)}) custom-call(f32[2,128,384]{2,1,0:T(8,128)} %get-tuple-element.37.nblock, f32[2,128,384]{2,1,0:T(8,128)} %get-tuple-element.38.sblock, f32[2,256,128]{2,1,0:T(8,128)} %copy-done.4, f32[2,256,128]{2,1,0:T(8,128)} %copy-done.5), custom_call_target="tpu_custom_call" | custom-call | tf_op jit(solution)/shard_map/send/pallas_call | solution.py:31
  86.7 1.9 %collective-permute-start.14 = (f32[128,640]{1,0:T(8,128)}, f32[128,640]{1,0:T(8,128)S(1)}, u32[]{:S(2)}, u32[]{:S(2)}) collective-permute-start(f32[128,640]{1,0:T(8,128)} %get-tuple-element.41), channel_id=1, source_target_pairs={{0,4},{4,8},{8,12},{12,16},{16,20},{20,24},{24,28},{1,5},{5,9},{9,... | collective-permute-start | bytes 983048 | tf_op jit(solution)/shard_map/ppermute | solution.py:448
  88.6 4.3 %collective-permute-start.15 = (f32[128,640]{1,0:T(8,128)}, f32[128,640]{1,0:T(8,128)S(1)}, u32[]{:S(2)}, u32[]{:S(2)}) collective-permute-start(f32[128,640]{1,0:T(8,128)} %get-tuple-element.42), channel_id=1, source_target_pairs={{4,0},{8,4},{12,8},{16,12},{20,16},{24,20},{28,24},{5,1},{9,5},{13... | collective-permute-start | bytes 983048 | tf_op jit(solution)/shard_map/ppermute | solution.py:447
  92.9 0.0 collective-permute-done.10.fromw
  92.9 0.0 copy-start.7
  92.9 0.0 collective-permute-done.11.frome
  92.9 0.0 copy-start.8
  92.9 0.7 copy-done.7
  93.6 0.1 copy-done.8
  93.7 5.0 %light.1 = (f32[2,320,320]{2,1,0:T(8,128)}, f32[320,320]{1,0:T(8,128)}) custom-call(s32[9,3]{1,0:T(8,128)} %reshape.12.info, f32[2,512,512]{2,1,0:T(8,128)} %probe.3, f32[2,320,320]{2,1,0:T(8,128)} %obj.7, f32[2,320,320]{2,1,0:T(8,128)} %get-tuple-element.32.own, f32[2,320,128]{2,1,0:T(8,128)} %copy-done.7, f32[2,320,128]{2,1,0:T(8,128)} %copy-done.8), custom_call_target="tpu_custom_call" | custom-call | flops 10000000000 | tf_op jit(solution)/shard_map/light/pallas_call | solution.py:31
  98.7 0.0 collective-permute-done.14.fromn
  98.7 7.6 %collective-permute-done.15.froms = f32[128,640]{1,0:T(8,128)S(1)} collective-permute-done((f32[128,640]{1,0:T(8,128)}, f32[128,640]{1,0:T(8,128)S(1)}, u32[]{:S(2)}, u32[]{:S(2)}) %collective-permute-start.15) | collective-permute-done | bytes 327712 | tf_op jit(solution)/shard_map/ppermute | solution.py:447
  106.3 0.0 copy-done.2
  106.3 0.8 copy-done.3
  107.1 2.9 %final.1 = f32[2,320,320]{2,1,0:T(8,128)} custom-call(f32[2,320,320]{2,1,0:T(8,128)} %obj.7, f32[2,320,320]{2,1,0:T(8,128)} %get-tuple-element.35.total, f32[320,320]{1,0:T(8,128)} %get-tuple-element.36.weight, f32[128,640]{1,0:T(8,128)} %copy-done.2, f32[128,640]{1,0:T(8,128)} %copy-done.3), custom_call_target="tpu_custom_call" | custom-call | tf_op jit(solution)/shard_map/final/pallas_call | solution.py:31
  (6 shorter events, 0.0 us)
Async XLA Ops:
  2.5 11.6 %collective-permute-start.4 = (f32[128,640]{1,0:T(8,128)}, f32[128,640]{1,0:T(8,128)S(1)}, u32[]{:S(2)}, u32[]{:S(2)}) collective-permute-start(f32[128,640]{1,0:T(8,128)} %get-tuple-element.24), channel_id=1, source_target_pairs={{0,4},{4,8},{8,12},{12,16},{16,20},{20,24},{24,28},{1,5},{5,9},{9,... | collective-permute-start | bytes 983048 | tf_op jit(solution)/shard_map/ppermute | solution.py:375
  5.7 16.5 %collective-permute-start.5 = (f32[128,640]{1,0:T(8,128)}, f32[128,640]{1,0:T(8,128)S(1)}, u32[]{:S(2)}, u32[]{:S(2)}) collective-permute-start(f32[128,640]{1,0:T(8,128)} %get-tuple-element.25), channel_id=1, source_target_pairs={{4,0},{8,4},{12,8},{16,12},{20,16},{24,20},{28,24},{5,1},{9,5},{13... | collective-permute-start | bytes 983048 | tf_op jit(solution)/shard_map/ppermute | solution.py:374
  8.7 25.9 %collective-permute-start.6 = (f32[2,320,128]{2,1,0:T(8,128)}, f32[2,320,128]{2,1,0:T(8,128)S(1)}, u32[]{:S(2)}, u32[]{:S(2)}) collective-permute-start(f32[2,320,128]{2,1,0:T(8,128)} %get-tuple-element.26), channel_id=1, source_target_pairs={{0,1},{1,2},{2,3},{4,5},{5,6},{6,7},{8,9},{9,10},{10,11},{12,13},{... | collective-permute-start | bytes 983048 | tf_op jit(solution)/shard_map/ppermute | solution.py:377
  10.0 24.6 %collective-permute-start.7 = (f32[2,320,128]{2,1,0:T(8,128)}, f32[2,320,128]{2,1,0:T(8,128)S(1)}, u32[]{:S(2)}, u32[]{:S(2)}) collective-permute-start(f32[2,320,128]{2,1,0:T(8,128)} %get-tuple-element.27), channel_id=1, source_target_pairs={{1,0},{2,1},{3,2},{5,4},{6,5},{7,6},{9,8},{10,9},{11,10},{13,12},{... | collective-permute-start | bytes 983048 | tf_op jit(solution)/shard_map/ppermute | solution.py:376
  14.1 8.0 %copy-start = (f32[128,640]{1,0:T(8,128)}, f32[128,640]{1,0:T(8,128)S(1)}, u32[]{:S(2)}) copy-start(f32[128,640]{1,0:T(8,128)S(1)} %collective-permute-done.4.north) | copy-start | bytes 983044
  22.2 0.7 copy-start.1
  25.0 9.6 %collective-permute-start.8 = (f32[2,256,128]{2,1,0:T(8,128)}, f32[2,256,128]{2,1,0:T(8,128)S(1)}, u32[]{:S(2)}, u32[]{:S(2)}) collective-permute-start(f32[2,256,128]{2,1,0:T(8,128)} %get-tuple-element.28), channel_id=1, source_target_pairs={{0,1},{1,2},{2,3},{4,5},{5,6},{6,7},{8,9},{9,10},{10,11},{12,13},{... | collective-permute-start | bytes 786440 | tf_op jit(solution)/shard_map/ppermute | solution.py:404
  26.3 8.3 %collective-permute-start.9 = (f32[2,256,128]{2,1,0:T(8,128)}, f32[2,256,128]{2,1,0:T(8,128)S(1)}, u32[]{:S(2)}, u32[]{:S(2)}) collective-permute-start(f32[2,256,128]{2,1,0:T(8,128)} %get-tuple-element.29), channel_id=1, source_target_pairs={{1,0},{2,1},{3,2},{5,4},{6,5},{7,6},{9,8},{10,9},{11,10},{13,12},{... | collective-permute-start | bytes 786440 | tf_op jit(solution)/shard_map/ppermute | solution.py:403
  34.6 0.7 copy-start.9
  34.6 0.8 copy-start.10
  34.6 0.9 copy-start.11
  34.6 1.0 copy-start.12
  35.6 26.2 %copy-start.6 = (s32[1,1,1,2]{3,2,1,0:T(1,128)S(1)}, s32[1,1,1,2]{3,2,1,0:T(1,128)}, u32[]{:S(2)}) copy-start(s32[1,1,1,2]{3,2,1,0:T(1,128)} %param.8) | copy-start | bytes 28
  50.7 33.0 %collective-permute-start.12 = (f32[2,256,128]{2,1,0:T(8,128)}, f32[2,256,128]{2,1,0:T(8,128)S(1)}, u32[]{:S(2)}, u32[]{:S(2)}) collective-permute-start(f32[2,256,128]{2,1,0:T(8,128)} %get-tuple-element.39), channel_id=1, source_target_pairs={{0,1},{1,2},{2,3},{4,5},{5,6},{6,7},{8,9},{9,10},{10,11},{12,13},{... | collective-permute-start | bytes 786440 | tf_op jit(solution)/shard_map/ppermute | solution.py:437
  52.0 31.7 %collective-permute-start.13 = (f32[2,256,128]{2,1,0:T(8,128)}, f32[2,256,128]{2,1,0:T(8,128)S(1)}, u32[]{:S(2)}, u32[]{:S(2)}) collective-permute-start(f32[2,256,128]{2,1,0:T(8,128)} %get-tuple-element.40), channel_id=1, source_target_pairs={{1,0},{2,1},{3,2},{5,4},{6,5},{7,6},{9,8},{10,9},{11,10},{13,12},{... | collective-permute-start | bytes 786440 | tf_op jit(solution)/shard_map/ppermute | solution.py:436
  56.2 36.6 %collective-permute-start.10 = (f32[2,320,128]{2,1,0:T(8,128)}, f32[2,320,128]{2,1,0:T(8,128)S(1)}, u32[]{:S(2)}, u32[]{:S(2)}) collective-permute-start(f32[2,320,128]{2,1,0:T(8,128)} %get-tuple-element.33), channel_id=1, source_target_pairs={{0,1},{1,2},{2,3},{4,5},{5,6},{6,7},{8,9},{9,10},{10,11},{12,13},{... | collective-permute-start | bytes 983048 | tf_op jit(solution)/shard_map/ppermute | solution.py:439
  57.5 35.3 %collective-permute-start.11 = (f32[2,320,128]{2,1,0:T(8,128)}, f32[2,320,128]{2,1,0:T(8,128)S(1)}, u32[]{:S(2)}, u32[]{:S(2)}) collective-permute-start(f32[2,320,128]{2,1,0:T(8,128)} %get-tuple-element.34), channel_id=1, source_target_pairs={{1,0},{2,1},{3,2},{5,4},{6,5},{7,6},{9,8},{10,9},{11,10},{13,12},{... | collective-permute-start | bytes 983048 | tf_op jit(solution)/shard_map/ppermute | solution.py:438
  61.9 5.2 %collective-permute-start = (s32[3]{0:T(128)S(1)}, s32[3]{0:T(128)S(1)}, u32[]{:S(2)}, u32[]{:S(2)}) collective-permute-start(s32[3]{0:T(128)S(1)} %get-tuple-element.46), channel_id=1, source_target_pairs={{0,4},{4,8},{8,12},{12,16},{16,20},{20,24},{24,28},{1,5},{5,9},{9,... | collective-permute-start | bytes 44 | tf_op jit(solution)/shard_map/ppermute | solution.py:380
  67.1 4.3 %collective-permute-start.1 = (s32[3]{0:T(128)S(1)}, s32[3]{0:T(128)S(1)}, u32[]{:S(2)}, u32[]{:S(2)}) collective-permute-start(s32[3]{0:T(128)S(1)} %get-tuple-element.46), channel_id=1, source_target_pairs={{4,0},{8,4},{12,8},{16,12},{20,16},{24,20},{28,24},{5,1},{9,5},{13... | collective-permute-start | bytes 44 | tf_op jit(solution)/shard_map/ppermute | solution.py:381
  71.4 6.6 %collective-permute-start.2 = (s32[3,3]{1,0:T(4,128)S(1)}, s32[3,3]{1,0:T(4,128)S(1)}, u32[]{:S(2)}, u32[]{:S(2)}) collective-permute-start(s32[3,3]{1,0:T(4,128)S(1)} %get-tuple-element.44), channel_id=1, source_target_pairs={{0,1},{1,2},{2,3},{4,5},{5,6},{6,7},{8,9},{9,10},{10,11},{12,13},{... | collective-permute-start | bytes 116 | tf_op jit(solution)/shard_map/ppermute | solution.py:383
  78.0 5.0 %collective-permute-start.3 = (s32[3,3]{1,0:T(4,128)S(1)}, s32[3,3]{1,0:T(4,128)S(1)}, u32[]{:S(2)}, u32[]{:S(2)}) collective-permute-start(s32[3,3]{1,0:T(4,128)S(1)} %get-tuple-element.44), channel_id=1, source_target_pairs={{1,0},{2,1},{3,2},{5,4},{6,5},{7,6},{9,8},{10,9},{11,10},{13,12},{... | collective-permute-start | bytes 116 | tf_op jit(solution)/shard_map/ppermute | solution.py:384
  83.7 0.7 copy-start.4
  83.7 0.8 copy-start.5
  86.7 12.0 %collective-permute-start.14 = (f32[128,640]{1,0:T(8,128)}, f32[128,640]{1,0:T(8,128)S(1)}, u32[]{:S(2)}, u32[]{:S(2)}) collective-permute-start(f32[128,640]{1,0:T(8,128)} %get-tuple-element.41), channel_id=1, source_target_pairs={{0,4},{4,8},{8,12},{12,16},{16,20},{20,24},{24,28},{1,5},{5,9},{9,... | collective-permute-start | bytes 983048 | tf_op jit(solution)/shard_map/ppermute | solution.py:448
  88.6 17.7 %collective-permute-start.15 = (f32[128,640]{1,0:T(8,128)}, f32[128,640]{1,0:T(8,128)S(1)}, u32[]{:S(2)}, u32[]{:S(2)}) collective-permute-start(f32[128,640]{1,0:T(8,128)} %get-tuple-element.42), channel_id=1, source_target_pairs={{4,0},{8,4},{12,8},{16,12},{20,16},{24,20},{28,24},{5,1},{9,5},{13... | collective-permute-start | bytes 983048 | tf_op jit(solution)/shard_map/ppermute | solution.py:447
  92.9 0.7 copy-start.7
  92.9 0.8 copy-start.8
  98.7 7.6 %copy-start.2 = (f32[128,640]{1,0:T(8,128)}, f32[128,640]{1,0:T(8,128)S(1)}, u32[]{:S(2)}) copy-start(f32[128,640]{1,0:T(8,128)S(1)} %collective-permute-done.14.fromn) | copy-start | bytes 983044
  106.3 0.8 copy-start.3
where the time goes:
time: 111 us; the launch traced here: 110 us
  starting transfers between devices  42.3 us (38%)
  Pallas kernels  35 us (32%)
  waiting for transfers between devices  27.7 us (25%)
  local copies, waits for them, and re-layouts  4.73 us (4%)
    pallas_call x7, Pallas kernels, call(): pl.pallas_call(kernel, name=name, out_shape=[jax.ShapeDtypeStruct(s, d) f...  35 us
    ppermute x1, waiting for transfers between devices, local(): from_south = lax.ppermute(north, 'row', up)  8.01 us
    ppermute x1, waiting for transfers between devices, local(): grad_s = lax.ppermute(nsend, 'row', up)  7.6 us
    ppermute x1, waiting for transfers between devices, local(): lefts = lax.ppermute(column, 'col', right)  5.28 us
    ppermute x1, starting transfers between devices, local(): edge_e = lax.ppermute(wedge, 'col', left)  4.27 us
    ppermute x1, starting transfers between devices, local(): corner_e = lax.ppermute(wcorn, 'col', left)  4.27 us
    ppermute x1, starting transfers between devices, local(): grad_s = lax.ppermute(nsend, 'row', up)  4.26 us
    ppermute x1, starting transfers between devices, local(): rights = lax.ppermute(column, 'col', left)  4.24 us
  transfers between devices with their start and end apart: 16, of which 7 were waited for; matrix products, arithmetic and copies ran while one was open for 1% of the time, Pallas kernels for 11%

commit v1 on v0

--- a/solution.py
+++ b/solution.py
@@ -23,19 +23,23 @@
 BF16 = jnp.bfloat16
 
 
-def call(kernel, name, out_shapes, n_smem, args, scratch=(), flops=0):
+def call(kernel, out_shapes, args, smem=(), hbm_out=False, scratch=(), flops=0, limit=16):
     specs = [
-        pl.BlockSpec(memory_space=pltpu.SMEM if i < n_smem else pltpu.VMEM)
-        for i in range(len(args))
+        pl.BlockSpec(memory_space=pltpu.SMEM if i in smem else pltpu.VMEM) for i in range(len(args))
+    ]
+    args = [
+        x if i in smem else pltpu.with_memory_space_constraint(x, pltpu.VMEM)
+        for i, x in enumerate(args)
     ]
     return pl.pallas_call(
         kernel,
-        name=name,
-        out_shape=[jax.ShapeDtypeStruct(s, d) for s, d in out_shapes],
+        out_shape=[
+            jax.ShapeDtypeStruct(s, F32) if hbm_out else pltpu.VMEM(s, F32) for s in out_shapes
+        ],
         in_specs=specs,
         out_specs=[pl.BlockSpec(memory_space=pltpu.VMEM) for _ in out_shapes],
         scratch_shapes=list(scratch),
-        compiler_params=pltpu.CompilerParams(vmem_limit_bytes=56 * 1024 * 1024),
+        compiler_params=pltpu.CompilerParams(vmem_limit_bytes=limit * 1024 * 1024),
         cost_estimate=pl.CostEstimate(flops=flops, bytes_accessed=0, transcendentals=0)
         if flops
         else None,
@@ -95,9 +99,11 @@
     return pltpu.roll(x, HALF, len(x.shape) - 1)
 
 
-def pack_kernel(obj, north, south, west, east):
+def pack_kernel(offs, obj, north, south, west, east, mine):
     rows, cols = obj.shape[1:]
-    first = lane_iota((OVL, LANES)) < HALF
+    lane = lane_iota((8, LANES))
+    info = jnp.where(lane == 0, offs[0], jnp.where(lane == 1, offs[1], 1))
+    mine[...] = info.astype(F32)
     for out, base in ((north, 0), (south, rows - OVL)):
         for c in range(2):
             out[:, c * 256 : c * 256 + 256] = obj[c, base : base + OVL, 0:256]
@@ -108,16 +114,19 @@
         east[c] = obj[c, :, cols - OVL : cols]
 
 
-def corner_kernel(north, south, west, east):
-    for base, halo in ((0, north), (OVL, south)):
-        for c in range(2):
-            west[c, base : base + OVL, :] = turn(halo[:, c * 256 : c * 256 + 128])
-            tail = halo[:, 512 + c * HALF : 512 + c * HALF + HALF]
-            east[c, base : base + OVL, 0:HALF] = halo[:, c * 256 + 192 : c * 256 + 256]
-            east[c, base : base + OVL, HALF:128] = tail
-
-
-def ready_kernel(offs, probe, counts, rolled, measured, wide):
+def corner_kernel(north, south, above, mine, below, token, west, east):
+    for part, halo in ((0, north), (1, south)):
+        for c in range(2):
+            rows = slice((2 * c + part) * OVL, (2 * c + part) * OVL + OVL)
+            west[rows, :] = turn(halo[:, c * 256 : c * 256 + 128])
+            east[rows, 0:HALF] = halo[:, c * 256 + 192 : c * 256 + 256]
+            east[rows, HALF:128] = halo[:, 512 + c * HALF : 512 + c * HALF + HALF]
+    for out in (west, east):
+        for t, ref in enumerate((above, mine, below)):
+            out[4 * OVL + 8 * t : 4 * OVL + 8 * t + 8, :] = ref[...]
+
+
+def ready_kernel(offs, probe, counts, rolled, measured, token, wide):
     size = probe.shape[-1]
     quarter = size // 4
     u = offs[0]
@@ -131,6 +140,7 @@
             rows = pl.ds(HALF - u + base, HALF)
             piece = jnp.concatenate([wide[c, t, rows, :] for t in range(4)], axis=1)
             rolled[c, base : base + HALF, :] = pltpu.roll(piece, v, 1)
+    token[...] = jnp.zeros(token.shape, F32)
     r = row_iota((size, size))
     k = lane_iota((size, size))
     order = jnp.where(r == 4 * (k % quarter) + k // quarter, 1.0, 0.0).astype(BF16)
@@ -168,9 +178,9 @@
             last = ref[start : start + count, 512:640]
             if c == 1:
                 last = turn(last)
-            start = start + (0 if part == "n" else OVL)
-            w = wcorner[c, start : start + count, :]
-            e = ecorner[c, start : start + count, :]
+            start = start + (2 * c + (part == "s")) * OVL
+            w = wcorner[start : start + count, :]
+            e = ecorner[start : start + count, :]
         return [jnp.where(lane < v, e, w), tiles[0], tiles[1], jnp.where(lane < HALF, last, e)]
 
     def patch(c, slot, count):
@@ -278,7 +288,9 @@
         out[:, 512:640] = jnp.where(first, last[0], turn(last[1]))
 
 
-def light_kernel(info, probe, obj, own, fromw, frome, total, weight, pad, acc):
+def light_kernel(
+    wcorner, ecorner, above, mine, below, probe, own, fromw, frome, total, weight, pad, acc
+):
     size = probe.shape[-1]
     cells = own.shape[1]
     pad[...] = jnp.zeros(pad.shape, F32)
@@ -289,18 +301,22 @@
         pad[1 + t, OVL : OVL + size, :] = x * x + y * y
     acc[...] = jnp.zeros(acc.shape, F32)
     first = lane_iota((HALF, LANES)) < HALF
+    unit = row_iota((8, LANES)) == 0
+    lane = lane_iota((8, LANES))
     for di in (0, -1, 1):
         for dj in (0, -1, 1):
-            at = (di + 1) * 3 + (dj + 1)
-            there = info[at, 2]
-            u = info[at, 0]
-            v = info[at, 1]
+            if dj == 0:
+                tile = (above, mine, below)[di + 1][...]
+            else:
+                tile = (wcorner if dj < 0 else ecorner)[4 * OVL + 8 * (di + 1) : 4 * OVL + 8 * (di + 2), :]
+            u, v, there = [jnp.sum(jnp.where(unit & (lane == i), tile, 0.0)) for i in range(3)]
+            u, v = u.astype(jnp.int32), v.astype(jnp.int32)
             start, count, put = {
                 0: (2 * OVL - u, cells, 0),
                 1: (OVL - u, OVL, cells - OVL),
                 -1: (size + HALF - u, OVL, 0),
             }[di]
-            seen = there.astype(F32)
+            seen = there
             for r in range(0, count, HALF):
                 rows = pl.ds(start + r, HALF)
                 to = slice(put + r, put + r + HALF)
@@ -364,58 +380,46 @@
     table_high, table_low = tables(size)
     high, low = jnp.asarray(table_high), jnp.asarray(table_low)
 
-    north, south, west, east = call(
+    north, south, west, east, mine = call(
         pack_kernel,
-        "pack",
-        [((OVL, 640), F32), ((OVL, 640), F32), ((2, cells, OVL), F32), ((2, cells, OVL), F32)],
-        0,
-        [object_slab],
+        [(OVL, 640), (OVL, 640), (2, cells, OVL), (2, cells, OVL), (8, LANES)],
+        [offs, object_slab],
+        smem=(0,),
     )
     from_south = lax.ppermute(north, "row", up)
     from_north = lax.ppermute(south, "row", down)
     from_east = lax.ppermute(west, "col", left)
     from_west = lax.ppermute(east, "col", right)
-
-    mine = jnp.concatenate([offs, jnp.ones((1,), jnp.int32)])
     above = lax.ppermute(mine, "row", down)
     below = lax.ppermute(mine, "row", up)
-    column = jnp.stack([above, mine, below])
-    lefts = lax.ppermute(column, "col", right)
-    rights = lax.ppermute(column, "col", left)
-    info = jnp.stack([lefts, column, rights], axis=1).reshape(9, 3)
-
-    rolled, measured = call(
+
+    rolled, measured, token = call(
         ready_kernel,
-        "ready",
-        [((2, size, size), F32), ((size, size), F32)],
-        1,
+        [(2, size, size), (size, size), (8, LANES)],
         [offs, probe_field, counts.reshape(size, size)],
+        smem=(0,),
         scratch=[pltpu.VMEM((2, 4, size + HALF, LANES), F32)],
         flops=20_000_000_000,
     )
     wcorner_out, ecorner_out = call(
         corner_kernel,
-        "corner",
-        [((2, 2 * OVL, OVL), F32), ((2, 2 * OVL, OVL), F32)],
-        0,
-        [from_north, from_south],
+        [(4 * OVL + 24, OVL), (4 * OVL + 24, OVL)],
+        [from_north, from_south, above, mine, below, token],
     )
     ecorner = lax.ppermute(wcorner_out, "col", left)
     wcorner = lax.ppermute(ecorner_out, "col", right)
 
     own, nblock, sblock, wedge, eedge, wcorn, ecorn = call(
         main_kernel,
-        "main",
         [
-            ((2, cells, cells), F32),
-            ((2, OVL, 384), F32),
-            ((2, OVL, 384), F32),
-            ((2, cells, OVL), F32),
-            ((2, cells, OVL), F32),
-            ((2, 2 * OVL, OVL), F32),
-            ((2, 2 * OVL, OVL), F32),
+            (2, cells, cells),
+            (2, OVL, 384),
+            (2, OVL, 384),
+            (2, cells, OVL),
+            (2, cells, OVL),
+            (2, 2 * OVL, OVL),
+            (2, 2 * OVL, OVL),
         ],
-        1,
         [
             offs,
             object_slab,
@@ -430,37 +434,29 @@
             high,
             low,
         ],
+        smem=(0,),
         scratch=[pltpu.VMEM((size, size), F32), pltpu.VMEM((size, size), F32)],
         flops=5_000_000_000,
     )
     corner_e = lax.ppermute(wcorn, "col", left)
     corner_w = lax.ppermute(ecorn, "col", right)
+    nsend, ssend = call(send_kernel, [(OVL, 640), (OVL, 640)], [nblock, sblock, corner_w, corner_e])
+    grad_s = lax.ppermute(nsend, "row", up)
+    grad_n = lax.ppermute(ssend, "row", down)
     edge_e = lax.ppermute(wedge, "col", left)
     edge_w = lax.ppermute(eedge, "col", right)
-    nsend, ssend = call(
-        send_kernel,
-        "send",
-        [((OVL, 640), F32), ((OVL, 640), F32)],
-        0,
-        [nblock, sblock, corner_w, corner_e],
-    )
-    grad_s = lax.ppermute(nsend, "row", up)
-    grad_n = lax.ppermute(ssend, "row", down)
     total, weight = call(
         light_kernel,
-        "light",
-        [((2, cells, cells), F32), ((cells, cells), F32)],
-        1,
-        [info, probe_field, object_slab, own, edge_w, edge_e],
+        [(2, cells, cells), (cells, cells)],
+        [wcorner, ecorner, above, mine, below, probe_field, own, edge_w, edge_e],
         scratch=[pltpu.VMEM((6, size + 2 * OVL, LANES), F32), pltpu.VMEM((cells, 384), F32)],
         flops=10_000_000_000,
     )
     (updated,) = call(
         final_kernel,
-        "final",
-        [((2, cells, cells), F32)],
-        0,
+        [(2, cells, cells)],
         [object_slab, total, weight, grad_n, grad_s],
+        hbm_out=True,
     )
     return updated
 

time: 111 us -> 83.2 us (0.75)
  the two profiles are of different devices: /device:TPU:27 before, /device:TPU:25 now
where the time goes in v1:
time: 83.2 us; the launch traced here: 82.6 us
  starting transfers between devices  39.2 us (47%)
  waiting for transfers between devices  19.5 us (23%)
  Pallas kernels  19 us (23%)
  local copies, waits for them, and re-layouts  4.68 us (6%)
    pallas_call x7, Pallas kernels, call(): pl.pallas_call(kernel, out_shape=[jax.ShapeDtypeStruct(s, F32) if hbm_out...  19 us
    ppermute x1, waiting for transfers between devices, local(): grad_s = lax.ppermute(nsend, 'row', up)  6.62 us
    ppermute x1, starting transfers between devices, local(): from_west = lax.ppermute(east, 'col', right)  4.8 us
    unnamed x16, local copies, waits for them, and re-layouts  4.68 us
    ppermute x1, waiting for transfers between devices, local(): corner_e = lax.ppermute(wcorn, 'col', left)  4.4 us
    ppermute x1, waiting for transfers between devices, local(): ecorner = lax.ppermute(wcorner_out, 'col', left)  4.4 us
    ppermute x1, starting transfers between devices, local(): grad_s = lax.ppermute(nsend, 'row', up)  4.26 us
    ppermute x1, starting transfers between devices, local(): from_south = lax.ppermute(north, 'row', up)  4.26 us
  transfers between devices with their start and end apart: 14, of which 6 were waited for; matrix products, arithmetic and copies ran while one was open for 0% of the time, Pallas kernels for 6%

profile of v1, /device:TPU:25, one launch (start us, length us, event | category | flops | bytes accessed | tf_op | source)
XLA Modules:
  0.0 82.6 jit_solution(5717837754374038223)
XLA Ops:
  0.0 0.0 copy-start
  0.0 1.2 %copy-done = f32[2,320,320]{2,1,0:T(8,128)S(1)} copy-done((f32[2,320,320]{2,1,0:T(8,128)S(1)}, f32[2,320,320]{2,1,0:T(8,128)}, u32[]{:S(2)}) %copy-start) | copy-done | bytes 819224
  1.2 0.0 copy-start.2
  1.2 0.7 copy-done.2
  1.9 0.9 %shard_map.64 = (f32[128,640]{1,0:T(8,128)S(1)}, f32[128,640]{1,0:T(8,128)S(1)}, f32[2,320,128]{2,1,0:T(8,128)S(1)}, f32[2,320,128]{2,1,0:T(8,128)S(1)}, f32[8,128]{1,0:T(8,128)S(1)}) custom-call(s32[2]{0:T(128)S(1)} %bitcast.2, f32[2,320,320]{2,1,0:T(8,128)S(1)} %copy-done), custom_call_target="tpu_custom_call" | custom-call | tf_op jit(solution)/shard_map/pallas_call | solution.py:34
  2.8 3.0 %collective-permute-start.3 = (f32[8,128]{1,0:T(8,128)S(1)}, f32[8,128]{1,0:T(8,128)S(1)}, u32[]{:S(2)}, u32[]{:S(2)}) collective-permute-start(f32[8,128]{1,0:T(8,128)S(1)} %get-tuple-element.28.mine), channel_id=1, source_target_pairs={{4,0},{8,4},{12,8},{16,12},{20,16},{24,20},{28,24},{5,1},{9,5},{13... | collective-permute-start | bytes 12296 | tf_op jit(solution)/shard_map/ppermute | solution.py:394
  5.8 2.2 %collective-permute-start.2 = (f32[8,128]{1,0:T(8,128)S(1)}, f32[8,128]{1,0:T(8,128)S(1)}, u32[]{:S(2)}, u32[]{:S(2)}) collective-permute-start(f32[8,128]{1,0:T(8,128)S(1)} %get-tuple-element.28.mine), channel_id=1, source_target_pairs={{0,4},{4,8},{8,12},{12,16},{16,20},{20,24},{24,28},{1,5},{5,9},{9,... | collective-permute-start | bytes 12296 | tf_op jit(solution)/shard_map/ppermute | solution.py:393
  8.0 1.9 %collective-permute-start = (f32[128,640]{1,0:T(8,128)S(1)}, f32[128,640]{1,0:T(8,128)S(1)}, u32[]{:S(2)}, u32[]{:S(2)}) collective-permute-start(f32[128,640]{1,0:T(8,128)S(1)} %get-tuple-element.26), channel_id=1, source_target_pairs={{0,4},{4,8},{8,12},{12,16},{16,20},{20,24},{24,28},{1,5},{5,9},{9,... | collective-permute-start | bytes 983048 | tf_op jit(solution)/shard_map/ppermute | solution.py:390
  10.0 4.3 %collective-permute-start.1 = (f32[128,640]{1,0:T(8,128)S(1)}, f32[128,640]{1,0:T(8,128)S(1)}, u32[]{:S(2)}, u32[]{:S(2)}) collective-permute-start(f32[128,640]{1,0:T(8,128)S(1)} %get-tuple-element.27), channel_id=1, source_target_pairs={{4,0},{8,4},{12,8},{16,12},{20,16},{24,20},{28,24},{5,1},{9,5},{13... | collective-permute-start | bytes 983048 | tf_op jit(solution)/shard_map/ppermute | solution.py:389
  14.2 4.8 %collective-permute-start.6 = (f32[2,320,128]{2,1,0:T(8,128)S(1)}, f32[2,320,128]{2,1,0:T(8,128)S(1)}, u32[]{:S(2)}, u32[]{:S(2)}) collective-permute-start(f32[2,320,128]{2,1,0:T(8,128)S(1)} %get-tuple-element.32), channel_id=1, source_target_pairs={{0,1},{1,2},{2,3},{4,5},{5,6},{6,7},{8,9},{9,10},{10,11},{12,13},{... | collective-permute-start | bytes 983048 | tf_op jit(solution)/shard_map/ppermute | solution.py:392
  19.1 0.0 collective-permute-done.3.below
  19.1 1.9 %collective-permute-start.7 = (f32[2,320,128]{2,1,0:T(8,128)S(1)}, f32[2,320,128]{2,1,0:T(8,128)S(1)}, u32[]{:S(2)}, u32[]{:S(2)}) collective-permute-start(f32[2,320,128]{2,1,0:T(8,128)S(1)} %get-tuple-element.33), channel_id=1, source_target_pairs={{1,0},{2,1},{3,2},{5,4},{6,5},{7,6},{9,8},{10,9},{11,10},{13,12},{... | collective-permute-start | bytes 983048 | tf_op jit(solution)/shard_map/ppermute | solution.py:391
  21.0 0.0 copy-start.3
  21.0 1.6 %copy-done.3 = f32[2,512,512]{2,1,0:T(8,128)S(1)} copy-done((f32[2,512,512]{2,1,0:T(8,128)S(1)}, f32[2,512,512]{2,1,0:T(8,128)}, u32[]{:S(2)}) %copy-start.3) | copy-done | bytes 2097176
  22.6 0.0 copy-start.5
  22.6 1.2 %copy-done.5 = s32[1,1,1,512,512]{4,3,2,1,0:T(8,128)S(1)} copy-done((s32[1,1,1,512,512]{4,3,2,1,0:T(8,128)S(1)}, s32[1,1,1,512,512]{4,3,2,1,0:T(8,128)}, u32[]{:S(2)}) %copy-start.5) | copy-done | bytes 1048600
  23.8 0.0 copy-start.1
  23.8 0.0 copy-start.6
  23.8 0.0 copy-start.7
  23.8 2.4 %shard_map.65 = (f32[2,512,512]{2,1,0:T(8,128)S(1)}, f32[512,512]{1,0:T(8,128)S(1)}, f32[8,128]{1,0:T(8,128)S(1)}) custom-call(s32[2]{0:T(128)S(1)} %bitcast.3, f32[2,512,512]{2,1,0:T(8,128)S(1)} %copy-done.3, s32[512,512]{1,0:T(8,128)S(1)} %bitcast.5), custom_call_target="tpu_custom_call" | custom-call | flops 20000000000 | tf_op jit(solution)/shard_map/pallas_call | solution.py:34
  26.2 0.0 collective-permute-done.2.above
  26.2 0.0 collective-permute-done.north
  26.2 1.3 %collective-permute-done.1.south = f32[128,640]{1,0:T(8,128)S(1)} collective-permute-done((f32[128,640]{1,0:T(8,128)S(1)}, f32[128,640]{1,0:T(8,128)S(1)}, u32[]{:S(2)}, u32[]{:S(2)}) %collective-permute-start.1) | collective-permute-done | bytes 327712 | tf_op jit(solution)/shard_map/ppermute | solution.py:389
  27.5 0.2 shard_map.66
  27.7 3.5 %collective-permute-start.4 = (f32[536,128]{1,0:T(8,128)S(1)}, f32[536,128]{1,0:T(8,128)S(1)}, u32[]{:S(2)}, u32[]{:S(2)}) collective-permute-start(f32[536,128]{1,0:T(8,128)S(1)} %get-tuple-element.30), channel_id=1, source_target_pairs={{0,1},{1,2},{2,3},{4,5},{5,6},{6,7},{8,9},{9,10},{10,11},{12,13},{... | collective-permute-start | bytes 823304 | tf_op jit(solution)/shard_map/ppermute | solution.py:410
  31.2 1.9 %collective-permute-start.5 = (f32[536,128]{1,0:T(8,128)S(1)}, f32[536,128]{1,0:T(8,128)S(1)}, u32[]{:S(2)}, u32[]{:S(2)}) collective-permute-start(f32[536,128]{1,0:T(8,128)S(1)} %get-tuple-element.31), channel_id=1, source_target_pairs={{1,0},{2,1},{3,2},{5,4},{6,5},{7,6},{9,8},{10,9},{11,10},{13,12},{... | collective-permute-start | bytes 823304 | tf_op jit(solution)/shard_map/ppermute | solution.py:409
  33.2 0.0 collective-permute-done.6.west
  33.2 0.0 collective-permute-done.7.east
  33.2 1.5 %collective-permute-done.4.wcorner = f32[536,128]{1,0:T(8,128)S(1)} collective-permute-done((f32[536,128]{1,0:T(8,128)S(1)}, f32[536,128]{1,0:T(8,128)S(1)}, u32[]{:S(2)}, u32[]{:S(2)}) %collective-permute-start.4) | collective-permute-done | bytes 274464 | tf_op jit(solution)/shard_map/ppermute | solution.py:410
  34.7 4.4 %collective-permute-done.5.ecorner = f32[536,128]{1,0:T(8,128)S(1)} collective-permute-done((f32[536,128]{1,0:T(8,128)S(1)}, f32[536,128]{1,0:T(8,128)S(1)}, u32[]{:S(2)}, u32[]{:S(2)}) %collective-permute-start.5) | collective-permute-done | bytes 274464 | tf_op jit(solution)/shard_map/ppermute | solution.py:409
  39.1 0.0 copy-done.1
  39.1 0.0 copy-done.6
  39.1 0.0 copy-done.7
  39.1 0.0 copy-start.4
  39.1 11.6 %shard_map.67 = (f32[2,320,320]{2,1,0:T(8,128)S(1)}, f32[2,128,384]{2,1,0:T(8,128)S(1)}, f32[2,128,384]{2,1,0:T(8,128)S(1)}, f32[2,320,128]{2,1,0:T(8,128)S(1)},...) custom-call(s32[2]{0:T(128)S(1)} %bitcast.4, f32[2,320,320]{2,1,0:T(8,128)S(1)} %copy-done.1, ...), custom_call_target="tpu_custom_call" | custom-call | flops 5000000000 | tf_op jit(solution)/shard_map/pallas_call | solution.py:34
  50.7 1.9 %collective-permute-start.8 = (f32[2,320,128]{2,1,0:T(8,128)S(1)}, f32[2,320,128]{2,1,0:T(8,128)S(1)}, u32[]{:S(2)}, u32[]{:S(2)}) collective-permute-start(f32[2,320,128]{2,1,0:T(8,128)S(1)} %get-tuple-element.37), channel_id=1, source_target_pairs={{0,1},{1,2},{2,3},{4,5},{5,6},{6,7},{8,9},{9,10},{10,11},{12,13},{... | collective-permute-start | bytes 983048 | tf_op jit(solution)/shard_map/ppermute | solution.py:447
  52.6 2.4 %collective-permute-start.9 = (f32[2,320,128]{2,1,0:T(8,128)S(1)}, f32[2,320,128]{2,1,0:T(8,128)S(1)}, u32[]{:S(2)}, u32[]{:S(2)}) collective-permute-start(f32[2,320,128]{2,1,0:T(8,128)S(1)} %get-tuple-element.38), channel_id=1, source_target_pairs={{1,0},{2,1},{3,2},{5,4},{6,5},{7,6},{9,8},{10,9},{11,10},{13,12},{... | collective-permute-start | bytes 983048 | tf_op jit(solution)/shard_map/ppermute | solution.py:446
  55.0 3.1 %collective-permute-start.10 = (f32[2,256,128]{2,1,0:T(8,128)S(1)}, f32[2,256,128]{2,1,0:T(8,128)S(1)}, u32[]{:S(2)}, u32[]{:S(2)}) collective-permute-start(f32[2,256,128]{2,1,0:T(8,128)S(1)} %get-tuple-element.43), channel_id=1, source_target_pairs={{0,1},{1,2},{2,3},{4,5},{5,6},{6,7},{8,9},{9,10},{10,11},{12,13},{... | collective-permute-start | bytes 786440 | tf_op jit(solution)/shard_map/ppermute | solution.py:442
  58.2 1.9 %collective-permute-start.11 = (f32[2,256,128]{2,1,0:T(8,128)S(1)}, f32[2,256,128]{2,1,0:T(8,128)S(1)}, u32[]{:S(2)}, u32[]{:S(2)}) collective-permute-start(f32[2,256,128]{2,1,0:T(8,128)S(1)} %get-tuple-element.44), channel_id=1, source_target_pairs={{1,0},{2,1},{3,2},{5,4},{6,5},{7,6},{9,8},{10,9},{11,10},{13,12},{... | collective-permute-start | bytes 786440 | tf_op jit(solution)/shard_map/ppermute | solution.py:441
  60.1 1.4 %collective-permute-done.10.fromw = f32[2,256,128]{2,1,0:T(8,128)S(1)} collective-permute-done((f32[2,256,128]{2,1,0:T(8,128)S(1)}, f32[2,256,128]{2,1,0:T(8,128)S(1)}, u32[]{:S(2)}, u32[]{:S(2)}) %collective-permute-start.10) | collective-permute-done | bytes 262176 | tf_op jit(solution)/shard_map/ppermute | solution.py:442
  61.5 4.4 %collective-permute-done.11.frome = f32[2,256,128]{2,1,0:T(8,128)S(1)} collective-permute-done((f32[2,256,128]{2,1,0:T(8,128)S(1)}, f32[2,256,128]{2,1,0:T(8,128)S(1)}, u32[]{:S(2)}, u32[]{:S(2)}) %collective-permute-start.11) | collective-permute-done | bytes 262176 | tf_op jit(solution)/shard_map/ppermute | solution.py:441
  65.9 0.1 shard_map.69
  66.0 1.9 %collective-permute-start.12 = (f32[128,640]{1,0:T(8,128)S(1)}, f32[128,640]{1,0:T(8,128)S(1)}, u32[]{:S(2)}, u32[]{:S(2)}) collective-permute-start(f32[128,640]{1,0:T(8,128)S(1)} %get-tuple-element.45), channel_id=1, source_target_pairs={{0,4},{4,8},{8,12},{12,16},{16,20},{20,24},{24,28},{1,5},{5,9},{9,... | collective-permute-start | bytes 983048 | tf_op jit(solution)/shard_map/ppermute | solution.py:445
  67.9 4.3 %collective-permute-start.13 = (f32[128,640]{1,0:T(8,128)S(1)}, f32[128,640]{1,0:T(8,128)S(1)}, u32[]{:S(2)}, u32[]{:S(2)}) collective-permute-start(f32[128,640]{1,0:T(8,128)S(1)} %get-tuple-element.46), channel_id=1, source_target_pairs={{4,0},{8,4},{12,8},{16,12},{20,16},{24,20},{28,24},{5,1},{9,5},{13... | collective-permute-start | bytes 983048 | tf_op jit(solution)/shard_map/ppermute | solution.py:444
  72.2 0.0 collective-permute-done.8.fromw
  72.2 0.0 collective-permute-done.9.frome
  72.2 0.0 copy-done.4
  72.2 2.6 %shard_map.68 = (f32[2,320,320]{2,1,0:T(8,128)S(1)}, f32[320,320]{1,0:T(8,128)S(1)}) custom-call(f32[536,128]{1,0:T(8,128)S(1)} %collective-permute-done.4.wcorner, f32[536,128]{1,0:T(8,128)S(1)} %collective-permute-done.5.ecorner, f32[8,128]{1,0:T(8,128)S(1)} %collective-permute-done.2.above, f32[8,128]{1,0:T(8,128)S(1)} %get-tuple-element.28.mine, ...), custom_call_target="tpu_custom_call" | custom-call | flops 10000000000 | tf_op jit(solution)/shard_map/pallas_call | solution.py:34
  74.8 0.0 collective-permute-done.12.fromn
  74.8 6.6 %collective-permute-done.13.froms = f32[128,640]{1,0:T(8,128)S(1)} collective-permute-done((f32[128,640]{1,0:T(8,128)S(1)}, f32[128,640]{1,0:T(8,128)S(1)}, u32[]{:S(2)}, u32[]{:S(2)}) %collective-permute-start.13) | collective-permute-done | bytes 327712 | tf_op jit(solution)/shard_map/ppermute | solution.py:444
  81.5 1.1 %shard_map.70 = f32[2,320,320]{2,1,0:T(8,128)} custom-call(f32[2,320,320]{2,1,0:T(8,128)S(1)} %copy-done.1, f32[2,320,320]{2,1,0:T(8,128)S(1)} %get-tuple-element.39.total, f32[320,320]{1,0:T(8,128)S(1)} %get-tuple-element.40.weight, f32[128,640]{1,0:T(8,128)S(1)} %collective-permute-done.12.fromn, f32[128,640]{1,0:T(8,128)S(1)} %collective-permute-done.13.froms), custom_call_target="tpu_custom_call" | custom-call | tf_op jit(solution)/shard_map/pallas_call | solution.py:34
Async XLA Ops:
  0.0 1.2 %copy-start = (f32[2,320,320]{2,1,0:T(8,128)S(1)}, f32[2,320,320]{2,1,0:T(8,128)}, u32[]{:S(2)}) copy-start(f32[2,320,320]{2,1,0:T(8,128)} %obj.5) | copy-start | bytes 2457604
  1.2 0.7 copy-start.2
  2.8 16.3 %collective-permute-start.3 = (f32[8,128]{1,0:T(8,128)S(1)}, f32[8,128]{1,0:T(8,128)S(1)}, u32[]{:S(2)}, u32[]{:S(2)}) collective-permute-start(f32[8,128]{1,0:T(8,128)S(1)} %get-tuple-element.28.mine), channel_id=1, source_target_pairs={{4,0},{8,4},{12,8},{16,12},{20,16},{24,20},{28,24},{5,1},{9,5},{13... | collective-permute-start | bytes 12296 | tf_op jit(solution)/shard_map/ppermute | solution.py:394
  5.8 20.4 %collective-permute-start.2 = (f32[8,128]{1,0:T(8,128)S(1)}, f32[8,128]{1,0:T(8,128)S(1)}, u32[]{:S(2)}, u32[]{:S(2)}) collective-permute-start(f32[8,128]{1,0:T(8,128)S(1)} %get-tuple-element.28.mine), channel_id=1, source_target_pairs={{0,4},{4,8},{8,12},{12,16},{16,20},{20,24},{24,28},{1,5},{5,9},{9,... | collective-permute-start | bytes 12296 | tf_op jit(solution)/shard_map/ppermute | solution.py:393
  8.0 18.2 %collective-permute-start = (f32[128,640]{1,0:T(8,128)S(1)}, f32[128,640]{1,0:T(8,128)S(1)}, u32[]{:S(2)}, u32[]{:S(2)}) collective-permute-start(f32[128,640]{1,0:T(8,128)S(1)} %get-tuple-element.26), channel_id=1, source_target_pairs={{0,4},{4,8},{8,12},{12,16},{16,20},{20,24},{24,28},{1,5},{5,9},{9,... | collective-permute-start | bytes 983048 | tf_op jit(solution)/shard_map/ppermute | solution.py:390
  10.0 17.5 %collective-permute-start.1 = (f32[128,640]{1,0:T(8,128)S(1)}, f32[128,640]{1,0:T(8,128)S(1)}, u32[]{:S(2)}, u32[]{:S(2)}) collective-permute-start(f32[128,640]{1,0:T(8,128)S(1)} %get-tuple-element.27), channel_id=1, source_target_pairs={{4,0},{8,4},{12,8},{16,12},{20,16},{24,20},{28,24},{5,1},{9,5},{13... | collective-permute-start | bytes 983048 | tf_op jit(solution)/shard_map/ppermute | solution.py:389
  14.2 18.9 %collective-permute-start.6 = (f32[2,320,128]{2,1,0:T(8,128)S(1)}, f32[2,320,128]{2,1,0:T(8,128)S(1)}, u32[]{:S(2)}, u32[]{:S(2)}) collective-permute-start(f32[2,320,128]{2,1,0:T(8,128)S(1)} %get-tuple-element.32), channel_id=1, source_target_pairs={{0,1},{1,2},{2,3},{4,5},{5,6},{6,7},{8,9},{9,10},{10,11},{12,13},{... | collective-permute-start | bytes 983048 | tf_op jit(solution)/shard_map/ppermute | solution.py:392
  19.1 14.1 %collective-permute-start.7 = (f32[2,320,128]{2,1,0:T(8,128)S(1)}, f32[2,320,128]{2,1,0:T(8,128)S(1)}, u32[]{:S(2)}, u32[]{:S(2)}) collective-permute-start(f32[2,320,128]{2,1,0:T(8,128)S(1)} %get-tuple-element.33), channel_id=1, source_target_pairs={{1,0},{2,1},{3,2},{5,4},{6,5},{7,6},{9,8},{10,9},{11,10},{13,12},{... | collective-permute-start | bytes 983048 | tf_op jit(solution)/shard_map/ppermute | solution.py:391
  21.0 1.6 %copy-start.3 = (f32[2,512,512]{2,1,0:T(8,128)S(1)}, f32[2,512,512]{2,1,0:T(8,128)}, u32[]{:S(2)}) copy-start(f32[2,512,512]{2,1,0:T(8,128)} %probe.3) | copy-start | bytes 6291460
  22.6 1.2 %copy-start.5 = (s32[1,1,1,512,512]{4,3,2,1,0:T(8,128)S(1)}, s32[1,1,1,512,512]{4,3,2,1,0:T(8,128)}, u32[]{:S(2)}) copy-start(s32[1,1,1,512,512]{4,3,2,1,0:T(8,128)} %param.9) | copy-start | bytes 3145732
  23.8 15.2 %copy-start.1 = (f32[2,320,320]{2,1,0:T(8,128)S(1)}, f32[2,320,320]{2,1,0:T(8,128)}, u32[]{:S(2)}) copy-start(f32[2,320,320]{2,1,0:T(8,128)} %obj.5) | copy-start | bytes 2457604
  23.8 15.2 %copy-start.6 = (bf16[8,256,256]{2,1,0:T(8,128)(2,1)S(1)}, bf16[8,256,256]{2,1,0:T(8,128)(2,1)}, u32[]{:S(2)}) copy-start(bf16[8,256,256]{2,1,0:T(8,128)(2,1)} %constant.5.clone.low) | copy-start | bytes 3145732
  23.8 15.2 %copy-start.7 = (bf16[8,256,256]{2,1,0:T(8,128)(2,1)S(1)}, bf16[8,256,256]{2,1,0:T(8,128)(2,1)}, u32[]{:S(2)}) copy-start(bf16[8,256,256]{2,1,0:T(8,128)(2,1)} %constant.4.clone.high) | copy-start | bytes 3145732
  27.7 6.9 %collective-permute-start.4 = (f32[536,128]{1,0:T(8,128)S(1)}, f32[536,128]{1,0:T(8,128)S(1)}, u32[]{:S(2)}, u32[]{:S(2)}) collective-permute-start(f32[536,128]{1,0:T(8,128)S(1)} %get-tuple-element.30), channel_id=1, source_target_pairs={{0,1},{1,2},{2,3},{4,5},{5,6},{6,7},{8,9},{9,10},{10,11},{12,13},{... | collective-permute-start | bytes 823304 | tf_op jit(solution)/shard_map/ppermute | solution.py:410
  31.2 7.8 %collective-permute-start.5 = (f32[536,128]{1,0:T(8,128)S(1)}, f32[536,128]{1,0:T(8,128)S(1)}, u32[]{:S(2)}, u32[]{:S(2)}) collective-permute-start(f32[536,128]{1,0:T(8,128)S(1)} %get-tuple-element.31), channel_id=1, source_target_pairs={{1,0},{2,1},{3,2},{5,4},{6,5},{7,6},{9,8},{10,9},{11,10},{13,12},{... | collective-permute-start | bytes 823304 | tf_op jit(solution)/shard_map/ppermute | solution.py:409
  39.1 33.1 %copy-start.4 = (f32[2,512,512]{2,1,0:T(8,128)S(1)}, f32[2,512,512]{2,1,0:T(8,128)}, u32[]{:S(2)}) copy-start(f32[2,512,512]{2,1,0:T(8,128)} %probe.3) | copy-start | bytes 6291460
  50.7 21.5 %collective-permute-start.8 = (f32[2,320,128]{2,1,0:T(8,128)S(1)}, f32[2,320,128]{2,1,0:T(8,128)S(1)}, u32[]{:S(2)}, u32[]{:S(2)}) collective-permute-start(f32[2,320,128]{2,1,0:T(8,128)S(1)} %get-tuple-element.37), channel_id=1, source_target_pairs={{0,1},{1,2},{2,3},{4,5},{5,6},{6,7},{8,9},{9,10},{10,11},{12,13},{... | collective-permute-start | bytes 983048 | tf_op jit(solution)/shard_map/ppermute | solution.py:447
  52.6 19.6 %collective-permute-start.9 = (f32[2,320,128]{2,1,0:T(8,128)S(1)}, f32[2,320,128]{2,1,0:T(8,128)S(1)}, u32[]{:S(2)}, u32[]{:S(2)}) collective-permute-start(f32[2,320,128]{2,1,0:T(8,128)S(1)} %get-tuple-element.38), channel_id=1, source_target_pairs={{1,0},{2,1},{3,2},{5,4},{6,5},{7,6},{9,8},{10,9},{11,10},{13,12},{... | collective-permute-start | bytes 983048 | tf_op jit(solution)/shard_map/ppermute | solution.py:446
  55.0 6.4 %collective-permute-start.10 = (f32[2,256,128]{2,1,0:T(8,128)S(1)}, f32[2,256,128]{2,1,0:T(8,128)S(1)}, u32[]{:S(2)}, u32[]{:S(2)}) collective-permute-start(f32[2,256,128]{2,1,0:T(8,128)S(1)} %get-tuple-element.43), channel_id=1, source_target_pairs={{0,1},{1,2},{2,3},{4,5},{5,6},{6,7},{8,9},{9,10},{10,11},{12,13},{... | collective-permute-start | bytes 786440 | tf_op jit(solution)/shard_map/ppermute | solution.py:442
  58.2 7.7 %collective-permute-start.11 = (f32[2,256,128]{2,1,0:T(8,128)S(1)}, f32[2,256,128]{2,1,0:T(8,128)S(1)}, u32[]{:S(2)}, u32[]{:S(2)}) collective-permute-start(f32[2,256,128]{2,1,0:T(8,128)S(1)} %get-tuple-element.44), channel_id=1, source_target_pairs={{1,0},{2,1},{3,2},{5,4},{6,5},{7,6},{9,8},{10,9},{11,10},{13,12},{... | collective-permute-start | bytes 786440 | tf_op jit(solution)/shard_map/ppermute | solution.py:441
  66.0 8.8 %collective-permute-start.12 = (f32[128,640]{1,0:T(8,128)S(1)}, f32[128,640]{1,0:T(8,128)S(1)}, u32[]{:S(2)}, u32[]{:S(2)}) collective-permute-start(f32[128,640]{1,0:T(8,128)S(1)} %get-tuple-element.45), channel_id=1, source_target_pairs={{0,4},{4,8},{8,12},{12,16},{16,20},{20,24},{24,28},{1,5},{5,9},{9,... | collective-permute-start | bytes 983048 | tf_op jit(solution)/shard_map/ppermute | solution.py:445
  67.9 13.5 %collective-permute-start.13 = (f32[128,640]{1,0:T(8,128)S(1)}, f32[128,640]{1,0:T(8,128)S(1)}, u32[]{:S(2)}, u32[]{:S(2)}) collective-permute-start(f32[128,640]{1,0:T(8,128)S(1)} %get-tuple-element.46), channel_id=1, source_target_pairs={{4,0},{8,4},{12,8},{16,12},{20,16},{24,20},{28,24},{5,1},{9,5},{13... | collective-permute-start | bytes 983048 | tf_op jit(solution)/shard_map/ppermute | solution.py:444

commit v2 on v1

v2 whole, which is shorter than its diff:
```python
import functools
import math

import jax
import jax.numpy as jnp
import ml_dtypes
import numpy as np
from jax import lax
from jax.experimental import pallas as pl
from jax.experimental.pallas import tpu as pltpu
from jax.sharding import PartitionSpec as P

OVL = 128
HALF = 64
LANES = 128

EPSILON = 0.01
PHOTON_SCALE = 0.01
STEP_SIZE = 0.5
REGULAR = 1.0

F32 = jnp.float32
BF16 = jnp.bfloat16


def call(kernel, out_shapes, args, smem=(), hbm_out=False, scratch=(), flops=0, limit=16):
    specs = [
        pl.BlockSpec(memory_space=pltpu.SMEM if i in smem else pltpu.VMEM) for i in range(len(args))
    ]
    args = [
        x if i in smem else pltpu.with_memory_space_constraint(x, pltpu.VMEM)
        for i, x in enumerate(args)
    ]
    return pl.pallas_call(
        kernel,
        out_shape=[
            jax.ShapeDtypeStruct(s, F32) if hbm_out else pltpu.VMEM(s, F32) for s in out_shapes
        ],
        in_specs=specs,
        out_specs=[pl.BlockSpec(memory_space=pltpu.VMEM) for _ in out_shapes],
        scratch_shapes=list(scratch),
        compiler_params=pltpu.CompilerParams(vmem_limit_bytes=limit * 1024 * 1024),
        cost_estimate=pl.CostEstimate(flops=flops, bytes_accessed=0, transcendentals=0)
        if flops
        else None,
    )(*args)


@functools.lru_cache(maxsize=None)
def tables(length):
    quarter = length // 4
    n = np.arange(quarter)[:, None]
    k = np.arange(quarter)[None, :]
    blocks = []
    for p in range(4):
        angle = 2.0 * np.pi * ((n * (4 * k + p)) % length) / length
        c = np.cos(angle) / math.sqrt(length)
        s = np.sin(angle) / math.sqrt(length)
        blocks.append(np.block([[c, -s], [s, c]]))
    blocks += [b.T for b in blocks]
    full = np.stack(blocks)
    high = full.astype(np.float32).astype(ml_dtypes.bfloat16)
    low = (full - high.astype(np.float64)).astype(np.float32).astype(ml_dtypes.bfloat16)
    return high, low


def split(x):
    high = x.astype(BF16)
    return high, (x - high.astype(F32)).astype(BF16)


def dot(a, b):
    return lax.dot_general(a, b, (((1,), (0,)), ((), ())), preferred_element_type=F32)


def mix_forward(x):
    (x0r, x0i), (x1r, x1i), (x2r, x2i), (x3r, x3i) = x
    ar, ai, br, bi = x0r + x2r, x0i + x2i, x0r - x2r, x0i - x2i
    cr, ci, dr, di = x1r + x3r, x1i + x3i, x1r - x3r, x1i - x3i
    return [(ar + cr, ai + ci), (br + di, bi - dr), (ar - cr, ai - ci), (br - di, bi + dr)]


def mix_inverse(x):
    (x0r, x0i), (x1r, x1i), (x2r, x2i), (x3r, x3i) = x
    ar, ai, br, bi = x0r + x2r, x0i + x2i, x0r - x2r, x0i - x2i
    cr, ci, dr, di = x1r + x3r, x1i + x3i, x1r - x3r, x1i - x3i
    return [(ar + cr, ai + ci), (br - di, bi + dr), (ar - cr, ai - ci), (br + di, bi - dr)]


def lane_iota(shape):
    return lax.broadcasted_iota(jnp.int32, shape, len(shape) - 1)


def row_iota(shape):
    return lax.broadcasted_iota(jnp.int32, shape, len(shape) - 2)


def turn(x):
    return pltpu.roll(x, HALF, len(x.shape) - 1)


def odd():
    return lax.axis_index("col") % 2 == 1


def pack_kernel(offs, obj, north, south, xside, dside):
    rows, cols = obj.shape[1:]
    lane = lane_iota((8, LANES))
    info = jnp.where(lane == 0, offs[0], jnp.where(lane == 1, offs[1], 1)).astype(F32)
    for out, base in ((north, 0), (south, rows - OVL)):
        for c in range(2):
            out[0:OVL, c * 256 : c * 256 + 256] = obj[c, base : base + OVL, 0:256]
            out[0:OVL, 512 + c * HALF : 512 + c * HALF + HALF] = obj[c, base : base + OVL, 256:cols]
        out[OVL : OVL + 8, 0:128] = info
        out[OVL : OVL + 8, 128:640] = jnp.zeros((8, 512), F32)
    right = odd()
    for c in range(2):
        west = turn(obj[c, :, 0:128])
        east = obj[c, :, cols - OVL : cols]
        xside[c] = jnp.where(right, east, west)
        dside[c] = jnp.where(right, west, east)


def corner_kernel(offs, north, south, token, xside, dside):
    right = odd()
    for part, halo in ((0, north), (1, south)):
        for c in range(2):
            rows = slice((2 * c + part) * OVL, (2 * c + part) * OVL + OVL)
            west = turn(halo[0:OVL, c * 256 : c * 256 + 128])
            lane = lane_iota((OVL, LANES))
            tail = halo[0:OVL, 512:640]
            if c == 0:
                tail = turn(tail)
            east = jnp.where(lane < HALF, turn(halo[0:OVL, c * 256 + 128 : c * 256 + 256]), tail)
            xside[rows, :] = jnp.where(right, east, west)
            dside[rows, :] = jnp.where(right, west, east)
    lane = lane_iota((8, LANES))
    info = jnp.where(lane == 0, offs[0], jnp.where(lane == 1, offs[1], 1)).astype(F32)
    for out in (xside, dside):
        out[4 * OVL : 4 * OVL + 8, :] = north[OVL : OVL + 8, 0:128]
        out[4 * OVL + 8 : 4 * OVL + 16, :] = info
        out[4 * OVL + 16 : 4 * OVL + 24, :] = south[OVL : OVL + 8, 0:128]


def ready_kernel(offs, probe, counts, rolled, measured, token, wide):
    size = probe.shape[-1]
    quarter = size // 4
    u = offs[0]
    v = offs[1]
    for c in range(2):
        for t in range(4):
            cols = slice(t * quarter, (t + 1) * quarter)
            wide[c, t, 0:HALF, :] = probe[c, size - HALF : size, cols]
            wide[c, t, HALF : HALF + size, :] = probe[c, :, cols]
        for base in range(0, size, HALF):
            rows = pl.ds(HALF - u + base, HALF)
            piece = jnp.concatenate([wide[c, t, rows, :] for t in range(4)], axis=1)
            rolled[c, base : base + HALF, :] = pltpu.roll(piece, v, 1)
    token[...] = jnp.zeros(token.shape, F32)
    r = row_iota((size, size))
    k = lane_iota((size, size))
    order = jnp.where(r == 4 * (k % quarter) + k // quarter, 1.0, 0.0).astype(BF16)
    for t in range(4):
        wide[0, t, 0:size, :] = counts[:, t * quarter : (t + 1) * quarter].astype(F32)
    for p in range(4):
        rows = jnp.concatenate([wide[0, t, pl.ds(p, quarter, stride=4), :] for t in range(4)], axis=1)
        high = jnp.floor(rows * (1.0 / 256.0))
        low = rows - 256.0 * high
        moved = 256.0 * dot(high.astype(BF16), order) + dot(low.astype(BF16), order)
        measured[p * quarter : (p + 1) * quarter, :] = jnp.sqrt(moved * PHOTON_SCALE)


def main_kernel(
    offs, obj, north, south, xside, dside, xcorner, dcorner, rolled, measured, high, low,
    own, nblock, sblock, xedge, dedge, xcorn, dcorn, ah, al, bh, bl, zf, tf,
):
    size = rolled.shape[-1]
    quarter = size // 4
    cells = obj.shape[1]
    u = offs[0]
    v = offs[1]
    right = odd()

    def pieces(c, part, base, count):
        lane = lane_iota((count, LANES))
        if part == "own":
            tiles = [obj[c, base : base + count, 0:128], obj[c, base : base + count, 128:256]]
            last = obj[c, base : base + count, 256:cells]
            last = jnp.concatenate([last, last], axis=1)
            x = xside[c, base : base + count, :]
            d = dside[c, base : base + count, :]
        else:
            ref, start = (north, base) if part == "n" else (south, base)
            tiles = [ref[start : start + count, c * 256 + 128 * t : c * 256 + 128 * t + 128] for t in range(2)]
            last = ref[start : start + count, 512:640]
            if c == 1:
                last = turn(last)
            start = start + (2 * c + (part == "s")) * OVL
            x = xcorner[start : start + count, :]
            d = dcorner[start : start + count, :]
        w, e = jnp.where(right, d, x), jnp.where(right, x, d)
        return [jnp.where(lane < v, e, w), tiles[0], tiles[1], jnp.where(lane < HALF, last, e)]

    def patch(c, slot, count):
        if slot < HALF:
            row = row_iota((count, LANES)) + slot
            a = pieces(c, "n", slot, count)
            b = pieces(c, "s", slot + HALF, count)
            return [jnp.where(row < u, y, x) for x, y in zip(a, b)]
        if slot < OVL:
            return pieces(c, "n", slot, count)
        if slot < OVL + cells:
            return pieces(c, "own", slot - OVL, count)
        return pieces(c, "s", slot - OVL - cells, count)

    def keep(hi, lo, at, x):
        hi[at], lo[at] = split(x)

    step = 32
    block = 256
    re, im = slice(0, quarter), slice(quarter, 2 * quarter)

    for top in range(0, size, block):
        for base in range(top, top + block, step):
            rows = slice(base, base + step)
            pr, pi = patch(0, base, step), patch(1, base, step)
            exits = []
            for q in range(4):
                cols = slice(q * quarter, (q + 1) * quarter)
                ar, ai = rolled[0, rows, cols], rolled[1, rows, cols]
                exits.append((ar * pr[q] - ai * pi[q], ar * pi[q] + ai * pr[q]))
            for p, (yr, yi) in enumerate(mix_forward(exits)):
                keep(ah, al, (p, rows, re), yr)
                keep(ah, al, (p, rows, im), yi)
        rows = slice(top, top + block)
        for p in range(4):
            a = ah[p, rows, :]
            zf[p, rows, :] = dot(a, high[p]) + dot(al[p, rows, :], high[p]) + dot(a, low[p])

    for half in range(2):
        pair = (2 * half, 2 * half + 1)
        for t, p in enumerate(pair):
            cols = slice(t * quarter, (t + 1) * quarter)
            for r in range(0, quarter, step):
                quads = []
                for q in range(4):
                    rows = slice(q * quarter + r, q * quarter + r + step)
                    quads.append((zf[p, rows, re], zf[p, rows, im]))
                for k, (yr, yi) in enumerate(mix_forward(quads)):
                    keep(bh, bl, (half, k, slice(r, r + step), cols), yr)
                    keep(bh, bl, (half, k, slice(quarter + r, quarter + r + step), cols), yi)
        for k in range(4):
            a = bh[half, k]
            z = dot(high[4 + k], a) + dot(high[4 + k], bl[half, k]) + dot(low[4 + k], a)
            zr, zi = z[re], z[im]
            m = measured[k * quarter : (k + 1) * quarter, half * block : (half + 1) * block]
            factor = 1.0 - m * lax.rsqrt(zr * zr + zi * zi + EPSILON)
            keep(bh, bl, (half, k, re), factor * zr)
            keep(bh, bl, (half, k, im), factor * zi)
        for k in range(4):
            a = bh[half, k]
            tf[half, k] = dot(high[k], a) + dot(high[k], bl[half, k]) + dot(low[k], a)
        for t, p in enumerate(pair):
            cols = slice(t * quarter, (t + 1) * quarter)
            for r in range(0, quarter, step):
                quads = [
                    (
                        tf[half, k, r : r + step, cols],
                        tf[half, k, quarter + r : quarter + r + step, cols],
                    )
                    for k in range(4)
                ]
                for q, (yr, yi) in enumerate(mix_inverse(quads)):
                    rows = slice(q * quarter + r, q * quarter + r + step)
                    keep(ah, al, (p, rows, re), yr)
                    keep(ah, al, (p, rows, im), yi)

    for top in (0, block):
        rows = slice(top, top + block)
        for p in range(4):
            a = ah[p, rows, :]
            zf[p, rows, :] = dot(a, high[4 + p]) + dot(al[p, rows, :], high[4 + p]) + dot(a, low[4 + p])
        for base in range(top, top + block, step):
            rows = slice(base, base + step)
            quads = [(zf[p, rows, re], zf[p, rows, im]) for p in range(4)]
            grads = ([], [])
            for q, (br, bi) in enumerate(mix_inverse(quads)):
                cols = slice(q * quarter, (q + 1) * quarter)
                ar, ai = rolled[0, rows, cols], rolled[1, rows, cols]
                grads[0].append(ar * br + ai * bi)
                grads[1].append(ar * bi - ai * br)
            lane = lane_iota((step, LANES))
            for c in range(2):
                g = grads[c]
                wout = turn(jnp.where(lane >= v, g[0], 0.0))
                eout = turn(jnp.where(lane < HALF, jnp.where(lane < v, g[0], 0.0), g[3]))
                xout, dout = jnp.where(right, eout, wout), jnp.where(right, wout, eout)
                if OVL <= base < OVL + cells:
                    o = base - OVL
                    own[c, o : o + step, 0:128] = g[1]
                    own[c, o : o + step, 128:256] = g[2]
                    own[c, o : o + step, 256:cells] = g[3][:, : cells - 256]
                    xedge[c, o : o + step, :] = xout
                    dedge[c, o : o + step, :] = dout
                    continue
                row = row_iota((step, LANES)) + base
                sends = []
                if base < OVL:
                    sends.append((nblock, 0, base, row >= u if base < HALF else None))
                if base < HALF:
                    sends.append((sblock, OVL, base + HALF, row < u))
                if base >= OVL + cells:
                    sends.append((sblock, OVL, base - OVL - cells, None))
                for out, off, o, mask in sends:
                    put = (lambda x: x) if mask is None else (lambda x: jnp.where(mask, x, 0.0))
                    out[c, o : o + step, 0:128] = put(g[1])
                    out[c, o : o + step, 128:256] = put(g[2])
                    out[c, o : o + step, 256:384] = put(g[3])
                    xcorn[c, off + o : off + o + step, :] = put(xout)
                    dcorn[c, off + o : off + o + step, :] = put(dout)


def send_kernel(nblock, sblock, xcorn, dcorn, north, south):
    right = odd()
    first = lane_iota((OVL, LANES)) < HALF
    for base, block, out in ((0, nblock, north), (OVL, sblock, south)):
        last = []
        for c in range(2):
            x = xcorn[c, base : base + OVL, :]
            d = dcorn[c, base : base + OVL, :]
            fw, fe = jnp.where(right, d, x), jnp.where(right, x, d)
            out[:, c * 256 : c * 256 + 128] = block[c, :, 0:128] + fw
            out[:, c * 256 + 128 : c * 256 + 256] = block[c, :, 128:256] + jnp.where(first, 0.0, fe)
            last.append(block[c, :, 256:384] + fe)
        out[:, 512:640] = jnp.where(first, last[0], turn(last[1]))


def light_kernel(
    offs, xcorner, dcorner, north, south, probe, own, xedge, dedge, total, weight, pad, acc
):
    size = probe.shape[-1]
    cells = own.shape[1]
    pad[...] = jnp.zeros(pad.shape, F32)
    for t in range(4):
        cols = slice(t * LANES, (t + 1) * LANES)
        x = probe[0, :, cols]
        y = probe[1, :, cols]
        pad[1 + t, OVL : OVL + size, :] = x * x + y * y
    acc[...] = jnp.zeros(acc.shape, F32)
    first = lane_iota((HALF, LANES)) < HALF
    right = odd()
    unit = row_iota((8, LANES)) == 0
    lane = lane_iota((8, LANES))
    for di in (0, -1, 1):
        for dj in (0, -1, 1):
            if di == 0 and dj == 0:
                u, v, there = offs[0], offs[1], 1.0
            else:
                at = slice(4 * OVL + 8 * (di + 1), 4 * OVL + 8 * (di + 2))
                if dj == 0:
                    tile = (north if di < 0 else south)[OVL : OVL + 8, 0:128]
                elif dj < 0:
                    tile = jnp.where(right, dcorner[at, :], xcorner[at, :])
                else:
                    tile = jnp.where(right, xcorner[at, :], dcorner[at, :])
                u, v, there = [jnp.sum(jnp.where(unit & (lane == i), tile, 0.0)) for i in range(3)]
                u, v = u.astype(jnp.int32), v.astype(jnp.int32)
            start, count, put = {
                0: (2 * OVL - u, cells, 0),
                1: (OVL - u, OVL, cells - OVL),
                -1: (size + HALF - u, OVL, 0),
            }[di]
            seen = there
            for r in range(0, count, HALF):
                rows = pl.ds(start + r, HALF)
                to = slice(put + r, put + r + HALF)
                lo, hi, shift = {0: (1, 5, 384 + v), -1: (4, 6, lax.rem(192 + v, 256)), 1: (0, 2, 128 + v)}[dj]
                x = pltpu.roll(jnp.concatenate([pad[t, rows, :] for t in range(lo, hi)], axis=1), shift, 1)
                if dj == 0:
                    x = x[:, 0:384]
                    acc[to, :] += x * seen
                    continue
                if dj == -1:
                    x = x[:, 0:128]
                    acc[to, 0:128] += x * seen
                    continue
                x = turn(x[:, 0:128]) * seen
                acc[to, 128:256] += jnp.where(first, 0.0, x)
                acc[to, 256:384] += x
    for r in range(0, cells, HALF):
        rows = slice(r, r + HALF)
        for c in range(2):
            x, d = xedge[c, rows, :], dedge[c, rows, :]
            fw, fe = jnp.where(right, d, x), jnp.where(right, x, d)
            total[c, rows, 0:128] = own[c, rows, 0:128] + fw
            total[c, rows, 128:256] = own[c, rows, 128:256] + jnp.where(first, 0.0, fe)
            total[c, rows, 256:cells] = own[c, rows, 256:cells] + fe[:, : cells - 256]
        weight[rows, :] = STEP_SIZE / (acc[rows, 0:cells] + REGULAR)


def final_kernel(obj, total, weight, fromn, froms, updated):
    cells = obj.shape[1]
    for r in range(0, cells, HALF):
        rows = slice(r, r + HALF)
        for c in range(2):
            g = [total[c, rows, 0:128], total[c, rows, 128:256], total[c, rows, 256:cells]]
            adds = []
            if r < OVL:
                adds.append((fromn, r))
            if r >= cells - OVL:
                adds.append((froms, r - cells + OVL))
            for ref, o in adds:
                src = slice(o, o + HALF)
                g[0] = g[0] + ref[src, c * 256 : c * 256 + 128]
                g[1] = g[1] + ref[src, c * 256 + 128 : c * 256 + 256]
                g[2] = g[2] + ref[src, 512 + c * HALF : 512 + c * HALF + HALF]
            for t, x in enumerate(g):
                cols = slice(128 * t, min(128 * t + 128, cells))
                updated[c, rows, cols] = obj[c, rows, cols] - x * weight[rows, cols]


def routes(axis):
    count = lax.axis_size(axis)
    up = [(i, i - 1) for i in range(1, count)]
    down = [(i, i + 1) for i in range(count - 1)]
    swaps = [
        [pair for i in range(first, count - 1, 2) for pair in ((i, i + 1), (i + 1, i))]
        for first in (1, 0)
    ]
    return up, down, *swaps


def local(object_slab, probe_field, offsets, counts):
    cells = object_slab.shape[1]
    size = probe_field.shape[-1]
    up, down, _, _ = routes("row")
    _, _, cross, inner = routes("col")
    offs = offsets.reshape(2)
    table_high, table_low = tables(size)
    high, low = jnp.asarray(table_high), jnp.asarray(table_low)

    north, south, west, east = call(
        pack_kernel,
        [(OVL + 8, 640), (OVL + 8, 640), (2, cells, OVL), (2, cells, OVL)],
        [offs, object_slab],
        smem=(0,),
    )
    from_south = lax.ppermute(north, "row", up)
    from_north = lax.ppermute(south, "row", down)
    side_x = lax.ppermute(west, "col", cross)
    side_d = lax.ppermute(east, "col", inner)

    rolled, measured, token = call(
        ready_kernel,
        [(2, size, size), (size, size), (8, LANES)],
        [offs, probe_field, counts.reshape(size, size)],
        smem=(0,),
        scratch=[pltpu.VMEM((2, 4, size + HALF, LANES), F32)],
        flops=20_000_000_000,
    )
    xcorner, dcorner = call(
        corner_kernel,
        [(4 * OVL + 24, OVL), (4 * OVL + 24, OVL)],
        [offs, from_north, from_south, token],
        smem=(0,),
    )
    corner_x = lax.ppermute(xcorner, "col", cross)
    corner_d = lax.ppermute(dcorner, "col", inner)

    own, nblock, sblock, xedge, dedge, xcorn, dcorn = call(
        main_kernel,
        [
            (2, cells, cells),
            (2, OVL, 384),
            (2, OVL, 384),
            (2, cells, OVL),
            (2, cells, OVL),
            (2, 2 * OVL, OVL),
            (2, 2 * OVL, OVL),
        ],
        [
            offs,
            object_slab,
            from_north,
            from_south,
            side_x,
            side_d,
            corner_x,
            corner_d,
            rolled,
            measured,
            high,
            low,
        ],
        smem=(0,),
        scratch=[
            pltpu.VMEM((4, size, size // 2), BF16),
            pltpu.VMEM((4, size, size // 2), BF16),
            pltpu.VMEM((2, 4, size // 2, size // 2), BF16),
            pltpu.VMEM((2, 4, size // 2, size // 2), BF16),
            pltpu.VMEM((4, size, size // 2), F32),
            pltpu.VMEM((2, 4, size // 2, size // 2), F32),
        ],
        flops=5_000_000_000,
        limit=20,
    )
    fix_x = lax.ppermute(xcorn, "col", cross)
    fix_d = lax.ppermute(dcorn, "col", inner)
    nsend, ssend = call(send_kernel, [(OVL, 640), (OVL, 640)], [nblock, sblock, fix_x, fix_d])
    grad_s = lax.ppermute(nsend, "row", up)
    grad_n = lax.ppermute(ssend, "row", down)
    edge_x = lax.ppermute(xedge, "col", cross)
    edge_d = lax.ppermute(dedge, "col", inner)
    total, weight = call(
        light_kernel,
        [(2, cells, cells), (cells, cells)],
        [offs, corner_x, corner_d, from_north, from_south, probe_field, own, edge_x, edge_d],
        smem=(0,),
        scratch=[pltpu.VMEM((6, size + 2 * OVL, LANES), F32), pltpu.VMEM((cells, 384), F32)],
        flops=10_000_000_000,
    )
    (updated,) = call(
        final_kernel,
        [(2, cells, cells)],
        [object_slab, total, weight, grad_n, grad_s],
        hbm_out=True,
    )
    return updated


def solution(mesh):
    return jax.shard_map(
        local,
        mesh=mesh,
        in_specs=(
            P(None, "row", "col"),
            P(),
            P("row", "col", None, None),
            P("row", "col", None, None, None),
        ),
        out_specs=P(None, "row", "col"),
        check_vma=False,
    )
```

time: 83.2 us -> 70.8 us (0.85)
  starting transfers between devices: 39.2 us -> 24.3 us
  waiting for transfers between devices: 19.5 us -> 26.4 us
  Pallas kernels: 19 us -> 14.8 us
    ppermute x10 -> x8, starting transfers between devices: 26.8 us -> 11.9 us  [the longest x1 3.68 us: local(): side_x = lax.ppermute(west, 'col', cross)]
    ppermute x1, waiting for transfers between devices: 1.26 us -> 8.27 us  [local(): from_south = lax.ppermute(north, 'row', up)]
    pallas_call x7, Pallas kernels: 19 us -> 14.8 us  [call(): pl.pallas_call(kernel, out_shape=[jax.ShapeDtypeStruct(s, F32) if hbm_out...]
    ppermute x1, starting transfers between devices: 1.92 us -> 3.15 us  [local(): from_north = lax.ppermute(south, 'row', down)]
    ppermute x1, starting transfers between devices: 4.26 us -> 3.03 us  [local(): from_south = lax.ppermute(north, 'row', up)]
    ppermute x10 -> x8, waiting for transfers between devices: 11.7 us -> 10.8 us  [the longest x1 5.47 us: local(): fix_x = lax.ppermute(xcorn, 'col', cross)]
    unnamed x16 -> x18, local copies, waits for them, and re-layouts: 4.68 us -> 4.69 us
  transfers between devices with their start and end apart: 14 -> 12, of which waited for: 6 -> 5; matrix products, arithmetic and copies ran while one was open for 0% -> 0% of each run, Pallas kernels for 6% -> 9%
where the time goes in v2:
time: 70.8 us; the launch traced here: 70.4 us
  waiting for transfers between devices  26.4 us (37%)
  starting transfers between devices  24.3 us (34%)
  Pallas kernels  14.8 us (21%)
  local copies, waits for them, and re-layouts  4.69 us (7%)
    pallas_call x7, Pallas kernels, call(): pl.pallas_call(kernel, out_shape=[jax.ShapeDtypeStruct(s, F32) if hbm_out...  14.8 us
    ppermute x1, waiting for transfers between devices, local(): from_south = lax.ppermute(north, 'row', up)  8.27 us
    ppermute x1, waiting for transfers between devices, local(): grad_s = lax.ppermute(nsend, 'row', up)  6.7 us
    ppermute x1, waiting for transfers between devices, local(): fix_x = lax.ppermute(xcorn, 'col', cross)  5.47 us
    ppermute x1, waiting for transfers between devices, local(): corner_x = lax.ppermute(xcorner, 'col', cross)  5.33 us
    unnamed x18, local copies, waits for them, and re-layouts  4.69 us
    ppermute x1, starting transfers between devices, local(): grad_s = lax.ppermute(nsend, 'row', up)  4.26 us
    ppermute x1, starting transfers between devices, local(): side_x = lax.ppermute(west, 'col', cross)  3.68 us
  transfers between devices with their start and end apart: 12, of which 5 were waited for; matrix products, arithmetic and copies ran while one was open for 0% of the time, Pallas kernels for 9%

profile of v2, /device:TPU:25, one launch (start us, length us, event | category | flops | bytes accessed | tf_op | source)
XLA Modules:
  0.0 70.4 jit_solution(3023962399077635588)
XLA Ops:
  0.0 0.0 copy-start
  0.0 1.2 %copy-done = f32[2,320,320]{2,1,0:T(8,128)S(1)} copy-done((f32[2,320,320]{2,1,0:T(8,128)S(1)}, f32[2,320,320]{2,1,0:T(8,128)}, u32[]{:S(2)}) %copy-start) | copy-done | bytes 819224
  1.2 0.0 copy-start.2
  1.2 0.7 copy-done.2
  1.9 1.2 %shard_map.64 = (f32[136,640]{1,0:T(8,128)S(1)}, f32[136,640]{1,0:T(8,128)S(1)}, f32[2,320,128]{2,1,0:T(8,128)S(1)}, f32[2,320,128]{2,1,0:T(8,128)S(1)}) custom-call(s32[2]{0:T(128)S(1)} %bitcast.2, f32[2,320,320]{2,1,0:T(8,128)S(1)} %copy-done), custom_call_target="tpu_custom_call" | custom-call | tf_op jit(solution)/shard_map/pallas_call | solution.py:34
  3.1 3.7 %collective-permute-start.4 = (f32[2,320,128]{2,1,0:T(8,128)S(1)}, f32[2,320,128]{2,1,0:T(8,128)S(1)}, u32[]{:S(2)}, u32[]{:S(2)}) collective-permute-start(f32[2,320,128]{2,1,0:T(8,128)S(1)} %get-tuple-element.30), channel_id=1, source_target_pairs={{1,2},{2,1},{5,6},{6,5},{9,10},{10,9},{13,14},{14,13},{17,18},{18,... | collective-permute-start | bytes 983048 | tf_op jit(solution)/shard_map/ppermute | solution.py:450
  6.8 0.1 collective-permute-start.5
  6.9 3.1 %collective-permute-start = (f32[136,640]{1,0:T(8,128)S(1)}, f32[136,640]{1,0:T(8,128)S(1)}, u32[]{:S(2)}, u32[]{:S(2)}) collective-permute-start(f32[136,640]{1,0:T(8,128)S(1)} %get-tuple-element.25), channel_id=1, source_target_pairs={{0,4},{4,8},{8,12},{12,16},{16,20},{20,24},{24,28},{1,5},{5,9},{9,... | collective-permute-start | bytes 1044488 | tf_op jit(solution)/shard_map/ppermute | solution.py:449
  10.0 3.0 %collective-permute-start.1 = (f32[136,640]{1,0:T(8,128)S(1)}, f32[136,640]{1,0:T(8,128)S(1)}, u32[]{:S(2)}, u32[]{:S(2)}) collective-permute-start(f32[136,640]{1,0:T(8,128)S(1)} %get-tuple-element.26), channel_id=1, source_target_pairs={{4,0},{8,4},{12,8},{16,12},{20,16},{24,20},{28,24},{5,1},{9,5},{13... | collective-permute-start | bytes 1044488 | tf_op jit(solution)/shard_map/ppermute | solution.py:448
  13.1 0.0 copy-start.4
  13.1 1.6 %copy-done.4 = f32[2,512,512]{2,1,0:T(8,128)S(1)} copy-done((f32[2,512,512]{2,1,0:T(8,128)S(1)}, f32[2,512,512]{2,1,0:T(8,128)}, u32[]{:S(2)}) %copy-start.4) | copy-done | bytes 2097176
  14.7 0.0 copy-start.6
  14.7 1.2 %copy-done.6 = s32[1,1,1,512,512]{4,3,2,1,0:T(8,128)S(1)} copy-done((s32[1,1,1,512,512]{4,3,2,1,0:T(8,128)S(1)}, s32[1,1,1,512,512]{4,3,2,1,0:T(8,128)}, u32[]{:S(2)}) %copy-start.6) | copy-done | bytes 1048600
  15.9 0.0 copy-start.1
  15.9 0.0 copy-start.3
  15.9 0.0 copy-start.7
  15.9 0.0 copy-start.8
  15.9 2.4 %shard_map.65 = (f32[2,512,512]{2,1,0:T(8,128)S(1)}, f32[512,512]{1,0:T(8,128)S(1)}, f32[8,128]{1,0:T(8,128)S(1)}) custom-call(s32[2]{0:T(128)S(1)} %bitcast.3, f32[2,512,512]{2,1,0:T(8,128)S(1)} %copy-done.4, s32[512,512]{1,0:T(8,128)S(1)} %bitcast.7), custom_call_target="tpu_custom_call" | custom-call | flops 20000000000 | tf_op jit(solution)/shard_map/pallas_call | solution.py:34
  18.3 0.6 collective-permute-done.north
  18.9 8.3 %collective-permute-done.1.south = f32[136,640]{1,0:T(8,128)S(1)} collective-permute-done((f32[136,640]{1,0:T(8,128)S(1)}, f32[136,640]{1,0:T(8,128)S(1)}, u32[]{:S(2)}, u32[]{:S(2)}) %collective-permute-start.1) | collective-permute-done | bytes 348192 | tf_op jit(solution)/shard_map/ppermute | solution.py:448
  27.2 0.8 %shard_map.66 = (f32[536,128]{1,0:T(8,128)S(1)}, f32[536,128]{1,0:T(8,128)S(1)}) custom-call(s32[2]{0:T(128)S(1)} %bitcast.4, f32[136,640]{1,0:T(8,128)S(1)} %collective-permute-done.north, f32[136,640]{1,0:T(8,128)S(1)} %collective-permute-done.1.south, f32[8,128]{1,0:T(8,128)S(1)} %get-tuple-element.27.token), custom_call_target="tpu_custom_call" | custom-call | tf_op jit(solution)/shard_map/pallas_call | solution.py:34
  28.0 2.4 %collective-permute-start.2 = (f32[536,128]{1,0:T(8,128)S(1)}, f32[536,128]{1,0:T(8,128)S(1)}, u32[]{:S(2)}, u32[]{:S(2)}) collective-permute-start(f32[536,128]{1,0:T(8,128)S(1)} %get-tuple-element.28), channel_id=1, source_target_pairs={{1,2},{2,1},{5,6},{6,5},{9,10},{10,9},{13,14},{14,13},{17,18},{18,... | collective-permute-start | bytes 823304 | tf_op jit(solution)/shard_map/ppermute | solution.py:467
  30.4 0.1 collective-permute-start.3
  30.5 0.0 collective-permute-done.4.xside
  30.5 0.0 collective-permute-done.5.dside
  30.5 5.3 %collective-permute-done.2.xcorner = f32[536,128]{1,0:T(8,128)S(1)} collective-permute-done((f32[536,128]{1,0:T(8,128)S(1)}, f32[536,128]{1,0:T(8,128)S(1)}, u32[]{:S(2)}, u32[]{:S(2)}) %collective-permute-start.2) | collective-permute-done | bytes 274464 | tf_op jit(solution)/shard_map/ppermute | solution.py:467
  35.8 0.0 collective-permute-done.3.dcorner
  35.8 0.0 copy-done.1
  35.8 0.0 copy-done.3
  35.8 0.0 copy-done.7
  35.8 0.0 copy-done.8
  35.8 0.0 copy-start.5
  35.9 6.0 %shard_map.67 = (f32[2,320,320]{2,1,0:T(8,128)S(1)}, f32[2,128,384]{2,1,0:T(8,128)S(1)}, f32[2,128,384]{2,1,0:T(8,128)S(1)}, f32[2,320,128]{2,1,0:T(8,128)S(1)},...) custom-call(s32[2]{0:T(128)S(1)} %bitcast.5, f32[2,320,320]{2,1,0:T(8,128)S(1)} %copy-done.1, ...), custom_call_target="tpu_custom_call" | custom-call | flops 5000000000 | tf_op jit(solution)/shard_map/pallas_call | solution.py:34
  41.8 2.4 %collective-permute-start.6 = (f32[2,320,128]{2,1,0:T(8,128)S(1)}, f32[2,320,128]{2,1,0:T(8,128)S(1)}, u32[]{:S(2)}, u32[]{:S(2)}) collective-permute-start(f32[2,320,128]{2,1,0:T(8,128)S(1)} %get-tuple-element.35), channel_id=1, source_target_pairs={{1,2},{2,1},{5,6},{6,5},{9,10},{10,9},{13,14},{14,13},{17,18},{18,... | collective-permute-start | bytes 983048 | tf_op jit(solution)/shard_map/ppermute | solution.py:512
  44.2 0.1 collective-permute-start.7
  44.3 3.2 %collective-permute-start.8 = (f32[2,256,128]{2,1,0:T(8,128)S(1)}, f32[2,256,128]{2,1,0:T(8,128)S(1)}, u32[]{:S(2)}, u32[]{:S(2)}) collective-permute-start(f32[2,256,128]{2,1,0:T(8,128)S(1)} %get-tuple-element.41), channel_id=1, source_target_pairs={{1,2},{2,1},{5,6},{6,5},{9,10},{10,9},{13,14},{14,13},{17,18},{18,... | collective-permute-start | bytes 786440 | tf_op jit(solution)/shard_map/ppermute | solution.py:507
  47.5 0.1 collective-permute-start.9
  47.6 5.5 %collective-permute-done.8.xcorn = f32[2,256,128]{2,1,0:T(8,128)S(1)} collective-permute-done((f32[2,256,128]{2,1,0:T(8,128)S(1)}, f32[2,256,128]{2,1,0:T(8,128)S(1)}, u32[]{:S(2)}, u32[]{:S(2)}) %collective-permute-start.8) | collective-permute-done | bytes 262176 | tf_op jit(solution)/shard_map/ppermute | solution.py:507
  53.0 0.0 collective-permute-done.9.dcorn
  53.0 0.1 shard_map.69
  53.1 1.9 %collective-permute-start.10 = (f32[128,640]{1,0:T(8,128)S(1)}, f32[128,640]{1,0:T(8,128)S(1)}, u32[]{:S(2)}, u32[]{:S(2)}) collective-permute-start(f32[128,640]{1,0:T(8,128)S(1)} %get-tuple-element.43), channel_id=1, source_target_pairs={{0,4},{4,8},{8,12},{12,16},{16,20},{20,24},{24,28},{1,5},{5,9},{9,... | collective-permute-start | bytes 983048 | tf_op jit(solution)/shard_map/ppermute | solution.py:511
  55.1 4.3 %collective-permute-start.11 = (f32[128,640]{1,0:T(8,128)S(1)}, f32[128,640]{1,0:T(8,128)S(1)}, u32[]{:S(2)}, u32[]{:S(2)}) collective-permute-start(f32[128,640]{1,0:T(8,128)S(1)} %get-tuple-element.44), channel_id=1, source_target_pairs={{4,0},{8,4},{12,8},{16,12},{20,16},{24,20},{28,24},{5,1},{9,5},{13... | collective-permute-start | bytes 983048 | tf_op jit(solution)/shard_map/ppermute | solution.py:510
  59.3 0.0 collective-permute-done.6.xedge
  59.4 0.0 collective-permute-done.7.dedge
  59.4 0.0 copy-done.5
  59.4 3.2 %shard_map.68 = (f32[2,320,320]{2,1,0:T(8,128)S(1)}, f32[320,320]{1,0:T(8,128)S(1)}) custom-call(s32[2]{0:T(128)S(1)} %bitcast.6, f32[536,128]{1,0:T(8,128)S(1)} %collective-permute-done.2.xcorner, f32[536,128]{1,0:T(8,128)S(1)} %collective-permute-done.3.dcorner, f32[136,640]{1,0:T(8,128)S(1)} %collective-permute-done.north, ...), custom_call_target="tpu_custom_call" | custom-call | flops 10000000000 | tf_op jit(solution)/shard_map/pallas_call | solution.py:34
  62.5 0.0 collective-permute-done.10.fromn
  62.5 6.7 %collective-permute-done.11.froms = f32[128,640]{1,0:T(8,128)S(1)} collective-permute-done((f32[128,640]{1,0:T(8,128)S(1)}, f32[128,640]{1,0:T(8,128)S(1)}, u32[]{:S(2)}, u32[]{:S(2)}) %collective-permute-start.11) | collective-permute-done | bytes 327712 | tf_op jit(solution)/shard_map/ppermute | solution.py:510
  69.2 1.1 %shard_map.70 = f32[2,320,320]{2,1,0:T(8,128)} custom-call(f32[2,320,320]{2,1,0:T(8,128)S(1)} %copy-done.1, f32[2,320,320]{2,1,0:T(8,128)S(1)} %get-tuple-element.37.total, f32[320,320]{1,0:T(8,128)S(1)} %get-tuple-element.38.weight, f32[128,640]{1,0:T(8,128)S(1)} %collective-permute-done.10.fromn, f32[128,640]{1,0:T(8,128)S(1)} %collective-permute-done.11.froms), custom_call_target="tpu_custom_call" | custom-call | tf_op jit(solution)/shard_map/pallas_call | solution.py:34
Async XLA Ops:
  0.0 1.2 %copy-start = (f32[2,320,320]{2,1,0:T(8,128)S(1)}, f32[2,320,320]{2,1,0:T(8,128)}, u32[]{:S(2)}) copy-start(f32[2,320,320]{2,1,0:T(8,128)} %obj.5) | copy-start | bytes 2457604
  1.2 0.7 copy-start.2
  3.1 27.4 %collective-permute-start.4 = (f32[2,320,128]{2,1,0:T(8,128)S(1)}, f32[2,320,128]{2,1,0:T(8,128)S(1)}, u32[]{:S(2)}, u32[]{:S(2)}) collective-permute-start(f32[2,320,128]{2,1,0:T(8,128)S(1)} %get-tuple-element.30), channel_id=1, source_target_pairs={{1,2},{2,1},{5,6},{6,5},{9,10},{10,9},{13,14},{14,13},{17,18},{18,... | collective-permute-start | bytes 983048 | tf_op jit(solution)/shard_map/ppermute | solution.py:450
  6.8 23.7 %collective-permute-start.5 = (f32[2,320,128]{2,1,0:T(8,128)S(1)}, f32[2,320,128]{2,1,0:T(8,128)S(1)}, u32[]{:S(2)}, u32[]{:S(2)}) collective-permute-start(f32[2,320,128]{2,1,0:T(8,128)S(1)} %get-tuple-element.31), channel_id=1, source_target_pairs={{0,1},{1,0},{2,3},{3,2},{4,5},{5,4},{6,7},{7,6},{8,9},{9,8},{10,11... | collective-permute-start | bytes 983048 | tf_op jit(solution)/shard_map/ppermute | solution.py:451
  6.9 12.1 %collective-permute-start = (f32[136,640]{1,0:T(8,128)S(1)}, f32[136,640]{1,0:T(8,128)S(1)}, u32[]{:S(2)}, u32[]{:S(2)}) collective-permute-start(f32[136,640]{1,0:T(8,128)S(1)} %get-tuple-element.25), channel_id=1, source_target_pairs={{0,4},{4,8},{8,12},{12,16},{16,20},{20,24},{24,28},{1,5},{5,9},{9,... | collective-permute-start | bytes 1044488 | tf_op jit(solution)/shard_map/ppermute | solution.py:449
  10.0 17.2 %collective-permute-start.1 = (f32[136,640]{1,0:T(8,128)S(1)}, f32[136,640]{1,0:T(8,128)S(1)}, u32[]{:S(2)}, u32[]{:S(2)}) collective-permute-start(f32[136,640]{1,0:T(8,128)S(1)} %get-tuple-element.26), channel_id=1, source_target_pairs={{4,0},{8,4},{12,8},{16,12},{20,16},{24,20},{28,24},{5,1},{9,5},{13... | collective-permute-start | bytes 1044488 | tf_op jit(solution)/shard_map/ppermute | solution.py:448
  13.1 1.6 %copy-start.4 = (f32[2,512,512]{2,1,0:T(8,128)S(1)}, f32[2,512,512]{2,1,0:T(8,128)}, u32[]{:S(2)}) copy-start(f32[2,512,512]{2,1,0:T(8,128)} %probe.3) | copy-start | bytes 6291460
  14.7 1.2 %copy-start.6 = (s32[1,1,1,512,512]{4,3,2,1,0:T(8,128)S(1)}, s32[1,1,1,512,512]{4,3,2,1,0:T(8,128)}, u32[]{:S(2)}) copy-start(s32[1,1,1,512,512]{4,3,2,1,0:T(8,128)} %param.9) | copy-start | bytes 3145732
  15.9 19.9 %copy-start.1 = (f32[2,320,320]{2,1,0:T(8,128)S(1)}, f32[2,320,320]{2,1,0:T(8,128)}, u32[]{:S(2)}) copy-start(f32[2,320,320]{2,1,0:T(8,128)} %obj.5) | copy-start | bytes 2457604
  15.9 19.9 %copy-start.3 = (s32[1,1,1,2]{3,2,1,0:T(1,128)S(1)}, s32[1,1,1,2]{3,2,1,0:T(1,128)}, u32[]{:S(2)}) copy-start(s32[1,1,1,2]{3,2,1,0:T(1,128)} %param.8) | copy-start | bytes 28
  15.9 19.9 %copy-start.7 = (bf16[8,256,256]{2,1,0:T(8,128)(2,1)S(1)}, bf16[8,256,256]{2,1,0:T(8,128)(2,1)}, u32[]{:S(2)}) copy-start(bf16[8,256,256]{2,1,0:T(8,128)(2,1)} %constant.5.clone.low) | copy-start | bytes 3145732
  15.9 19.9 %copy-start.8 = (bf16[8,256,256]{2,1,0:T(8,128)(2,1)S(1)}, bf16[8,256,256]{2,1,0:T(8,128)(2,1)}, u32[]{:S(2)}) copy-start(bf16[8,256,256]{2,1,0:T(8,128)(2,1)} %constant.4.clone.high) | copy-start | bytes 3145732
  28.0 7.8 %collective-permute-start.2 = (f32[536,128]{1,0:T(8,128)S(1)}, f32[536,128]{1,0:T(8,128)S(1)}, u32[]{:S(2)}, u32[]{:S(2)}) collective-permute-start(f32[536,128]{1,0:T(8,128)S(1)} %get-tuple-element.28), channel_id=1, source_target_pairs={{1,2},{2,1},{5,6},{6,5},{9,10},{10,9},{13,14},{14,13},{17,18},{18,... | collective-permute-start | bytes 823304 | tf_op jit(solution)/shard_map/ppermute | solution.py:467
  30.4 5.4 %collective-permute-start.3 = (f32[536,128]{1,0:T(8,128)S(1)}, f32[536,128]{1,0:T(8,128)S(1)}, u32[]{:S(2)}, u32[]{:S(2)}) collective-permute-start(f32[536,128]{1,0:T(8,128)S(1)} %get-tuple-element.29), channel_id=1, source_target_pairs={{0,1},{1,0},{2,3},{3,2},{4,5},{5,4},{6,7},{7,6},{8,9},{9,8},{10,11... | collective-permute-start | bytes 823304 | tf_op jit(solution)/shard_map/ppermute | solution.py:468
  35.8 23.5 %copy-start.5 = (f32[2,512,512]{2,1,0:T(8,128)S(1)}, f32[2,512,512]{2,1,0:T(8,128)}, u32[]{:S(2)}) copy-start(f32[2,512,512]{2,1,0:T(8,128)} %probe.3) | copy-start | bytes 6291460
  41.8 17.5 %collective-permute-start.6 = (f32[2,320,128]{2,1,0:T(8,128)S(1)}, f32[2,320,128]{2,1,0:T(8,128)S(1)}, u32[]{:S(2)}, u32[]{:S(2)}) collective-permute-start(f32[2,320,128]{2,1,0:T(8,128)S(1)} %get-tuple-element.35), channel_id=1, source_target_pairs={{1,2},{2,1},{5,6},{6,5},{9,10},{10,9},{13,14},{14,13},{17,18},{18,... | collective-permute-start | bytes 983048 | tf_op jit(solution)/shard_map/ppermute | solution.py:512
  44.2 15.1 %collective-permute-start.7 = (f32[2,320,128]{2,1,0:T(8,128)S(1)}, f32[2,320,128]{2,1,0:T(8,128)S(1)}, u32[]{:S(2)}, u32[]{:S(2)}) collective-permute-start(f32[2,320,128]{2,1,0:T(8,128)S(1)} %get-tuple-element.36), channel_id=1, source_target_pairs={{0,1},{1,0},{2,3},{3,2},{4,5},{5,4},{6,7},{7,6},{8,9},{9,8},{10,11... | collective-permute-start | bytes 983048 | tf_op jit(solution)/shard_map/ppermute | solution.py:513
  44.3 8.7 %collective-permute-start.8 = (f32[2,256,128]{2,1,0:T(8,128)S(1)}, f32[2,256,128]{2,1,0:T(8,128)S(1)}, u32[]{:S(2)}, u32[]{:S(2)}) collective-permute-start(f32[2,256,128]{2,1,0:T(8,128)S(1)} %get-tuple-element.41), channel_id=1, source_target_pairs={{1,2},{2,1},{5,6},{6,5},{9,10},{10,9},{13,14},{14,13},{17,18},{18,... | collective-permute-start | bytes 786440 | tf_op jit(solution)/shard_map/ppermute | solution.py:507
  47.5 5.5 %collective-permute-start.9 = (f32[2,256,128]{2,1,0:T(8,128)S(1)}, f32[2,256,128]{2,1,0:T(8,128)S(1)}, u32[]{:S(2)}, u32[]{:S(2)}) collective-permute-start(f32[2,256,128]{2,1,0:T(8,128)S(1)} %get-tuple-element.42), channel_id=1, source_target_pairs={{0,1},{1,0},{2,3},{3,2},{4,5},{5,4},{6,7},{7,6},{8,9},{9,8},{10,11... | collective-permute-start | bytes 786440 | tf_op jit(solution)/shard_map/ppermute | solution.py:508
  53.1 9.4 %collective-permute-start.10 = (f32[128,640]{1,0:T(8,128)S(1)}, f32[128,640]{1,0:T(8,128)S(1)}, u32[]{:S(2)}, u32[]{:S(2)}) collective-permute-start(f32[128,640]{1,0:T(8,128)S(1)} %get-tuple-element.43), channel_id=1, source_target_pairs={{0,4},{4,8},{8,12},{12,16},{16,20},{20,24},{24,28},{1,5},{5,9},{9,... | collective-permute-start | bytes 983048 | tf_op jit(solution)/shard_map/ppermute | solution.py:511
  55.1 14.2 %collective-permute-start.11 = (f32[128,640]{1,0:T(8,128)S(1)}, f32[128,640]{1,0:T(8,128)S(1)}, u32[]{:S(2)}, u32[]{:S(2)}) collective-permute-start(f32[128,640]{1,0:T(8,128)S(1)} %get-tuple-element.44), channel_id=1, source_target_pairs={{4,0},{8,4},{12,8},{16,12},{20,16},{24,20},{28,24},{5,1},{9,5},{13... | collective-permute-start | bytes 983048 | tf_op jit(solution)/shard_map/ppermute | solution.py:510

commit v3 on v2

--- a/solution.py
+++ b/solution.py
@@ -99,21 +99,36 @@
     return pltpu.roll(x, HALF, len(x.shape) - 1)
 
 
-def odd():
-    return lax.axis_index("col") % 2 == 1
-
-
-def pack_kernel(offs, obj, north, south, xside, dside):
+def odd(axis):
+    return lax.axis_index(axis) % 2 == 1
+
+
+def row_kernel(offs, obj, inner, cross, held, numbers, sems):
     rows, cols = obj.shape[1:]
+    far = odd("row")
+    bases = jnp.where(far, 0, rows - OVL), jnp.where(far, rows - OVL, 0)
+    copies = [pltpu.make_async_copy(offs, numbers, sems.at[2])]
+    for t, base in enumerate(bases):
+        part = obj.at[:, pl.ds(pl.multiple_of(base, 8), OVL), :]
+        copies.append(pltpu.make_async_copy(part, held.at[t], sems.at[t]))
+    for copy in (copies[1], copies[0], copies[2]):
+        copy.start()
+    copies[0].wait()
     lane = lane_iota((8, LANES))
-    info = jnp.where(lane == 0, offs[0], jnp.where(lane == 1, offs[1], 1)).astype(F32)
-    for out, base in ((north, 0), (south, rows - OVL)):
-        for c in range(2):
-            out[0:OVL, c * 256 : c * 256 + 256] = obj[c, base : base + OVL, 0:256]
-            out[0:OVL, 512 + c * HALF : 512 + c * HALF + HALF] = obj[c, base : base + OVL, 256:cols]
+    first, second = numbers[0, 0, 0, 0], numbers[0, 0, 0, 1]
+    info = jnp.where(lane == 0, first, jnp.where(lane == 1, second, 1)).astype(F32)
+    for t, out in enumerate((inner, cross)):
         out[OVL : OVL + 8, 0:128] = info
         out[OVL : OVL + 8, 128:640] = jnp.zeros((8, 512), F32)
-    right = odd()
+        copies[1 + t].wait()
+        for c in range(2):
+            out[0:OVL, c * 256 : c * 256 + 256] = held[t, c, :, 0:256]
+            out[0:OVL, 512 + c * HALF : 512 + c * HALF + HALF] = held[t, c, :, 256:cols]
+
+
+def side_kernel(obj, xside, dside):
+    cols = obj.shape[2]
+    right = odd("col")
     for c in range(2):
         west = turn(obj[c, :, 0:128])
         east = obj[c, :, cols - OVL : cols]
@@ -121,25 +136,33 @@
         dside[c] = jnp.where(right, west, east)
 
 
-def corner_kernel(offs, north, south, token, xside, dside):
-    right = odd()
-    for part, halo in ((0, north), (1, south)):
+def corner_kernel(offs, inner, cross, token, xside, dside):
+    right = odd("col")
+    far = odd("row")
+
+    def halo(part, rows, cols):
+        a, b = inner[rows, cols], cross[rows, cols]
+        return jnp.where(far, a, b) if part == 0 else jnp.where(far, b, a)
+
+    top = slice(0, OVL)
+    for part in range(2):
         for c in range(2):
             rows = slice((2 * c + part) * OVL, (2 * c + part) * OVL + OVL)
-            west = turn(halo[0:OVL, c * 256 : c * 256 + 128])
+            west = turn(halo(part, top, slice(c * 256, c * 256 + 128)))
             lane = lane_iota((OVL, LANES))
-            tail = halo[0:OVL, 512:640]
+            tail = halo(part, top, slice(512, 640))
             if c == 0:
                 tail = turn(tail)
-            east = jnp.where(lane < HALF, turn(halo[0:OVL, c * 256 + 128 : c * 256 + 256]), tail)
+            middle = turn(halo(part, top, slice(c * 256 + 128, c * 256 + 256)))
+            east = jnp.where(lane < HALF, middle, tail)
             xside[rows, :] = jnp.where(right, east, west)
             dside[rows, :] = jnp.where(right, west, east)
     lane = lane_iota((8, LANES))
     info = jnp.where(lane == 0, offs[0], jnp.where(lane == 1, offs[1], 1)).astype(F32)
     for out in (xside, dside):
-        out[4 * OVL : 4 * OVL + 8, :] = north[OVL : OVL + 8, 0:128]
+        out[4 * OVL : 4 * OVL + 8, :] = halo(0, slice(OVL, OVL + 8), slice(0, 128))
         out[4 * OVL + 8 : 4 * OVL + 16, :] = info
-        out[4 * OVL + 16 : 4 * OVL + 24, :] = south[OVL : OVL + 8, 0:128]
+        out[4 * OVL + 16 : 4 * OVL + 24, :] = halo(1, slice(OVL, OVL + 8), slice(0, 128))
 
 
 def ready_kernel(offs, probe, counts, rolled, measured, token, wide):
@@ -171,7 +194,7 @@
 
 
 def main_kernel(
-    offs, obj, north, south, xside, dside, xcorner, dcorner, rolled, measured, high, low,
+    offs, obj, inner, cross, xside, dside, xcorner, dcorner, rolled, measured, high, low,
     own, nblock, sblock, xedge, dedge, xcorn, dcorn, ah, al, bh, bl, zf, tf,
 ):
     size = rolled.shape[-1]
@@ -179,7 +202,8 @@
     cells = obj.shape[1]
     u = offs[0]
     v = offs[1]
-    right = odd()
+    right = odd("col")
+    far = odd("row")
 
     def pieces(c, part, base, count):
         lane = lane_iota((count, LANES))
@@ -190,12 +214,13 @@
             x = xside[c, base : base + count, :]
             d = dside[c, base : base + count, :]
         else:
-            ref, start = (north, base) if part == "n" else (south, base)
-            tiles = [ref[start : start + count, c * 256 + 128 * t : c * 256 + 128 * t + 128] for t in range(2)]
-            last = ref[start : start + count, 512:640]
-            if c == 1:
-                last = turn(last)
-            start = start + (2 * c + (part == "s")) * OVL
+            tiles = []
+            for at in (c * 256, c * 256 + 128, 512):
+                x = inner[base : base + count, at : at + 128]
+                d = cross[base : base + count, at : at + 128]
+                tiles.append(jnp.where(far, x, d) if part == "n" else jnp.where(far, d, x))
+            last = turn(tiles[2]) if c == 1 else tiles[2]
+            start = base + (2 * c + (part == "s")) * OVL
             x = xcorner[start : start + count, :]
             d = dcorner[start : start + count, :]
         w, e = jnp.where(right, d, x), jnp.where(right, x, d)
@@ -320,26 +345,31 @@
                     dcorn[c, off + o : off + o + step, :] = put(dout)
 
 
-def send_kernel(nblock, sblock, xcorn, dcorn, north, south):
-    right = odd()
+def send_kernel(nblock, sblock, xcorn, dcorn, inner, cross):
+    right = odd("col")
+    far = odd("row")
     first = lane_iota((OVL, LANES)) < HALF
-    for base, block, out in ((0, nblock, north), (OVL, sblock, south)):
-        last = []
+    tiles = []
+    for base, block in ((0, nblock), (OVL, sblock)):
+        last, part = [], []
         for c in range(2):
             x = xcorn[c, base : base + OVL, :]
             d = dcorn[c, base : base + OVL, :]
             fw, fe = jnp.where(right, d, x), jnp.where(right, x, d)
-            out[:, c * 256 : c * 256 + 128] = block[c, :, 0:128] + fw
-            out[:, c * 256 + 128 : c * 256 + 256] = block[c, :, 128:256] + jnp.where(first, 0.0, fe)
+            part.append(block[c, :, 0:128] + fw)
+            part.append(block[c, :, 128:256] + jnp.where(first, 0.0, fe))
             last.append(block[c, :, 256:384] + fe)
-        out[:, 512:640] = jnp.where(first, last[0], turn(last[1]))
-
-
-def light_kernel(
-    offs, xcorner, dcorner, north, south, probe, own, xedge, dedge, total, weight, pad, acc
-):
+        part.append(jnp.where(first, last[0], turn(last[1])))
+        tiles.append(part)
+    for t, (n, s) in enumerate(zip(*tiles)):
+        inner[:, t * 128 : t * 128 + 128] = jnp.where(far, n, s)
+        cross[:, t * 128 : t * 128 + 128] = jnp.where(far, s, n)
+
+
+def light_kernel(offs, xcorner, dcorner, inner, cross, probe, weight, pad, acc):
     size = probe.shape[-1]
-    cells = own.shape[1]
+    cells = weight.shape[0]
+    far = odd("row")
     pad[...] = jnp.zeros(pad.shape, F32)
     for t in range(4):
         cols = slice(t * LANES, (t + 1) * LANES)
@@ -348,7 +378,7 @@
         pad[1 + t, OVL : OVL + size, :] = x * x + y * y
     acc[...] = jnp.zeros(acc.shape, F32)
     first = lane_iota((HALF, LANES)) < HALF
-    right = odd()
+    right = odd("col")
     unit = row_iota((8, LANES)) == 0
     lane = lane_iota((8, LANES))
     for di in (0, -1, 1):
@@ -358,7 +388,8 @@
             else:
                 at = slice(4 * OVL + 8 * (di + 1), 4 * OVL + 8 * (di + 2))
                 if dj == 0:
-                    tile = (north if di < 0 else south)[OVL : OVL + 8, 0:128]
+                    a, b = inner[OVL : OVL + 8, 0:128], cross[OVL : OVL + 8, 0:128]
+                    tile = jnp.where(far, a, b) if di < 0 else jnp.where(far, b, a)
                 elif dj < 0:
                     tile = jnp.where(right, dcorner[at, :], xcorner[at, :])
                 else:
@@ -389,66 +420,81 @@
                 acc[to, 256:384] += x
     for r in range(0, cells, HALF):
         rows = slice(r, r + HALF)
+        weight[rows, :] = STEP_SIZE / (acc[rows, 0:cells] + REGULAR)
+
+
+def final_kernel(obj, own, weight, xedge, dedge, inner, cross, updated):
+    cells = obj.shape[1]
+    right = odd("col")
+    far = odd("row")
+    first = lane_iota((HALF, LANES)) < HALF
+    for r in range(0, cells, HALF):
+        rows = slice(r, r + HALF)
         for c in range(2):
             x, d = xedge[c, rows, :], dedge[c, rows, :]
             fw, fe = jnp.where(right, d, x), jnp.where(right, x, d)
-            total[c, rows, 0:128] = own[c, rows, 0:128] + fw
-            total[c, rows, 128:256] = own[c, rows, 128:256] + jnp.where(first, 0.0, fe)
-            total[c, rows, 256:cells] = own[c, rows, 256:cells] + fe[:, : cells - 256]
-        weight[rows, :] = STEP_SIZE / (acc[rows, 0:cells] + REGULAR)
-
-
-def final_kernel(obj, total, weight, fromn, froms, updated):
-    cells = obj.shape[1]
-    for r in range(0, cells, HALF):
-        rows = slice(r, r + HALF)
-        for c in range(2):
-            g = [total[c, rows, 0:128], total[c, rows, 128:256], total[c, rows, 256:cells]]
+            g = [
+                own[c, rows, 0:128] + fw,
+                own[c, rows, 128:256] + jnp.where(first, 0.0, fe),
+                own[c, rows, 256:cells] + fe[:, : cells - 256],
+            ]
             adds = []
             if r < OVL:
-                adds.append((fromn, r))
+                adds.append((0, r))
             if r >= cells - OVL:
-                adds.append((froms, r - cells + OVL))
-            for ref, o in adds:
+                adds.append((1, r - cells + OVL))
+            for part, o in adds:
                 src = slice(o, o + HALF)
-                g[0] = g[0] + ref[src, c * 256 : c * 256 + 128]
-                g[1] = g[1] + ref[src, c * 256 + 128 : c * 256 + 256]
-                g[2] = g[2] + ref[src, 512 + c * HALF : 512 + c * HALF + HALF]
+
+                def take(cols):
+                    a, b = inner[src, cols], cross[src, cols]
+                    return jnp.where(far, a, b) if part == 0 else jnp.where(far, b, a)
+
+                g[0] = g[0] + take(slice(c * 256, c * 256 + 128))
+                g[1] = g[1] + take(slice(c * 256 + 128, c * 256 + 256))
+                g[2] = g[2] + take(slice(512 + c * HALF, 512 + c * HALF + HALF))
             for t, x in enumerate(g):
                 cols = slice(128 * t, min(128 * t + 128, cells))
                 updated[c, rows, cols] = obj[c, rows, cols] - x * weight[rows, cols]
 
 
-def routes(axis):
+def swaps(axis):
     count = lax.axis_size(axis)
-    up = [(i, i - 1) for i in range(1, count)]
-    down = [(i, i + 1) for i in range(count - 1)]
-    swaps = [
+    return [
         [pair for i in range(first, count - 1, 2) for pair in ((i, i + 1), (i + 1, i))]
         for first in (1, 0)
     ]
-    return up, down, *swaps
 
 
 def local(object_slab, probe_field, offsets, counts):
     cells = object_slab.shape[1]
     size = probe_field.shape[-1]
-    up, down, _, _ = routes("row")
-    _, _, cross, inner = routes("col")
+    row_cross, row_inner = swaps("row")
+    col_cross, col_inner = swaps("col")
     offs = offsets.reshape(2)
     table_high, table_low = tables(size)
     high, low = jnp.asarray(table_high), jnp.asarray(table_low)
 
-    north, south, west, east = call(
-        pack_kernel,
-        [(OVL + 8, 640), (OVL + 8, 640), (2, cells, OVL), (2, cells, OVL)],
-        [offs, object_slab],
-        smem=(0,),
-    )
-    from_south = lax.ppermute(north, "row", up)
-    from_north = lax.ppermute(south, "row", down)
-    side_x = lax.ppermute(west, "col", cross)
-    side_d = lax.ppermute(east, "col", inner)
+    to_inner, to_cross = pl.pallas_call(
+        row_kernel,
+        name="rows",
+        out_shape=[pltpu.VMEM((OVL + 8, 640), F32) for _ in range(2)],
+        in_specs=[pl.BlockSpec(memory_space=pltpu.HBM) for _ in range(2)],
+        out_specs=[pl.BlockSpec(memory_space=pltpu.VMEM) for _ in range(2)],
+        scratch_shapes=[
+            pltpu.VMEM((2, 2, OVL, cells), F32),
+            pltpu.SMEM((1, 1, 1, 2), jnp.int32),
+            pltpu.SemaphoreType.DMA((3,)),
+        ],
+        compiler_params=pltpu.CompilerParams(vmem_limit_bytes=8 * 1024 * 1024),
+    )(*[pltpu.with_memory_space_constraint(x, pltpu.HBM) for x in (offsets, object_slab)])
+    halo_inner = lax.ppermute(to_inner, "row", row_inner)
+    halo_cross = lax.ppermute(to_cross, "row", row_cross)
+    xside, dside = call(
+        side_kernel, [(2, cells, OVL), (2, cells, OVL)], [object_slab], flops=5_000_000_000
+    )
+    side_x = lax.ppermute(xside, "col", col_cross)
+    side_d = lax.ppermute(dside, "col", col_inner)
 
     rolled, measured, token = call(
         ready_kernel,
@@ -461,11 +507,11 @@
     xcorner, dcorner = call(
         corner_kernel,
         [(4 * OVL + 24, OVL), (4 * OVL + 24, OVL)],
-        [offs, from_north, from_south, token],
+        [offs, halo_inner, halo_cross, token],
         smem=(0,),
     )
-    corner_x = lax.ppermute(xcorner, "col", cross)
-    corner_d = lax.ppermute(dcorner, "col", inner)
+    corner_x = lax.ppermute(xcorner, "col", col_cross)
+    corner_d = lax.ppermute(dcorner, "col", col_inner)
 
     own, nblock, sblock, xedge, dedge, xcorn, dcorn = call(
         main_kernel,
@@ -481,8 +527,8 @@
         [
             offs,
             object_slab,
-            from_north,
-            from_south,
+            halo_inner,
+            halo_cross,
             side_x,
             side_d,
             corner_x,
@@ -504,17 +550,17 @@
         flops=5_000_000_000,
         limit=20,
     )
-    fix_x = lax.ppermute(xcorn, "col", cross)
-    fix_d = lax.ppermute(dcorn, "col", inner)
-    nsend, ssend = call(send_kernel, [(OVL, 640), (OVL, 640)], [nblock, sblock, fix_x, fix_d])
-    grad_s = lax.ppermute(nsend, "row", up)
-    grad_n = lax.ppermute(ssend, "row", down)
-    edge_x = lax.ppermute(xedge, "col", cross)
-    edge_d = lax.ppermute(dedge, "col", inner)
-    total, weight = call(
+    fix_x = lax.ppermute(xcorn, "col", col_cross)
+    fix_d = lax.ppermute(dcorn, "col", col_inner)
+    to_inner, to_cross = call(send_kernel, [(OVL, 640), (OVL, 640)], [nblock, sblock, fix_x, fix_d])
+    grad_inner = lax.ppermute(to_inner, "row", row_inner)
+    grad_cross = lax.ppermute(to_cross, "row", row_cross)
+    edge_x = lax.ppermute(xedge, "col", col_cross)
+    edge_d = lax.ppermute(dedge, "col", col_inner)
+    (weight,) = call(
         light_kernel,
-        [(2, cells, cells), (cells, cells)],
-        [offs, corner_x, corner_d, from_north, from_south, probe_field, own, edge_x, edge_d],
+        [(cells, cells)],
+        [offs, corner_x, corner_d, halo_inner, halo_cross, probe_field],
         smem=(0,),
         scratch=[pltpu.VMEM((6, size + 2 * OVL, LANES), F32), pltpu.VMEM((cells, 384), F32)],
         flops=10_000_000_000,
@@ -522,7 +568,7 @@
     (updated,) = call(
         final_kernel,
         [(2, cells, cells)],
-        [object_slab, total, weight, grad_n, grad_s],
+        [object_slab, own, weight, edge_x, edge_d, grad_inner, grad_cross],
         hbm_out=True,
     )
     return updated

time: 70.8 us -> 63.4 us (0.90)
  the two profiles are of different devices: /device:TPU:25 before, /device:TPU:1 now
where the time goes in v3:
time: 63.4 us; the launch traced here: 63.2 us
  waiting for transfers between devices  27.6 us (44%)
  starting transfers between devices  18.6 us (29%)
  Pallas kernels  15.5 us (24%)
  local copies, waits for them, and re-layouts  1.23 us (2%)
    pallas_call x7, Pallas kernels, call(): pl.pallas_call(kernel, out_shape=[jax.ShapeDtypeStruct(s, F32) if hbm_out...  14.3 us
    ppermute x1, waiting for transfers between devices, local(): halo_inner = lax.ppermute(to_inner, 'row', row_inner)  11.3 us
    ppermute x1, waiting for transfers between devices, local(): grad_inner = lax.ppermute(to_inner, 'row', row_inner)  9.76 us
    ppermute x1, starting transfers between devices, local(): side_x = lax.ppermute(xside, 'col', col_cross)  4.63 us
    ppermute x1, waiting for transfers between devices, local(): corner_x = lax.ppermute(xcorner, 'col', col_cross)  4.5 us
    ppermute x1, starting transfers between devices, local(): corner_x = lax.ppermute(xcorner, 'col', col_cross)  3.22 us
    ppermute x1, starting transfers between devices, local(): fix_x = lax.ppermute(xcorn, 'col', col_cross)  3.21 us
    ppermute x1, starting transfers between devices, local(): edge_x = lax.ppermute(xedge, 'col', col_cross)  2.35 us
  transfers between devices with their start and end apart: 12, of which 4 were waited for; matrix products, arithmetic and copies ran while one was open for 0% of the time, Pallas kernels for 12%

profile of v3, /device:TPU:1, one launch (start us, length us, event | category | flops | bytes accessed | tf_op | source)
XLA Modules:
  0.0 63.2 jit_solution(4113563819422034000)
XLA Ops:
  0.0 0.0 copy-start
  0.0 1.2 %copy-done = f32[2,320,320]{2,1,0:T(8,128)S(1)} copy-done((f32[2,320,320]{2,1,0:T(8,128)S(1)}, f32[2,320,320]{2,1,0:T(8,128)}, u32[]{:S(2)}) %copy-start) | copy-done | bytes 819224
  1.2 0.0 copy-start.2
  1.2 0.0 copy-start.3
  1.2 0.0 copy-start.4
  1.2 0.7 %shard_map.64 = (f32[2,320,128]{2,1,0:T(8,128)S(1)}, f32[2,320,128]{2,1,0:T(8,128)S(1)}) custom-call(f32[2,320,320]{2,1,0:T(8,128)S(1)} %copy-done), custom_call_target="tpu_custom_call" | custom-call | flops 5000000000 | tf_op jit(solution)/shard_map/pallas_call | solution.py:34
  1.9 4.6 %collective-permute-start.2 = (f32[2,320,128]{2,1,0:T(8,128)S(1)}, f32[2,320,128]{2,1,0:T(8,128)S(1)}, u32[]{:S(2)}, u32[]{:S(2)}) collective-permute-start(f32[2,320,128]{2,1,0:T(8,128)S(1)} %get-tuple-element.25), channel_id=1, source_target_pairs={{1,2},{2,1},{5,6},{6,5},{9,10},{10,9},{13,14},{14,13},{17,18},{18,... | collective-permute-start | bytes 983048 | tf_op jit(solution)/shard_map/ppermute | solution.py:496
  6.5 0.1 collective-permute-start.3
  6.6 1.3 %rows.1 = (f32[136,640]{1,0:T(8,128)S(1)}, f32[136,640]{1,0:T(8,128)S(1)}) custom-call(s32[1,1,1,2]{3,2,1,0:T(1,128)} %offs.1, f32[2,320,320]{2,1,0:T(8,128)} %obj.7), custom_call_target="tpu_custom_call" | custom-call | tf_op jit(solution)/shard_map/rows/pallas_call | solution.py:478
  7.9 1.3 %collective-permute-start = (f32[136,640]{1,0:T(8,128)S(1)}, f32[136,640]{1,0:T(8,128)S(1)}, u32[]{:S(2)}, u32[]{:S(2)}) collective-permute-start(f32[136,640]{1,0:T(8,128)S(1)} %get-tuple-element.23), channel_id=1, source_target_pairs={{0,4},{4,0},{8,12},{12,8},{16,20},{20,16},{24,28},{28,24},{1,5},{5... | collective-permute-start | bytes 1044488 | tf_op jit(solution)/shard_map/ppermute | solution.py:491
  9.2 0.7 %collective-permute-start.1 = (f32[136,640]{1,0:T(8,128)S(1)}, f32[136,640]{1,0:T(8,128)S(1)}, u32[]{:S(2)}, u32[]{:S(2)}) collective-permute-start(f32[136,640]{1,0:T(8,128)S(1)} %get-tuple-element.24), channel_id=1, source_target_pairs={{4,8},{8,4},{12,16},{16,12},{20,24},{24,20},{5,9},{9,5},{13,17},{1... | collective-permute-start | bytes 1044488 | tf_op jit(solution)/shard_map/ppermute | solution.py:492
  9.9 0.0 copy-done.2
  9.9 0.0 copy-done.3
  9.9 0.0 copy-done.4
  9.9 0.0 copy-start.1
  9.9 0.0 copy-start.5
  9.9 0.0 copy-start.6
  9.9 2.4 %shard_map.65 = (f32[2,512,512]{2,1,0:T(8,128)S(1)}, f32[512,512]{1,0:T(8,128)S(1)}, f32[8,128]{1,0:T(8,128)S(1)}) custom-call(s32[2]{0:T(128)S(1)} %bitcast.2, f32[2,512,512]{2,1,0:T(8,128)S(1)} %copy-done.3, s32[512,512]{1,0:T(8,128)S(1)} %bitcast.6), custom_call_target="tpu_custom_call" | custom-call | flops 20000000000 | tf_op jit(solution)/shard_map/pallas_call | solution.py:34
  12.3 11.3 %collective-permute-done.inner = f32[136,640]{1,0:T(8,128)S(1)} collective-permute-done((f32[136,640]{1,0:T(8,128)S(1)}, f32[136,640]{1,0:T(8,128)S(1)}, u32[]{:S(2)}, u32[]{:S(2)}) %collective-permute-start) | collective-permute-done | bytes 348192 | tf_op jit(solution)/shard_map/ppermute | solution.py:491
  23.7 0.0 collective-permute-done.1.cross
  23.7 0.8 %shard_map.66 = (f32[536,128]{1,0:T(8,128)S(1)}, f32[536,128]{1,0:T(8,128)S(1)}) custom-call(s32[2]{0:T(128)S(1)} %bitcast.3, f32[136,640]{1,0:T(8,128)S(1)} %collective-permute-done.inner, f32[136,640]{1,0:T(8,128)S(1)} %collective-permute-done.1.cross, f32[8,128]{1,0:T(8,128)S(1)} %get-tuple-element.27.token), custom_call_target="tpu_custom_call" | custom-call | tf_op jit(solution)/shard_map/pallas_call | solution.py:34
  24.5 3.2 %collective-permute-start.4 = (f32[536,128]{1,0:T(8,128)S(1)}, f32[536,128]{1,0:T(8,128)S(1)}, u32[]{:S(2)}, u32[]{:S(2)}) collective-permute-start(f32[536,128]{1,0:T(8,128)S(1)} %get-tuple-element.28), channel_id=1, source_target_pairs={{1,2},{2,1},{5,6},{6,5},{9,10},{10,9},{13,14},{14,13},{17,18},{18,... | collective-permute-start | bytes 823304 | tf_op jit(solution)/shard_map/ppermute | solution.py:513
  27.7 0.1 collective-permute-start.5
  27.8 0.0 collective-permute-done.2.xside
  27.8 0.0 collective-permute-done.3.dside
  27.8 4.5 %collective-permute-done.4.xcorner = f32[536,128]{1,0:T(8,128)S(1)} collective-permute-done((f32[536,128]{1,0:T(8,128)S(1)}, f32[536,128]{1,0:T(8,128)S(1)}, u32[]{:S(2)}, u32[]{:S(2)}) %collective-permute-start.4) | collective-permute-done | bytes 274464 | tf_op jit(solution)/shard_map/ppermute | solution.py:513
  32.3 0.0 collective-permute-done.5.dcorner
  32.3 0.0 copy-done.1
  32.3 0.0 copy-done.5
  32.3 0.0 copy-done.6
  32.3 6.0 %shard_map.67 = (f32[2,320,320]{2,1,0:T(8,128)S(1)}, f32[2,128,384]{2,1,0:T(8,128)S(1)}, f32[2,128,384]{2,1,0:T(8,128)S(1)}, f32[2,320,128]{2,1,0:T(8,128)S(1)},...) custom-call(s32[2]{0:T(128)S(1)} %bitcast.4, f32[2,320,320]{2,1,0:T(8,128)S(1)} %copy-done.1, ...), custom_call_target="tpu_custom_call" | custom-call | flops 5000000000 | tf_op jit(solution)/shard_map/pallas_call | solution.py:34
  38.3 3.2 %collective-permute-start.8 = (f32[2,256,128]{2,1,0:T(8,128)S(1)}, f32[2,256,128]{2,1,0:T(8,128)S(1)}, u32[]{:S(2)}, u32[]{:S(2)}) collective-permute-start(f32[2,256,128]{2,1,0:T(8,128)S(1)} %get-tuple-element.37), channel_id=1, source_target_pairs={{1,2},{2,1},{5,6},{6,5},{9,10},{10,9},{13,14},{14,13},{17,18},{18,... | collective-permute-start | bytes 786440 | tf_op jit(solution)/shard_map/ppermute | solution.py:553
  41.5 0.1 collective-permute-start.9
  41.6 2.3 %collective-permute-start.6 = (f32[2,320,128]{2,1,0:T(8,128)S(1)}, f32[2,320,128]{2,1,0:T(8,128)S(1)}, u32[]{:S(2)}, u32[]{:S(2)}) collective-permute-start(f32[2,320,128]{2,1,0:T(8,128)S(1)} %get-tuple-element.33), channel_id=1, source_target_pairs={{1,2},{2,1},{5,6},{6,5},{9,10},{10,9},{13,14},{14,13},{17,18},{18,... | collective-permute-start | bytes 983048 | tf_op jit(solution)/shard_map/ppermute | solution.py:558
  43.9 0.1 collective-permute-start.7
  44.0 2.0 %collective-permute-done.8.xcorn = f32[2,256,128]{2,1,0:T(8,128)S(1)} collective-permute-done((f32[2,256,128]{2,1,0:T(8,128)S(1)}, f32[2,256,128]{2,1,0:T(8,128)S(1)}, u32[]{:S(2)}, u32[]{:S(2)}) %collective-permute-start.8) | collective-permute-done | bytes 262176 | tf_op jit(solution)/shard_map/ppermute | solution.py:553
  46.0 0.0 collective-permute-done.9.dcorn
  46.0 0.1 shard_map.69
  46.1 2.3 %collective-permute-start.10 = (f32[128,640]{1,0:T(8,128)S(1)}, f32[128,640]{1,0:T(8,128)S(1)}, u32[]{:S(2)}, u32[]{:S(2)}) collective-permute-start(f32[128,640]{1,0:T(8,128)S(1)} %get-tuple-element.39), channel_id=1, source_target_pairs={{0,4},{4,0},{8,12},{12,8},{16,20},{20,16},{24,28},{28,24},{1,5},{5... | collective-permute-start | bytes 983048 | tf_op jit(solution)/shard_map/ppermute | solution.py:556
  48.4 0.7 %collective-permute-start.11 = (f32[128,640]{1,0:T(8,128)S(1)}, f32[128,640]{1,0:T(8,128)S(1)}, u32[]{:S(2)}, u32[]{:S(2)}) collective-permute-start(f32[128,640]{1,0:T(8,128)S(1)} %get-tuple-element.40), channel_id=1, source_target_pairs={{4,8},{8,4},{12,16},{16,12},{20,24},{24,20},{5,9},{9,5},{13,17},{1... | collective-permute-start | bytes 983048 | tf_op jit(solution)/shard_map/ppermute | solution.py:557
  49.1 3.1 %shard_map.68.weight = f32[320,320]{1,0:T(8,128)S(1)} custom-call(s32[2]{0:T(128)S(1)} %bitcast.5, f32[536,128]{1,0:T(8,128)S(1)} %collective-permute-done.4.xcorner, f32[536,128]{1,0:T(8,128)S(1)} %collective-permute-done.5.dcorner, f32[136,640]{1,0:T(8,128)S(1)} %collective-permute-done.inner, f32[136,640]{1,0:T(8,128)S(1)} %collective-permute-done.1.cross, ...), custom_call_target="tpu_custom_call" | custom-call | flops 10000000000 | tf_op jit(solution)/shard_map/pallas_call | solution.py:34
  52.2 0.0 collective-permute-done.6.xedge
  52.2 0.0 collective-permute-done.7.dedge
  52.2 9.8 %collective-permute-done.10.inner = f32[128,640]{1,0:T(8,128)S(1)} collective-permute-done((f32[128,640]{1,0:T(8,128)S(1)}, f32[128,640]{1,0:T(8,128)S(1)}, u32[]{:S(2)}, u32[]{:S(2)}) %collective-permute-start.10) | collective-permute-done | bytes 327712 | tf_op jit(solution)/shard_map/ppermute | solution.py:556
  61.9 0.0 collective-permute-done.11.cross
  61.9 1.2 %shard_map.70 = f32[2,320,320]{2,1,0:T(8,128)} custom-call(f32[2,320,320]{2,1,0:T(8,128)S(1)} %copy-done.1, f32[2,320,320]{2,1,0:T(8,128)S(1)} %get-tuple-element.32.own, f32[320,320]{1,0:T(8,128)S(1)} %shard_map.68.weight, f32[2,320,128]{2,1,0:T(8,128)S(1)} %collective-permute-done.6.xedge, f32[2,320,128]{2,1,0:T(8,128)S(1)} %collective-permute-done.7.dedge, ...), custom_call_target="tpu_custom_call" | custom-call | tf_op jit(solution)/shard_map/pallas_call | solution.py:34
Async XLA Ops:
  0.0 1.2 %copy-start = (f32[2,320,320]{2,1,0:T(8,128)S(1)}, f32[2,320,320]{2,1,0:T(8,128)}, u32[]{:S(2)}) copy-start(f32[2,320,320]{2,1,0:T(8,128)} %obj.7) | copy-start | bytes 2457604
  1.2 8.7 %copy-start.2 = (s32[1,1,1,2]{3,2,1,0:T(1,128)S(1)}, s32[1,1,1,2]{3,2,1,0:T(1,128)}, u32[]{:S(2)}) copy-start(s32[1,1,1,2]{3,2,1,0:T(1,128)} %offs.1) | copy-start | bytes 28
  1.2 8.7 %copy-start.3 = (f32[2,512,512]{2,1,0:T(8,128)S(1)}, f32[2,512,512]{2,1,0:T(8,128)}, u32[]{:S(2)}) copy-start(f32[2,512,512]{2,1,0:T(8,128)} %probe.3) | copy-start | bytes 6291460
  1.2 8.7 %copy-start.4 = (s32[1,1,1,512,512]{4,3,2,1,0:T(8,128)S(1)}, s32[1,1,1,512,512]{4,3,2,1,0:T(8,128)}, u32[]{:S(2)}) copy-start(s32[1,1,1,512,512]{4,3,2,1,0:T(8,128)} %param.9) | copy-start | bytes 3145732
  1.9 25.9 %collective-permute-start.2 = (f32[2,320,128]{2,1,0:T(8,128)S(1)}, f32[2,320,128]{2,1,0:T(8,128)S(1)}, u32[]{:S(2)}, u32[]{:S(2)}) collective-permute-start(f32[2,320,128]{2,1,0:T(8,128)S(1)} %get-tuple-element.25), channel_id=1, source_target_pairs={{1,2},{2,1},{5,6},{6,5},{9,10},{10,9},{13,14},{14,13},{17,18},{18,... | collective-permute-start | bytes 983048 | tf_op jit(solution)/shard_map/ppermute | solution.py:496
  6.5 21.3 %collective-permute-start.3 = (f32[2,320,128]{2,1,0:T(8,128)S(1)}, f32[2,320,128]{2,1,0:T(8,128)S(1)}, u32[]{:S(2)}, u32[]{:S(2)}) collective-permute-start(f32[2,320,128]{2,1,0:T(8,128)S(1)} %get-tuple-element.26), channel_id=1, source_target_pairs={{0,1},{1,0},{2,3},{3,2},{4,5},{5,4},{6,7},{7,6},{8,9},{9,8},{10,11... | collective-permute-start | bytes 983048 | tf_op jit(solution)/shard_map/ppermute | solution.py:497
  7.9 15.8 %collective-permute-start = (f32[136,640]{1,0:T(8,128)S(1)}, f32[136,640]{1,0:T(8,128)S(1)}, u32[]{:S(2)}, u32[]{:S(2)}) collective-permute-start(f32[136,640]{1,0:T(8,128)S(1)} %get-tuple-element.23), channel_id=1, source_target_pairs={{0,4},{4,0},{8,12},{12,8},{16,20},{20,16},{24,28},{28,24},{1,5},{5... | collective-permute-start | bytes 1044488 | tf_op jit(solution)/shard_map/ppermute | solution.py:491
  9.2 14.5 %collective-permute-start.1 = (f32[136,640]{1,0:T(8,128)S(1)}, f32[136,640]{1,0:T(8,128)S(1)}, u32[]{:S(2)}, u32[]{:S(2)}) collective-permute-start(f32[136,640]{1,0:T(8,128)S(1)} %get-tuple-element.24), channel_id=1, source_target_pairs={{4,8},{8,4},{12,16},{16,12},{20,24},{24,20},{5,9},{9,5},{13,17},{1... | collective-permute-start | bytes 1044488 | tf_op jit(solution)/shard_map/ppermute | solution.py:492
  9.9 22.4 %copy-start.1 = (f32[2,320,320]{2,1,0:T(8,128)S(1)}, f32[2,320,320]{2,1,0:T(8,128)}, u32[]{:S(2)}) copy-start(f32[2,320,320]{2,1,0:T(8,128)} %obj.7) | copy-start | bytes 2457604
  9.9 22.4 %copy-start.5 = (bf16[8,256,256]{2,1,0:T(8,128)(2,1)S(1)}, bf16[8,256,256]{2,1,0:T(8,128)(2,1)}, u32[]{:S(2)}) copy-start(bf16[8,256,256]{2,1,0:T(8,128)(2,1)} %constant.5.clone.low) | copy-start | bytes 3145732
  9.9 22.4 %copy-start.6 = (bf16[8,256,256]{2,1,0:T(8,128)(2,1)S(1)}, bf16[8,256,256]{2,1,0:T(8,128)(2,1)}, u32[]{:S(2)}) copy-start(bf16[8,256,256]{2,1,0:T(8,128)(2,1)} %constant.4.clone.high) | copy-start | bytes 3145732
  24.5 7.8 %collective-permute-start.4 = (f32[536,128]{1,0:T(8,128)S(1)}, f32[536,128]{1,0:T(8,128)S(1)}, u32[]{:S(2)}, u32[]{:S(2)}) collective-permute-start(f32[536,128]{1,0:T(8,128)S(1)} %get-tuple-element.28), channel_id=1, source_target_pairs={{1,2},{2,1},{5,6},{6,5},{9,10},{10,9},{13,14},{14,13},{17,18},{18,... | collective-permute-start | bytes 823304 | tf_op jit(solution)/shard_map/ppermute | solution.py:513
  27.7 4.6 %collective-permute-start.5 = (f32[536,128]{1,0:T(8,128)S(1)}, f32[536,128]{1,0:T(8,128)S(1)}, u32[]{:S(2)}, u32[]{:S(2)}) collective-permute-start(f32[536,128]{1,0:T(8,128)S(1)} %get-tuple-element.29), channel_id=1, source_target_pairs={{0,1},{1,0},{2,3},{3,2},{4,5},{5,4},{6,7},{7,6},{8,9},{9,8},{10,11... | collective-permute-start | bytes 823304 | tf_op jit(solution)/shard_map/ppermute | solution.py:514
  38.3 7.7 %collective-permute-start.8 = (f32[2,256,128]{2,1,0:T(8,128)S(1)}, f32[2,256,128]{2,1,0:T(8,128)S(1)}, u32[]{:S(2)}, u32[]{:S(2)}) collective-permute-start(f32[2,256,128]{2,1,0:T(8,128)S(1)} %get-tuple-element.37), channel_id=1, source_target_pairs={{1,2},{2,1},{5,6},{6,5},{9,10},{10,9},{13,14},{14,13},{17,18},{18,... | collective-permute-start | bytes 786440 | tf_op jit(solution)/shard_map/ppermute | solution.py:553
  41.5 4.5 %collective-permute-start.9 = (f32[2,256,128]{2,1,0:T(8,128)S(1)}, f32[2,256,128]{2,1,0:T(8,128)S(1)}, u32[]{:S(2)}, u32[]{:S(2)}) collective-permute-start(f32[2,256,128]{2,1,0:T(8,128)S(1)} %get-tuple-element.38), channel_id=1, source_target_pairs={{0,1},{1,0},{2,3},{3,2},{4,5},{5,4},{6,7},{7,6},{8,9},{9,8},{10,11... | collective-permute-start | bytes 786440 | tf_op jit(solution)/shard_map/ppermute | solution.py:554
  41.6 10.6 %collective-permute-start.6 = (f32[2,320,128]{2,1,0:T(8,128)S(1)}, f32[2,320,128]{2,1,0:T(8,128)S(1)}, u32[]{:S(2)}, u32[]{:S(2)}) collective-permute-start(f32[2,320,128]{2,1,0:T(8,128)S(1)} %get-tuple-element.33), channel_id=1, source_target_pairs={{1,2},{2,1},{5,6},{6,5},{9,10},{10,9},{13,14},{14,13},{17,18},{18,... | collective-permute-start | bytes 983048 | tf_op jit(solution)/shard_map/ppermute | solution.py:558
  43.9 8.2 %collective-permute-start.7 = (f32[2,320,128]{2,1,0:T(8,128)S(1)}, f32[2,320,128]{2,1,0:T(8,128)S(1)}, u32[]{:S(2)}, u32[]{:S(2)}) collective-permute-start(f32[2,320,128]{2,1,0:T(8,128)S(1)} %get-tuple-element.34), channel_id=1, source_target_pairs={{0,1},{1,0},{2,3},{3,2},{4,5},{5,4},{6,7},{7,6},{8,9},{9,8},{10,11... | collective-permute-start | bytes 983048 | tf_op jit(solution)/shard_map/ppermute | solution.py:559
  46.1 15.8 %collective-permute-start.10 = (f32[128,640]{1,0:T(8,128)S(1)}, f32[128,640]{1,0:T(8,128)S(1)}, u32[]{:S(2)}, u32[]{:S(2)}) collective-permute-start(f32[128,640]{1,0:T(8,128)S(1)} %get-tuple-element.39), channel_id=1, source_target_pairs={{0,4},{4,0},{8,12},{12,8},{16,20},{20,16},{24,28},{28,24},{1,5},{5... | collective-permute-start | bytes 983048 | tf_op jit(solution)/shard_map/ppermute | solution.py:556
  48.4 13.6 %collective-permute-start.11 = (f32[128,640]{1,0:T(8,128)S(1)}, f32[128,640]{1,0:T(8,128)S(1)}, u32[]{:S(2)}, u32[]{:S(2)}) collective-permute-start(f32[128,640]{1,0:T(8,128)S(1)} %get-tuple-element.40), channel_id=1, source_target_pairs={{4,8},{8,4},{12,16},{16,12},{20,24},{24,20},{5,9},{9,5},{13,17},{1... | collective-permute-start | bytes 983048 | tf_op jit(solution)/shard_map/ppermute | solution.py:557

commit v4 on v3

v4 whole, which is shorter than its diff:
```python
import functools
import math

import jax
import jax.numpy as jnp
import ml_dtypes
import numpy as np
from jax import lax
from jax.experimental import pallas as pl
from jax.experimental.pallas import tpu as pltpu
from jax.sharding import PartitionSpec as P

OVL = 128
HALF = 64
LANES = 128

EPSILON = 0.01
PHOTON_SCALE = 0.01
STEP_SIZE = 0.5
REGULAR = 1.0

F32 = jnp.float32
BF16 = jnp.bfloat16


def call(kernel, out_shapes, args, smem=(), hbm_out=False, dtype=F32, scratch=(), flops=0, limit=16):
    specs = [
        pl.BlockSpec(memory_space=pltpu.SMEM if i in smem else pltpu.VMEM) for i in range(len(args))
    ]
    args = [
        x if i in smem else pltpu.with_memory_space_constraint(x, pltpu.VMEM)
        for i, x in enumerate(args)
    ]
    return pl.pallas_call(
        kernel,
        out_shape=[
            jax.ShapeDtypeStruct(s, F32) if hbm_out else pltpu.VMEM(s, dtype) for s in out_shapes
        ],
        in_specs=specs,
        out_specs=[pl.BlockSpec(memory_space=pltpu.VMEM) for _ in out_shapes],
        scratch_shapes=list(scratch),
        compiler_params=pltpu.CompilerParams(vmem_limit_bytes=limit * 1024 * 1024),
        cost_estimate=pl.CostEstimate(flops=flops, bytes_accessed=0, transcendentals=0)
        if flops
        else None,
    )(*args)


@functools.lru_cache(maxsize=None)
def tables(length):
    quarter = length // 4
    n = np.arange(quarter)[:, None]
    k = np.arange(quarter)[None, :]
    blocks = []
    for p in range(4):
        angle = 2.0 * np.pi * ((n * (4 * k + p)) % length) / length
        c = np.cos(angle) / math.sqrt(length)
        s = np.sin(angle) / math.sqrt(length)
        blocks.append(np.block([[c, -s], [s, c]]))
    blocks += [b.T for b in blocks]
    full = np.stack(blocks)
    high = full.astype(np.float32).astype(ml_dtypes.bfloat16)
    low = (full - high.astype(np.float64)).astype(np.float32).astype(ml_dtypes.bfloat16)
    return high, low


def split(x):
    high = x.astype(BF16)
    return high, (x - high.astype(F32)).astype(BF16)


def dot(a, b):
    return lax.dot_general(a, b, (((1,), (0,)), ((), ())), preferred_element_type=F32)


def mix_forward(x):
    (x0r, x0i), (x1r, x1i), (x2r, x2i), (x3r, x3i) = x
    ar, ai, br, bi = x0r + x2r, x0i + x2i, x0r - x2r, x0i - x2i
    cr, ci, dr, di = x1r + x3r, x1i + x3i, x1r - x3r, x1i - x3i
    return [(ar + cr, ai + ci), (br + di, bi - dr), (ar - cr, ai - ci), (br - di, bi + dr)]


def mix_inverse(x):
    (x0r, x0i), (x1r, x1i), (x2r, x2i), (x3r, x3i) = x
    ar, ai, br, bi = x0r + x2r, x0i + x2i, x0r - x2r, x0i - x2i
    cr, ci, dr, di = x1r + x3r, x1i + x3i, x1r - x3r, x1i - x3i
    return [(ar + cr, ai + ci), (br - di, bi + dr), (ar - cr, ai - ci), (br + di, bi - dr)]


def lane_iota(shape):
    return lax.broadcasted_iota(jnp.int32, shape, len(shape) - 1)


def row_iota(shape):
    return lax.broadcasted_iota(jnp.int32, shape, len(shape) - 2)


def turn(x):
    return pltpu.roll(x, HALF, len(x.shape) - 1)


def odd(axis):
    return lax.axis_index(axis) % 2 == 1


def row_kernel(offs, obj, inner, cross, held, numbers, sems):
    rows, cols = obj.shape[1:]
    far = odd("row")
    bases = jnp.where(far, 0, rows - OVL), jnp.where(far, rows - OVL, 0)
    copies = [pltpu.make_async_copy(offs, numbers, sems.at[2])]
    for t, base in enumerate(bases):
        part = obj.at[:, pl.ds(pl.multiple_of(base, 8), OVL), :]
        copies.append(pltpu.make_async_copy(part, held.at[t], sems.at[t]))
    for copy in (copies[1], copies[0], copies[2]):
        copy.start()
    copies[0].wait()
    lane = lane_iota((8, LANES))
    first, second = numbers[0, 0, 0, 0], numbers[0, 0, 0, 1]
    info = jnp.where(lane == 0, first, jnp.where(lane == 1, second, 1)).astype(F32)
    for t, out in enumerate((inner, cross)):
        out[5 * OVL : 5 * OVL + 8, :] = info
        copies[1 + t].wait()
        for c in range(2):
            for k in range(2):
                at = (2 * c + k) * OVL
                out[at : at + OVL, :] = held[t, c, :, 128 * k : 128 * k + 128]
            out[4 * OVL : 5 * OVL, c * HALF : c * HALF + HALF] = held[t, c, :, 256:cols]


def side_kernel(obj, xside, dside):
    cols = obj.shape[2]
    right = odd("col")
    for c in range(2):
        west = turn(obj[c, :, 0:128])
        east = obj[c, :, cols - OVL : cols]
        xside[c] = jnp.where(right, east, west)
        dside[c] = jnp.where(right, west, east)


def corner_kernel(offs, inner, cross, xside, dside):
    right = odd("col")
    lane = lane_iota((OVL, LANES))
    for part, halo in enumerate((inner, cross)):
        for c in range(2):
            west = turn(halo[2 * c * OVL : 2 * c * OVL + OVL, :])
            tail = halo[4 * OVL : 5 * OVL, :]
            middle = turn(halo[(2 * c + 1) * OVL : (2 * c + 2) * OVL, :])
            east = jnp.where(lane < HALF, middle, turn(tail) if c == 0 else tail)
            rows = slice((2 * part + c) * OVL, (2 * part + c) * OVL + OVL)
            xside[rows, :] = jnp.where(right, east, west)
            dside[rows, :] = jnp.where(right, west, east)
    lane = lane_iota((8, LANES))
    info = jnp.where(lane == 0, offs[0], jnp.where(lane == 1, offs[1], 1)).astype(F32)
    for out in (xside, dside):
        out[4 * OVL : 4 * OVL + 8, :] = inner[5 * OVL : 5 * OVL + 8, :]
        out[4 * OVL + 8 : 4 * OVL + 16, :] = cross[5 * OVL : 5 * OVL + 8, :]
        out[4 * OVL + 16 : 4 * OVL + 24, :] = info


def ready_kernel(offs, probe, counts, rolled, measured, wide):
    size = probe.shape[-1]
    quarter = size // 4
    u = offs[0]
    v = offs[1]
    for c in range(2):
        for t in range(4):
            cols = slice(t * quarter, (t + 1) * quarter)
            wide[c, t, 0:HALF, :] = probe[c, size - HALF : size, cols]
            wide[c, t, HALF : HALF + size, :] = probe[c, :, cols]
        for base in range(0, size, HALF):
            rows = pl.ds(HALF - u + base, HALF)
            piece = jnp.concatenate([wide[c, t, rows, :] for t in range(4)], axis=1)
            rolled[c, base : base + HALF, :] = pltpu.roll(piece, v, 1)
    r = row_iota((size, size))
    k = lane_iota((size, size))
    order = jnp.where(r == 4 * (k % quarter) + k // quarter, 1.0, 0.0).astype(BF16)
    for t in range(4):
        wide[0, t, 0:size, :] = counts[:, t * quarter : (t + 1) * quarter].astype(F32)
    for p in range(4):
        rows = jnp.concatenate([wide[0, t, pl.ds(p, quarter, stride=4), :] for t in range(4)], axis=1)
        high = jnp.floor(rows * (1.0 / 256.0))
        low = rows - 256.0 * high
        moved = 256.0 * dot(high.astype(BF16), order) + dot(low.astype(BF16), order)
        measured[p * quarter : (p + 1) * quarter, :] = jnp.sqrt(moved * PHOTON_SCALE)


def keep(hi, lo, at, x):
    hi[at], lo[at] = split(x)


STEP = 32


def enter(tiles, rolled, rows, hi, lo, at):
    quarter = rolled.shape[-1] // 4
    exits = []
    for q in range(4):
        cols = slice(q * quarter, (q + 1) * quarter)
        ar, ai = rolled[0, rows, cols], rolled[1, rows, cols]
        exits.append((ar * tiles[0][q] - ai * tiles[1][q], ar * tiles[1][q] + ai * tiles[0][q]))
    for p, (yr, yi) in enumerate(mix_forward(exits)):
        keep(hi, lo, (p, at, slice(0, quarter)), yr)
        keep(hi, lo, (p, at, slice(quarter, 2 * quarter)), yi)


def leave(z, at, rolled, rows, v, right):
    quarter = rolled.shape[-1] // 4
    quads = [(z[p, at, 0:quarter], z[p, at, quarter : 2 * quarter]) for p in range(4)]
    grads = ([], [])
    for q, (br, bi) in enumerate(mix_inverse(quads)):
        cols = slice(q * quarter, (q + 1) * quarter)
        ar, ai = rolled[0, rows, cols], rolled[1, rows, cols]
        grads[0].append(ar * br + ai * bi)
        grads[1].append(ar * bi - ai * br)
    lane = lane_iota((STEP, LANES))
    for g in grads:
        wout = turn(jnp.where(lane >= v, g[0], 0.0))
        eout = turn(jnp.where(lane < HALF, jnp.where(lane < v, g[0], 0.0), g[3]))
        yield g[1:], jnp.where(right, eout, wout), jnp.where(right, wout, eout)


def right_product(hi, lo, rows, p, high, low, k):
    a = hi[p, rows, :]
    return dot(a, high[k]) + dot(lo[p, rows, :], high[k]) + dot(a, low[k])


def left_product(hi, lo, at, high, low, k):
    a = hi[at]
    return dot(high[k], a) + dot(high[k], lo[at]) + dot(low[k], a)


def fore_kernel(offs, obj, xside, dside, rolled, high, low, z, hi, lo):
    cells = obj.shape[1]
    v = offs[1]
    right = odd("col")
    lane = lane_iota((STEP, LANES))
    for top in range(0, cells, cells // 2):
        for base in range(top, top + cells // 2, STEP):
            rows = slice(base, base + STEP)
            tiles = []
            for c in range(2):
                last = obj[c, rows, 256:cells]
                last = jnp.concatenate([last, last], axis=1)
                x, d = xside[c, rows, :], dside[c, rows, :]
                w, e = jnp.where(right, d, x), jnp.where(right, x, d)
                tiles.append(
                    [
                        jnp.where(lane < v, e, w),
                        obj[c, rows, 0:128],
                        obj[c, rows, 128:256],
                        jnp.where(lane < HALF, last, e),
                    ]
                )
            enter(tiles, rolled, slice(base + OVL, base + OVL + STEP), hi, lo, rows)
        rows = slice(top, top + cells // 2)
        for p in range(4):
            z[p, rows, :] = right_product(hi, lo, rows, p, high, low, p)


def main_kernel(
    offs, inner, cross, xcorner, dcorner, rolled, measured, zown, high, low,
    own_hi, own_lo, nblock, sblock, xcorn, dcorn, ah, al, bh, bl, zh, tf,
):
    size = rolled.shape[-1]
    quarter = size // 4
    cells = zown.shape[1]
    u = offs[0]
    v = offs[1]
    right = odd("col")
    far = odd("row")
    lane = lane_iota((STEP, LANES))

    def pieces(c, part, base):
        def take(first, second, at, again):
            a, b = first[at : at + STEP, :], second[again : again + STEP, :]
            return jnp.where(far, a, b) if part == 0 else jnp.where(far, b, a)

        tiles = [take(inner, cross, t * OVL + base, t * OVL + base) for t in (2 * c, 2 * c + 1, 4)]
        last = turn(tiles[2]) if c == 1 else tiles[2]
        x = take(xcorner, xcorner, c * OVL + base, (2 + c) * OVL + base)
        d = take(dcorner, dcorner, c * OVL + base, (2 + c) * OVL + base)
        w, e = jnp.where(right, d, x), jnp.where(right, x, d)
        return [jnp.where(lane < v, e, w), tiles[0], tiles[1], jnp.where(lane < HALF, last, e)]

    def patch(c, slot):
        if slot >= OVL:
            return pieces(c, 1, slot - OVL - cells)
        above = pieces(c, 0, slot)
        if slot >= HALF:
            return above
        row = row_iota((STEP, LANES)) + slot
        return [jnp.where(row < u, y, x) for x, y in zip(above, pieces(c, 1, slot + HALF))]

    block = 2 * quarter
    re, im = slice(0, quarter), slice(quarter, 2 * quarter)
    count = size - cells
    slots = [b if b < OVL else b + cells for b in range(0, count, STEP)]

    for base, slot in zip(range(0, count, STEP), slots):
        rows = slice(slot, slot + STEP)
        enter([patch(c, slot) for c in range(2)], rolled, rows, ah, al, slice(base, base + STEP))
    for p in range(4):
        zh[p] = right_product(ah, al, slice(0, count), p, high, low, p)

    def place(slot, halo, own):
        if slot < OVL:
            return halo, slice(slot, slot + STEP)
        if slot < OVL + cells:
            return own, slice(slot - OVL, slot - OVL + STEP)
        return halo, slice(slot - cells, slot - cells + STEP)

    for half in range(2):
        pair = (2 * half, 2 * half + 1)
        for t, p in enumerate(pair):
            cols = slice(t * quarter, (t + 1) * quarter)
            for r in range(0, quarter, STEP):
                quads = []
                for q in range(4):
                    z, rows = place(q * quarter + r, zh, zown)
                    quads.append((z[p, rows, re], z[p, rows, im]))
                for k, (yr, yi) in enumerate(mix_forward(quads)):
                    keep(bh, bl, (half, k, slice(r, r + STEP), cols), yr)
                    keep(bh, bl, (half, k, slice(quarter + r, quarter + r + STEP), cols), yi)
        for k in range(4):
            z = left_product(bh, bl, (half, k), high, low, 4 + k)
            zr, zi = z[re], z[im]
            m = measured[k * quarter : (k + 1) * quarter, half * block : (half + 1) * block]
            factor = 1.0 - m * lax.rsqrt(zr * zr + zi * zi + EPSILON)
            keep(bh, bl, (half, k, re), factor * zr)
            keep(bh, bl, (half, k, im), factor * zi)
        for k in range(4):
            tf[half, k] = left_product(bh, bl, (half, k), high, low, k)
        for t, p in enumerate(pair):
            cols = slice(t * quarter, (t + 1) * quarter)
            for r in range(0, quarter, STEP):
                again = slice(quarter + r, quarter + r + STEP)
                quads = [(tf[half, k, r : r + STEP, cols], tf[half, k, again, cols]) for k in range(4)]
                for q, (yr, yi) in enumerate(mix_inverse(quads)):
                    hi, rows = place(q * quarter + r, ah, own_hi)
                    lo, rows = place(q * quarter + r, al, own_lo)
                    keep(hi, lo, (p, rows, re), yr)
                    keep(hi, lo, (p, rows, im), yi)

    for p in range(4):
        zh[p] = right_product(ah, al, slice(0, count), p, high, low, 4 + p)
    for base, slot in zip(range(0, count, STEP), slots):
        at, rows = slice(base, base + STEP), slice(slot, slot + STEP)
        row = row_iota((STEP, LANES)) + slot
        sends = []
        if slot < OVL:
            sends.append((0, slot, row >= u if slot < HALF else None))
        if slot < HALF:
            sends.append((1, slot + HALF, row < u))
        if slot >= OVL:
            sends.append((1, slot - OVL - cells, None))
        for c, (g, xout, dout) in enumerate(leave(zh, at, rolled, rows, v, right)):
            for part, o, mask in sends:
                to = slice(o, o + STEP)
                put = (lambda x: x) if mask is None else (lambda x: jnp.where(mask, x, 0.0))
                block = (nblock, sblock)[part]
                for t in range(3):
                    block[c, to, 128 * t : 128 * t + 128] = put(g[t])
                xcorn[part, c, to, :] = put(xout)
                dcorn[part, c, to, :] = put(dout)


def after_kernel(offs, hi, lo, rolled, high, low, own, xedge, dedge, z):
    cells = own.shape[1]
    v = offs[1]
    right = odd("col")
    for top in range(0, cells, cells // 2):
        rows = slice(top, top + cells // 2)
        for p in range(4):
            z[p, rows, :] = right_product(hi, lo, rows, p, high, low, 4 + p)
        for base in range(top, top + cells // 2, STEP):
            at, rows = slice(base, base + STEP), slice(base + OVL, base + OVL + STEP)
            for c, (g, xout, dout) in enumerate(leave(z, at, rolled, rows, v, right)):
                own[c, at, 0:128] = g[0]
                own[c, at, 128:256] = g[1]
                own[c, at, 256:cells] = g[2][:, : cells - 256]
                xedge[c, at, :] = xout
                dedge[c, at, :] = dout


def send_kernel(nblock, sblock, xcorn, dcorn, inner, cross):
    right = odd("col")
    far = odd("row")
    first = lane_iota((OVL, LANES)) < HALF
    tiles = []
    for part, block in enumerate((nblock, sblock)):
        last, out = [], []
        for c in range(2):
            x, d = xcorn[part, c], dcorn[part, c]
            fw, fe = jnp.where(right, d, x), jnp.where(right, x, d)
            out.append(block[c, :, 0:128] + fw)
            out.append(block[c, :, 128:256] + jnp.where(first, 0.0, fe))
            last.append(block[c, :, 256:384] + fe)
        out.append(jnp.where(first, last[0], turn(last[1])))
        tiles.append(out)
    for t, (n, s) in enumerate(zip(*tiles)):
        inner[t * OVL : t * OVL + OVL, :] = jnp.where(far, n, s)
        cross[t * OVL : t * OVL + OVL, :] = jnp.where(far, s, n)


def light_kernel(
    offs, xcorner, dcorner, inner, cross, probe, weight, pad, acc
):
    size = probe.shape[-1]
    cells = weight.shape[0]
    far = odd("row")
    pad[...] = jnp.zeros(pad.shape, F32)
    for t in range(4):
        cols = slice(t * LANES, (t + 1) * LANES)
        x = probe[0, :, cols]
        y = probe[1, :, cols]
        pad[1 + t, OVL : OVL + size, :] = x * x + y * y
    acc[...] = jnp.zeros(acc.shape, F32)
    first = lane_iota((HALF, LANES)) < HALF
    right = odd("col")
    unit = row_iota((8, LANES)) == 0
    lane = lane_iota((8, LANES))
    for di in (0, -1, 1):
        for dj in (0, -1, 1):
            if di == 0 and dj == 0:
                u, v, there = offs[0], offs[1], 1.0
            else:

                def take(first, second, at, again):
                    a, b = first[at : at + 8, :], second[again : again + 8, :]
                    return jnp.where(far, a, b) if di < 0 else jnp.where(far, b, a)

                if dj == 0:
                    tile = take(inner, cross, 5 * OVL, 5 * OVL)
                else:
                    if di == 0:
                        x, d = [ref[4 * OVL + 16 : 4 * OVL + 24, :] for ref in (xcorner, dcorner)]
                    else:
                        x, d = [take(ref, ref, 4 * OVL, 4 * OVL + 8) for ref in (xcorner, dcorner)]
                    tile = jnp.where(right, d, x) if dj < 0 else jnp.where(right, x, d)
                u, v, there = [jnp.sum(jnp.where(unit & (lane == i), tile, 0.0)) for i in range(3)]
                u, v = u.astype(jnp.int32), v.astype(jnp.int32)
            start, count, put = {
                0: (2 * OVL - u, cells, 0),
                1: (OVL - u, OVL, cells - OVL),
                -1: (size + HALF - u, OVL, 0),
            }[di]
            seen = there
            for r in range(0, count, HALF):
                rows = pl.ds(start + r, HALF)
                to = slice(put + r, put + r + HALF)
                lo, hi, shift = {0: (1, 5, 384 + v), -1: (4, 6, lax.rem(192 + v, 256)), 1: (0, 2, 128 + v)}[dj]
                x = pltpu.roll(jnp.concatenate([pad[t, rows, :] for t in range(lo, hi)], axis=1), shift, 1)
                if dj == 0:
                    x = x[:, 0:384]
                    acc[to, :] += x * seen
                    continue
                if dj == -1:
                    x = x[:, 0:128]
                    acc[to, 0:128] += x * seen
                    continue
                x = turn(x[:, 0:128]) * seen
                acc[to, 128:256] += jnp.where(first, 0.0, x)
                acc[to, 256:384] += x
    for r in range(0, cells, HALF):
        rows = slice(r, r + HALF)
        weight[rows, :] = STEP_SIZE / (acc[rows, 0:cells] + REGULAR)


def final_kernel(obj, own, weight, xedge, dedge, inner, cross, updated):
    cells = obj.shape[1]
    right = odd("col")
    far = odd("row")
    first = lane_iota((HALF, LANES)) < HALF
    for r in range(0, cells, HALF):
        rows = slice(r, r + HALF)
        for c in range(2):
            x, d = xedge[c, rows, :], dedge[c, rows, :]
            fw, fe = jnp.where(right, d, x), jnp.where(right, x, d)
            g = [
                own[c, rows, 0:128] + fw,
                own[c, rows, 128:256] + jnp.where(first, 0.0, fe),
                own[c, rows, 256:cells] + fe[:, : cells - 256],
            ]
            adds = []
            if r < OVL:
                adds.append((0, r))
            if r >= cells - OVL:
                adds.append((1, r - cells + OVL))
            for part, o in adds:

                def take(tile, cols=slice(0, LANES)):
                    src = slice(tile * OVL + o, tile * OVL + o + HALF)
                    a, b = inner[src, cols], cross[src, cols]
                    return jnp.where(far, a, b) if part == 0 else jnp.where(far, b, a)

                g[0] = g[0] + take(2 * c)
                g[1] = g[1] + take(2 * c + 1)
                g[2] = g[2] + take(4, slice(c * HALF, c * HALF + HALF))
            for t, x in enumerate(g):
                cols = slice(128 * t, min(128 * t + 128, cells))
                updated[c, rows, cols] = obj[c, rows, cols] - x * weight[rows, cols]


def swaps(axis):
    count = lax.axis_size(axis)
    return [
        [pair for i in range(first, count - 1, 2) for pair in ((i, i + 1), (i + 1, i))]
        for first in (1, 0)
    ]


def local(object_slab, probe_field, offsets, counts):
    cells = object_slab.shape[1]
    size = probe_field.shape[-1]
    row_cross, row_inner = swaps("row")
    col_cross, col_inner = swaps("col")
    offs = offsets.reshape(2)
    table_high, table_low = tables(size)
    high, low = jnp.asarray(table_high), jnp.asarray(table_low)

    to_inner, to_cross = pl.pallas_call(
        row_kernel,
        name="rows",
        out_shape=[pltpu.VMEM((5 * OVL + 8, LANES), F32) for _ in range(2)],
        in_specs=[pl.BlockSpec(memory_space=pltpu.HBM) for _ in range(2)],
        out_specs=[pl.BlockSpec(memory_space=pltpu.VMEM) for _ in range(2)],
        scratch_shapes=[
            pltpu.VMEM((2, 2, OVL, cells), F32),
            pltpu.SMEM((1, 1, 1, 2), jnp.int32),
            pltpu.SemaphoreType.DMA((3,)),
        ],
        compiler_params=pltpu.CompilerParams(vmem_limit_bytes=8 * 1024 * 1024),
    )(*[pltpu.with_memory_space_constraint(x, pltpu.HBM) for x in (offsets, object_slab)])
    halo_inner = lax.ppermute(to_inner, "row", row_inner)
    halo_cross = lax.ppermute(to_cross, "row", row_cross)
    xside, dside = call(
        side_kernel, [(2, cells, OVL), (2, cells, OVL)], [object_slab], flops=5_000_000_000
    )
    side_x = lax.ppermute(xside, "col", col_cross)
    side_d = lax.ppermute(dside, "col", col_inner)

    rolled, measured = call(
        ready_kernel,
        [(2, size, size), (size, size)],
        [offs, probe_field, counts.reshape(size, size)],
        smem=(0,),
        scratch=[pltpu.VMEM((2, 4, size + HALF, LANES), F32)],
        flops=5_000_000_000,
    )
    half, count = size // 2, size - cells
    (zown,) = call(
        fore_kernel,
        [(4, cells, half)],
        [offs, object_slab, side_x, side_d, rolled, high, low],
        smem=(0,),
        scratch=[pltpu.VMEM((4, cells, half), BF16) for _ in range(2)],
        flops=2_000_000_000,
    )
    xcorner, dcorner = call(
        corner_kernel, [(4 * OVL + 24, OVL)] * 2, [offs, halo_inner, halo_cross], smem=(0,)
    )
    corner_x = lax.ppermute(xcorner, "col", col_cross)
    corner_d = lax.ppermute(dcorner, "col", col_inner)
    shapes = [
        ((4, cells, half), BF16),
        ((4, cells, half), BF16),
        ((2, OVL, 384), F32),
        ((2, OVL, 384), F32),
        ((2, 2, OVL, OVL), F32),
        ((2, 2, OVL, OVL), F32),
    ]
    operands = [halo_inner, halo_cross, corner_x, corner_d, rolled, measured, zown, high, low]
    own_hi, own_lo, nblock, sblock, xcorn, dcorn = pl.pallas_call(
        main_kernel,
        name="main",
        out_shape=[pltpu.VMEM(s, d) for s, d in shapes],
        in_specs=[pl.BlockSpec(memory_space=pltpu.SMEM)]
        + [pl.BlockSpec(memory_space=pltpu.VMEM) for _ in operands],
        out_specs=[pl.BlockSpec(memory_space=pltpu.VMEM) for _ in shapes],
        scratch_shapes=[
            pltpu.VMEM((4, count, half), BF16),
            pltpu.VMEM((4, count, half), BF16),
            pltpu.VMEM((2, 4, half, half), BF16),
            pltpu.VMEM((2, 4, half, half), BF16),
            pltpu.VMEM((4, count, half), F32),
            pltpu.VMEM((2, 4, half, half), F32),
        ],
        compiler_params=pltpu.CompilerParams(vmem_limit_bytes=20 * 1024 * 1024),
        cost_estimate=pl.CostEstimate(flops=5_000_000_000, bytes_accessed=0, transcendentals=0),
    )(offs, *[pltpu.with_memory_space_constraint(x, pltpu.VMEM) for x in operands])
    fix_x = lax.ppermute(xcorn, "col", col_cross)
    fix_d = lax.ppermute(dcorn, "col", col_inner)
    own, xedge, dedge = call(
        after_kernel,
        [(2, cells, cells), (2, cells, OVL), (2, cells, OVL)],
        [offs, own_hi, own_lo, rolled, high, low],
        smem=(0,),
        scratch=[pltpu.VMEM((4, cells, half), F32)],
        flops=2_000_000_000,
    )
    to_inner, to_cross = call(send_kernel, [(5 * OVL, LANES)] * 2, [nblock, sblock, fix_x, fix_d])
    grad_inner = lax.ppermute(to_inner, "row", row_inner)
    grad_cross = lax.ppermute(to_cross, "row", row_cross)
    edge_x = lax.ppermute(xedge, "col", col_cross)
    edge_d = lax.ppermute(dedge, "col", col_inner)
    (weight,) = call(
        light_kernel,
        [(cells, cells)],
        [offs, corner_x, corner_d, halo_inner, halo_cross, probe_field],
        smem=(0,),
        scratch=[pltpu.VMEM((6, size + 2 * OVL, LANES), F32), pltpu.VMEM((cells, 384), F32)],
        flops=10_000_000_000,
    )
    (updated,) = call(
        final_kernel,
        [(2, cells, cells)],
        [object_slab, own, weight, edge_x, edge_d, grad_inner, grad_cross],
        hbm_out=True,
    )
    return updated


def solution(mesh):
    return jax.shard_map(
        local,
        mesh=mesh,
        in_specs=(
            P(None, "row", "col"),
            P(),
            P("row", "col", None, None),
            P("row", "col", None, None, None),
        ),
        out_specs=P(None, "row", "col"),
        check_vma=False,
    )
```

time: 63.4 us -> 57.6 us (0.909)
  the two profiles are of different devices: /device:TPU:1 before, /device:TPU:0 now
where the time goes in v4:
time: 57.6 us; the launch traced here: 57.4 us
  starting transfers between devices  20 us (35%)
  waiting for transfers between devices  18.7 us (32%)
  Pallas kernels  17.2 us (30%)
  local copies, waits for them, and re-layouts  1.22 us (2%)
    pallas_call x8, Pallas kernels, call(): pl.pallas_call(kernel, out_shape=[jax.ShapeDtypeStruct(s, F32) if hbm_out...  11.5 us
    ppermute x1, waiting for transfers between devices, local(): grad_inner = lax.ppermute(to_inner, 'row', row_inner)  10.8 us
    ppermute x1, waiting for transfers between devices, local(): halo_inner = lax.ppermute(to_inner, 'row', row_inner)  7.88 us
    pallas_call x1, Pallas kernels, local(): pl.pallas_call(main_kernel, name='main', out_shape=[pltpu.VMEM(s, d) for...  4.5 us
    ppermute x1, starting transfers between devices, local(): halo_inner = lax.ppermute(to_inner, 'row', row_inner)  3.06 us
    ppermute x1, starting transfers between devices, local(): fix_d = lax.ppermute(dcorn, 'col', col_inner)  2.93 us
    ppermute x1, starting transfers between devices, local(): corner_d = lax.ppermute(dcorner, 'col', col_inner)  2.9 us
    ppermute x1, starting transfers between devices, local(): side_d = lax.ppermute(dside, 'col', col_inner)  2.9 us
  transfers between devices with their start and end apart: 12, of which 2 were waited for; matrix products, arithmetic and copies ran while one was open for 0% of the time, Pallas kernels for 18%

profile of v4, /device:TPU:0, one launch (start us, length us, event | category | flops | bytes accessed | tf_op | source)
XLA Modules:
  0.0 57.4 jit_solution(8004717833487449506)
XLA Ops:
  0.0 1.2 %rows.1 = (f32[648,128]{1,0:T(8,128)S(1)}, f32[648,128]{1,0:T(8,128)S(1)}) custom-call(s32[1,1,1,2]{3,2,1,0:T(1,128)} %offs.1, f32[2,320,320]{2,1,0:T(8,128)} %obj.7), custom_call_target="tpu_custom_call" | custom-call | tf_op jit(solution)/shard_map/rows/pallas_call | solution.py:521
  1.2 3.1 %collective-permute-start = (f32[648,128]{1,0:T(8,128)S(1)}, f32[648,128]{1,0:T(8,128)S(1)}, u32[]{:S(2)}, u32[]{:S(2)}) collective-permute-start(f32[648,128]{1,0:T(8,128)S(1)} %get-tuple-element.24), channel_id=1, source_target_pairs={{0,4},{4,0},{8,12},{12,8},{16,20},{20,16},{24,28},{28,24},{1,5},{5... | collective-permute-start | bytes 995336 | tf_op jit(solution)/shard_map/ppermute | solution.py:534
  4.3 0.7 %collective-permute-start.1 = (f32[648,128]{1,0:T(8,128)S(1)}, f32[648,128]{1,0:T(8,128)S(1)}, u32[]{:S(2)}, u32[]{:S(2)}) collective-permute-start(f32[648,128]{1,0:T(8,128)S(1)} %get-tuple-element.25), channel_id=1, source_target_pairs={{4,8},{8,4},{12,16},{16,12},{20,24},{24,20},{5,9},{9,5},{13,17},{1... | collective-permute-start | bytes 995336 | tf_op jit(solution)/shard_map/ppermute | solution.py:535
  5.0 0.0 copy-start
  5.0 1.2 %copy-done = f32[2,320,320]{2,1,0:T(8,128)S(1)} copy-done((f32[2,320,320]{2,1,0:T(8,128)S(1)}, f32[2,320,320]{2,1,0:T(8,128)}, u32[]{:S(2)}) %copy-start) | copy-done | bytes 819224
  6.2 0.0 copy-start.2
  6.2 0.0 copy-start.3
  6.2 0.0 copy-start.4
  6.2 0.7 %shard_map.66 = (f32[2,320,128]{2,1,0:T(8,128)S(1)}, f32[2,320,128]{2,1,0:T(8,128)S(1)}) custom-call(f32[2,320,320]{2,1,0:T(8,128)S(1)} %copy-done), custom_call_target="tpu_custom_call" | custom-call | flops 5000000000 | tf_op jit(solution)/shard_map/pallas_call | solution.py:34
  6.9 0.8 %collective-permute-start.4 = (f32[2,320,128]{2,1,0:T(8,128)S(1)}, f32[2,320,128]{2,1,0:T(8,128)S(1)}, u32[]{:S(2)}, u32[]{:S(2)}) collective-permute-start(f32[2,320,128]{2,1,0:T(8,128)S(1)} %get-tuple-element.30), channel_id=1, source_target_pairs={{1,2},{2,1},{5,6},{6,5},{9,10},{10,9},{13,14},{14,13},{17,18},{18,... | collective-permute-start | bytes 983048 | tf_op jit(solution)/shard_map/ppermute | solution.py:539
  7.7 2.9 %collective-permute-start.5 = (f32[2,320,128]{2,1,0:T(8,128)S(1)}, f32[2,320,128]{2,1,0:T(8,128)S(1)}, u32[]{:S(2)}, u32[]{:S(2)}) collective-permute-start(f32[2,320,128]{2,1,0:T(8,128)S(1)} %get-tuple-element.31), channel_id=1, source_target_pairs={{0,1},{1,0},{2,3},{3,2},{4,5},{5,4},{6,7},{7,6},{8,9},{9,8},{10,11... | collective-permute-start | bytes 983048 | tf_op jit(solution)/shard_map/ppermute | solution.py:540
  10.6 7.9 %collective-permute-done.inner = f32[648,128]{1,0:T(8,128)S(1)} collective-permute-done((f32[648,128]{1,0:T(8,128)S(1)}, f32[648,128]{1,0:T(8,128)S(1)}, u32[]{:S(2)}, u32[]{:S(2)}) %collective-permute-start) | collective-permute-done | bytes 331808 | tf_op jit(solution)/shard_map/ppermute | solution.py:534
  18.5 0.0 collective-permute-done.1.cross
  18.5 0.0 copy-done.2
  18.5 0.8 %shard_map.64 = (f32[536,128]{1,0:T(8,128)S(1)}, f32[536,128]{1,0:T(8,128)S(1)}) custom-call(s32[2]{0:T(128)S(1)} %bitcast.2, f32[648,128]{1,0:T(8,128)S(1)} %collective-permute-done.inner, f32[648,128]{1,0:T(8,128)S(1)} %collective-permute-done.1.cross), custom_call_target="tpu_custom_call" | custom-call | tf_op jit(solution)/shard_map/pallas_call | solution.py:34
  19.3 0.7 %collective-permute-start.2 = (f32[536,128]{1,0:T(8,128)S(1)}, f32[536,128]{1,0:T(8,128)S(1)}, u32[]{:S(2)}, u32[]{:S(2)}) collective-permute-start(f32[536,128]{1,0:T(8,128)S(1)} %get-tuple-element.26), channel_id=1, source_target_pairs={{1,2},{2,1},{5,6},{6,5},{9,10},{10,9},{13,14},{14,13},{17,18},{18,... | collective-permute-start | bytes 823304 | tf_op jit(solution)/shard_map/ppermute | solution.py:562
  19.9 2.9 %collective-permute-start.3 = (f32[536,128]{1,0:T(8,128)S(1)}, f32[536,128]{1,0:T(8,128)S(1)}, u32[]{:S(2)}, u32[]{:S(2)}) collective-permute-start(f32[536,128]{1,0:T(8,128)S(1)} %get-tuple-element.27), channel_id=1, source_target_pairs={{0,1},{1,0},{2,3},{3,2},{4,5},{5,4},{6,7},{7,6},{8,9},{9,8},{10,11... | collective-permute-start | bytes 823304 | tf_op jit(solution)/shard_map/ppermute | solution.py:563
  22.8 0.0 copy-done.3
  22.9 0.0 copy-done.4
  22.9 0.0 copy-start.1
  22.9 0.0 copy-start.5
  22.9 0.0 copy-start.6
  22.9 2.4 %shard_map.65 = (f32[2,512,512]{2,1,0:T(8,128)S(1)}, f32[512,512]{1,0:T(8,128)S(1)}) custom-call(s32[2]{0:T(128)S(1)} %bitcast.3, f32[2,512,512]{2,1,0:T(8,128)S(1)} %copy-done.3, s32[512,512]{1,0:T(8,128)S(1)} %bitcast.8), custom_call_target="tpu_custom_call" | custom-call | flops 5000000000 | tf_op jit(solution)/shard_map/pallas_call | solution.py:34
  25.3 0.0 collective-permute-done.4.xside
  25.3 0.0 collective-permute-done.5.dside
  25.3 0.0 copy-done.1
  25.3 0.0 copy-done.5
  25.3 0.0 copy-done.6
  25.3 1.7 %shard_map.67.zown = f32[4,320,256]{2,1,0:T(8,128)S(1)} custom-call(s32[2]{0:T(128)S(1)} %bitcast.4, f32[2,320,320]{2,1,0:T(8,128)S(1)} %copy-done.1, f32[2,320,128]{2,1,0:T(8,128)S(1)} %collective-permute-done.4.xside, f32[2,320,128]{2,1,0:T(8,128)S(1)} %collective-permute-done.5.dside, f32[2,512,512]{2,1,0:T(8,128)S(1)} %get-tuple-element.28.rolled, ...), custom_call_target="tpu_custom_call" | custom-call | flops 2000000000 | tf_op jit(solution)/shard_map/pallas_call | solution.py:34
  27.0 0.0 collective-permute-done.2.xcorner
  27.0 0.0 collective-permute-done.3.dcorner
  27.1 4.5 %main.1 = (bf16[4,320,256]{2,1,0:T(8,128)(2,1)S(1)}, bf16[4,320,256]{2,1,0:T(8,128)(2,1)S(1)}, f32[2,128,384]{2,1,0:T(8,128)S(1)}, f32[2,128,384]{2,1,0:T(8,128)...) custom-call(s32[2]{0:T(128)S(1)} %bitcast.5, f32[648,128]{1,0:T(8,128)S(1)} %collective-permute-done.inner, ...), custom_call_target="tpu_custom_call" | custom-call | flops 5000000000 | tf_op jit(solution)/shard_map/main/pallas_call | solution.py:573
  31.6 0.7 %collective-permute-start.8 = (f32[2,2,128,128]{3,2,1,0:T(8,128)S(1)}, f32[2,2,128,128]{3,2,1,0:T(8,128)S(1)}, u32[]{:S(2)}, u32[]{:S(2)}) collective-permute-start(f32[2,2,128,128]{3,2,1,0:T(8,128)S(1)} %get-tuple-element.39), channel_id=1, source_target_pairs={{1,2},{2,1},{5,6},{6,5},{9,10},{10,9},{13,14},{14,13},{17,18},{18,... | collective-permute-start | bytes 786440 | tf_op jit(solution)/shard_map/ppermute | solution.py:591
  32.2 2.9 %collective-permute-start.9 = (f32[2,2,128,128]{3,2,1,0:T(8,128)S(1)}, f32[2,2,128,128]{3,2,1,0:T(8,128)S(1)}, u32[]{:S(2)}, u32[]{:S(2)}) collective-permute-start(f32[2,2,128,128]{3,2,1,0:T(8,128)S(1)} %get-tuple-element.40), channel_id=1, source_target_pairs={{0,1},{1,0},{2,3},{3,2},{4,5},{5,4},{6,7},{7,6},{8,9},{9,8},{10,11... | collective-permute-start | bytes 786440 | tf_op jit(solution)/shard_map/ppermute | solution.py:592
  35.2 1.5 %shard_map.68 = (f32[2,320,320]{2,1,0:T(8,128)S(1)}, f32[2,320,128]{2,1,0:T(8,128)S(1)}, f32[2,320,128]{2,1,0:T(8,128)S(1)}) custom-call(s32[2]{0:T(128)S(1)} %bitcast.6, bf16[4,320,256]{2,1,0:T(8,128)(2,1)S(1)} %get-tuple-element.32.hi, bf16[4,320,256]{2,1,0:T(8,128)(2,1)S(1)} %get-tuple-element.33.lo, f32[2,512,512]{2,1,0:T(8,128)S(1)} %get-tuple-element.28.rolled, ...), custom_call_target="tpu_custom_call" | custom-call | flops 2000000000 | tf_op jit(solution)/shard_map/pallas_call | solution.py:34
  36.7 0.7 %collective-permute-start.6 = (f32[2,320,128]{2,1,0:T(8,128)S(1)}, f32[2,320,128]{2,1,0:T(8,128)S(1)}, u32[]{:S(2)}, u32[]{:S(2)}) collective-permute-start(f32[2,320,128]{2,1,0:T(8,128)S(1)} %get-tuple-element.35), channel_id=1, source_target_pairs={{1,2},{2,1},{5,6},{6,5},{9,10},{10,9},{13,14},{14,13},{17,18},{18,... | collective-permute-start | bytes 983048 | tf_op jit(solution)/shard_map/ppermute | solution.py:604
  37.4 1.5 %collective-permute-start.7 = (f32[2,320,128]{2,1,0:T(8,128)S(1)}, f32[2,320,128]{2,1,0:T(8,128)S(1)}, u32[]{:S(2)}, u32[]{:S(2)}) collective-permute-start(f32[2,320,128]{2,1,0:T(8,128)S(1)} %get-tuple-element.36), channel_id=1, source_target_pairs={{0,1},{1,0},{2,3},{3,2},{4,5},{5,4},{6,7},{7,6},{8,9},{9,8},{10,11... | collective-permute-start | bytes 983048 | tf_op jit(solution)/shard_map/ppermute | solution.py:605
  38.9 0.0 collective-permute-done.8.xcorn
  38.9 0.0 collective-permute-done.9.dcorn
  38.9 0.1 shard_map.70
  39.0 2.5 %collective-permute-start.10 = (f32[640,128]{1,0:T(8,128)S(1)}, f32[640,128]{1,0:T(8,128)S(1)}, u32[]{:S(2)}, u32[]{:S(2)}) collective-permute-start(f32[640,128]{1,0:T(8,128)S(1)} %get-tuple-element.41), channel_id=1, source_target_pairs={{0,4},{4,0},{8,12},{12,8},{16,20},{20,16},{24,28},{28,24},{1,5},{5... | collective-permute-start | bytes 983048 | tf_op jit(solution)/shard_map/ppermute | solution.py:602
  41.5 0.7 %collective-permute-start.11 = (f32[640,128]{1,0:T(8,128)S(1)}, f32[640,128]{1,0:T(8,128)S(1)}, u32[]{:S(2)}, u32[]{:S(2)}) collective-permute-start(f32[640,128]{1,0:T(8,128)S(1)} %get-tuple-element.42), channel_id=1, source_target_pairs={{4,8},{8,4},{12,16},{16,12},{20,24},{24,20},{5,9},{9,5},{13,17},{1... | collective-permute-start | bytes 983048 | tf_op jit(solution)/shard_map/ppermute | solution.py:603
  42.2 3.1 %shard_map.69.weight = f32[320,320]{1,0:T(8,128)S(1)} custom-call(s32[2]{0:T(128)S(1)} %bitcast.7, f32[536,128]{1,0:T(8,128)S(1)} %collective-permute-done.2.xcorner, f32[536,128]{1,0:T(8,128)S(1)} %collective-permute-done.3.dcorner, f32[648,128]{1,0:T(8,128)S(1)} %collective-permute-done.inner, f32[648,128]{1,0:T(8,128)S(1)} %collective-permute-done.1.cross, ...), custom_call_target="tpu_custom_call" | custom-call | flops 10000000000 | tf_op jit(solution)/shard_map/pallas_call | solution.py:34
  45.3 0.0 collective-permute-done.6.xedge
  45.3 0.0 collective-permute-done.7.dedge
  45.3 10.8 %collective-permute-done.10.inner = f32[640,128]{1,0:T(8,128)S(1)} collective-permute-done((f32[640,128]{1,0:T(8,128)S(1)}, f32[640,128]{1,0:T(8,128)S(1)}, u32[]{:S(2)}, u32[]{:S(2)}) %collective-permute-start.10) | collective-permute-done | bytes 327712 | tf_op jit(solution)/shard_map/ppermute | solution.py:602
  56.1 0.0 collective-permute-done.11.cross
  56.1 1.2 %shard_map.71 = f32[2,320,320]{2,1,0:T(8,128)} custom-call(f32[2,320,320]{2,1,0:T(8,128)S(1)} %copy-done.1, f32[2,320,320]{2,1,0:T(8,128)S(1)} %get-tuple-element.34.own, f32[320,320]{1,0:T(8,128)S(1)} %shard_map.69.weight, f32[2,320,128]{2,1,0:T(8,128)S(1)} %collective-permute-done.6.xedge, f32[2,320,128]{2,1,0:T(8,128)S(1)} %collective-permute-done.7.dedge, ...), custom_call_target="tpu_custom_call" | custom-call | tf_op jit(solution)/shard_map/pallas_call | solution.py:34
Async XLA Ops:
  1.2 17.2 %collective-permute-start = (f32[648,128]{1,0:T(8,128)S(1)}, f32[648,128]{1,0:T(8,128)S(1)}, u32[]{:S(2)}, u32[]{:S(2)}) collective-permute-start(f32[648,128]{1,0:T(8,128)S(1)} %get-tuple-element.24), channel_id=1, source_target_pairs={{0,4},{4,0},{8,12},{12,8},{16,20},{20,16},{24,28},{28,24},{1,5},{5... | collective-permute-start | bytes 995336 | tf_op jit(solution)/shard_map/ppermute | solution.py:534
  4.3 14.2 %collective-permute-start.1 = (f32[648,128]{1,0:T(8,128)S(1)}, f32[648,128]{1,0:T(8,128)S(1)}, u32[]{:S(2)}, u32[]{:S(2)}) collective-permute-start(f32[648,128]{1,0:T(8,128)S(1)} %get-tuple-element.25), channel_id=1, source_target_pairs={{4,8},{8,4},{12,16},{16,12},{20,24},{24,20},{5,9},{9,5},{13,17},{1... | collective-permute-start | bytes 995336 | tf_op jit(solution)/shard_map/ppermute | solution.py:535
  5.0 1.2 %copy-start = (f32[2,320,320]{2,1,0:T(8,128)S(1)}, f32[2,320,320]{2,1,0:T(8,128)}, u32[]{:S(2)}) copy-start(f32[2,320,320]{2,1,0:T(8,128)} %obj.7) | copy-start | bytes 2457604
  6.2 12.3 %copy-start.2 = (s32[1,1,1,2]{3,2,1,0:T(1,128)S(1)}, s32[1,1,1,2]{3,2,1,0:T(1,128)}, u32[]{:S(2)}) copy-start(s32[1,1,1,2]{3,2,1,0:T(1,128)} %offs.1) | copy-start | bytes 28
  6.2 16.7 %copy-start.3 = (f32[2,512,512]{2,1,0:T(8,128)S(1)}, f32[2,512,512]{2,1,0:T(8,128)}, u32[]{:S(2)}) copy-start(f32[2,512,512]{2,1,0:T(8,128)} %probe.3) | copy-start | bytes 6291460
  6.2 16.7 %copy-start.4 = (s32[1,1,1,512,512]{4,3,2,1,0:T(8,128)S(1)}, s32[1,1,1,512,512]{4,3,2,1,0:T(8,128)}, u32[]{:S(2)}) copy-start(s32[1,1,1,512,512]{4,3,2,1,0:T(8,128)} %param.9) | copy-start | bytes 3145732
  6.9 18.4 %collective-permute-start.4 = (f32[2,320,128]{2,1,0:T(8,128)S(1)}, f32[2,320,128]{2,1,0:T(8,128)S(1)}, u32[]{:S(2)}, u32[]{:S(2)}) collective-permute-start(f32[2,320,128]{2,1,0:T(8,128)S(1)} %get-tuple-element.30), channel_id=1, source_target_pairs={{1,2},{2,1},{5,6},{6,5},{9,10},{10,9},{13,14},{14,13},{17,18},{18,... | collective-permute-start | bytes 983048 | tf_op jit(solution)/shard_map/ppermute | solution.py:539
  7.7 17.6 %collective-permute-start.5 = (f32[2,320,128]{2,1,0:T(8,128)S(1)}, f32[2,320,128]{2,1,0:T(8,128)S(1)}, u32[]{:S(2)}, u32[]{:S(2)}) collective-permute-start(f32[2,320,128]{2,1,0:T(8,128)S(1)} %get-tuple-element.31), channel_id=1, source_target_pairs={{0,1},{1,0},{2,3},{3,2},{4,5},{5,4},{6,7},{7,6},{8,9},{9,8},{10,11... | collective-permute-start | bytes 983048 | tf_op jit(solution)/shard_map/ppermute | solution.py:540
  19.3 7.8 %collective-permute-start.2 = (f32[536,128]{1,0:T(8,128)S(1)}, f32[536,128]{1,0:T(8,128)S(1)}, u32[]{:S(2)}, u32[]{:S(2)}) collective-permute-start(f32[536,128]{1,0:T(8,128)S(1)} %get-tuple-element.26), channel_id=1, source_target_pairs={{1,2},{2,1},{5,6},{6,5},{9,10},{10,9},{13,14},{14,13},{17,18},{18,... | collective-permute-start | bytes 823304 | tf_op jit(solution)/shard_map/ppermute | solution.py:562
  19.9 7.1 %collective-permute-start.3 = (f32[536,128]{1,0:T(8,128)S(1)}, f32[536,128]{1,0:T(8,128)S(1)}, u32[]{:S(2)}, u32[]{:S(2)}) collective-permute-start(f32[536,128]{1,0:T(8,128)S(1)} %get-tuple-element.27), channel_id=1, source_target_pairs={{0,1},{1,0},{2,3},{3,2},{4,5},{5,4},{6,7},{7,6},{8,9},{9,8},{10,11... | collective-permute-start | bytes 823304 | tf_op jit(solution)/shard_map/ppermute | solution.py:563
  22.9 2.4 %copy-start.1 = (f32[2,320,320]{2,1,0:T(8,128)S(1)}, f32[2,320,320]{2,1,0:T(8,128)}, u32[]{:S(2)}) copy-start(f32[2,320,320]{2,1,0:T(8,128)} %obj.7) | copy-start | bytes 2457604
  22.9 2.4 %copy-start.5 = (bf16[8,256,256]{2,1,0:T(8,128)(2,1)S(1)}, bf16[8,256,256]{2,1,0:T(8,128)(2,1)}, u32[]{:S(2)}) copy-start(bf16[8,256,256]{2,1,0:T(8,128)(2,1)} %constant.4.clone.high) | copy-start | bytes 3145732
  22.9 2.4 %copy-start.6 = (bf16[8,256,256]{2,1,0:T(8,128)(2,1)S(1)}, bf16[8,256,256]{2,1,0:T(8,128)(2,1)}, u32[]{:S(2)}) copy-start(bf16[8,256,256]{2,1,0:T(8,128)(2,1)} %constant.5.clone.low) | copy-start | bytes 3145732
  31.6 7.3 %collective-permute-start.8 = (f32[2,2,128,128]{3,2,1,0:T(8,128)S(1)}, f32[2,2,128,128]{3,2,1,0:T(8,128)S(1)}, u32[]{:S(2)}, u32[]{:S(2)}) collective-permute-start(f32[2,2,128,128]{3,2,1,0:T(8,128)S(1)} %get-tuple-element.39), channel_id=1, source_target_pairs={{1,2},{2,1},{5,6},{6,5},{9,10},{10,9},{13,14},{14,13},{17,18},{18,... | collective-permute-start | bytes 786440 | tf_op jit(solution)/shard_map/ppermute | solution.py:591
  32.2 6.6 %collective-permute-start.9 = (f32[2,2,128,128]{3,2,1,0:T(8,128)S(1)}, f32[2,2,128,128]{3,2,1,0:T(8,128)S(1)}, u32[]{:S(2)}, u32[]{:S(2)}) collective-permute-start(f32[2,2,128,128]{3,2,1,0:T(8,128)S(1)} %get-tuple-element.40), channel_id=1, source_target_pairs={{0,1},{1,0},{2,3},{3,2},{4,5},{5,4},{6,7},{7,6},{8,9},{9,8},{10,11... | collective-permute-start | bytes 786440 | tf_op jit(solution)/shard_map/ppermute | solution.py:592
  36.7 8.6 %collective-permute-start.6 = (f32[2,320,128]{2,1,0:T(8,128)S(1)}, f32[2,320,128]{2,1,0:T(8,128)S(1)}, u32[]{:S(2)}, u32[]{:S(2)}) collective-permute-start(f32[2,320,128]{2,1,0:T(8,128)S(1)} %get-tuple-element.35), channel_id=1, source_target_pairs={{1,2},{2,1},{5,6},{6,5},{9,10},{10,9},{13,14},{14,13},{17,18},{18,... | collective-permute-start | bytes 983048 | tf_op jit(solution)/shard_map/ppermute | solution.py:604
  37.4 7.9 %collective-permute-start.7 = (f32[2,320,128]{2,1,0:T(8,128)S(1)}, f32[2,320,128]{2,1,0:T(8,128)S(1)}, u32[]{:S(2)}, u32[]{:S(2)}) collective-permute-start(f32[2,320,128]{2,1,0:T(8,128)S(1)} %get-tuple-element.36), channel_id=1, source_target_pairs={{0,1},{1,0},{2,3},{3,2},{4,5},{5,4},{6,7},{7,6},{8,9},{9,8},{10,11... | collective-permute-start | bytes 983048 | tf_op jit(solution)/shard_map/ppermute | solution.py:605
  39.0 17.1 %collective-permute-start.10 = (f32[640,128]{1,0:T(8,128)S(1)}, f32[640,128]{1,0:T(8,128)S(1)}, u32[]{:S(2)}, u32[]{:S(2)}) collective-permute-start(f32[640,128]{1,0:T(8,128)S(1)} %get-tuple-element.41), channel_id=1, source_target_pairs={{0,4},{4,0},{8,12},{12,8},{16,20},{20,16},{24,28},{28,24},{1,5},{5... | collective-permute-start | bytes 983048 | tf_op jit(solution)/shard_map/ppermute | solution.py:602
  41.5 14.6 %collective-permute-start.11 = (f32[640,128]{1,0:T(8,128)S(1)}, f32[640,128]{1,0:T(8,128)S(1)}, u32[]{:S(2)}, u32[]{:S(2)}) collective-permute-start(f32[640,128]{1,0:T(8,128)S(1)} %get-tuple-element.42), channel_id=1, source_target_pairs={{4,8},{8,4},{12,16},{16,12},{20,24},{24,20},{5,9},{9,5},{13,17},{1... | collective-permute-start | bytes 983048 | tf_op jit(solution)/shard_map/ppermute | solution.py:603

commit v5 on v4

--- a/solution.py
+++ b/solution.py
@@ -12,6 +12,7 @@
 
 OVL = 128
 HALF = 64
+KEPT = 192
 LANES = 128
 
 EPSILON = 0.01
@@ -23,18 +24,13 @@
 BF16 = jnp.bfloat16
 
 
-def call(kernel, out_shapes, args, smem=(), hbm_out=False, dtype=F32, scratch=(), flops=0, limit=16):
-    specs = [
-        pl.BlockSpec(memory_space=pltpu.SMEM if i in smem else pltpu.VMEM) for i in range(len(args))
-    ]
-    args = [
-        x if i in smem else pltpu.with_memory_space_constraint(x, pltpu.VMEM)
-        for i, x in enumerate(args)
-    ]
+def call(kernel, out_shapes, args, hbm_out=False, scratch=(), flops=0, limit=16):
+    specs = [pl.BlockSpec(memory_space=pltpu.VMEM) for _ in args]
+    args = [pltpu.with_memory_space_constraint(x, pltpu.VMEM) for x in args]
     return pl.pallas_call(
         kernel,
         out_shape=[
-            jax.ShapeDtypeStruct(s, F32) if hbm_out else pltpu.VMEM(s, dtype) for s in out_shapes
+            jax.ShapeDtypeStruct(s, F32) if hbm_out else pltpu.VMEM(s, F32) for s in out_shapes
         ],
         in_specs=specs,
         out_specs=[pl.BlockSpec(memory_space=pltpu.VMEM) for _ in out_shapes],
@@ -103,7 +99,27 @@
     return lax.axis_index(axis) % 2 == 1
 
 
-def row_kernel(offs, obj, inner, cross, held, numbers, sems):
+def paired(axis, x, first):
+    place, count = lax.axis_index(axis), lax.axis_size(axis)
+    if first == 0 and count % 2 == 0:
+        return x
+    if first == 0:
+        return jnp.where(place < count - 1, x, 0.0)
+    alone = place == 0 if count % 2 else (place == 0) | (place == count - 1)
+    return jnp.where(alone, 0.0, x)
+
+
+def offsets_tile(u, v):
+    row = row_iota((8, LANES))
+    return jnp.where(row == 0, u, jnp.where(row == 1, v, 1)).astype(F32)
+
+
+def number(tile, i):
+    picked = (lane_iota(tile.shape) == 0) & (row_iota(tile.shape) == i)
+    return jnp.sum(jnp.where(picked, tile, 0.0))
+
+
+def row_kernel(offs, obj, inner, cross, mine, held, numbers, sems):
     rows, cols = obj.shape[1:]
     far = odd("row")
     bases = jnp.where(far, 0, rows - OVL), jnp.where(far, rows - OVL, 0)
@@ -114,54 +130,66 @@
     for copy in (copies[1], copies[0], copies[2]):
         copy.start()
     copies[0].wait()
-    lane = lane_iota((8, LANES))
-    first, second = numbers[0, 0, 0, 0], numbers[0, 0, 0, 1]
-    info = jnp.where(lane == 0, first, jnp.where(lane == 1, second, 1)).astype(F32)
+    info = offsets_tile(numbers[0, 0, 0, 0], numbers[0, 0, 0, 1])
+    mine[...] = info
     for t, out in enumerate((inner, cross)):
-        out[5 * OVL : 5 * OVL + 8, :] = info
+        out[5 * OVL : 5 * OVL + 8, :] = paired("row", info, t)
         copies[1 + t].wait()
         for c in range(2):
             for k in range(2):
                 at = (2 * c + k) * OVL
-                out[at : at + OVL, :] = held[t, c, :, 128 * k : 128 * k + 128]
-            out[4 * OVL : 5 * OVL, c * HALF : c * HALF + HALF] = held[t, c, :, 256:cols]
-
-
-def side_kernel(obj, xside, dside):
-    cols = obj.shape[2]
+                out[at : at + OVL, :] = paired("row", held[t, c, :, 128 * k : 128 * k + 128], t)
+            tail = paired("row", held[t, c, :, 256:cols], t)
+            out[4 * OVL : 5 * OVL, c * HALF : c * HALF + HALF] = tail
+
+
+def side_kernel(mine, obj, xside, dside):
+    cells, cols = obj.shape[1:]
     right = odd("col")
+    info = mine[...]
     for c in range(2):
+        rows = slice(c * cells, c * cells + cells)
         west = turn(obj[c, :, 0:128])
         east = obj[c, :, cols - OVL : cols]
-        xside[c] = jnp.where(right, east, west)
-        dside[c] = jnp.where(right, west, east)
-
-
-def corner_kernel(offs, inner, cross, xside, dside):
-    right = odd("col")
-    lane = lane_iota((OVL, LANES))
-    for part, halo in enumerate((inner, cross)):
-        for c in range(2):
-            west = turn(halo[2 * c * OVL : 2 * c * OVL + OVL, :])
-            tail = halo[4 * OVL : 5 * OVL, :]
-            middle = turn(halo[(2 * c + 1) * OVL : (2 * c + 2) * OVL, :])
-            east = jnp.where(lane < HALF, middle, turn(tail) if c == 0 else tail)
-            rows = slice((2 * part + c) * OVL, (2 * part + c) * OVL + OVL)
-            xside[rows, :] = jnp.where(right, east, west)
-            dside[rows, :] = jnp.where(right, west, east)
-    lane = lane_iota((8, LANES))
-    info = jnp.where(lane == 0, offs[0], jnp.where(lane == 1, offs[1], 1)).astype(F32)
-    for out in (xside, dside):
-        out[4 * OVL : 4 * OVL + 8, :] = inner[5 * OVL : 5 * OVL + 8, :]
-        out[4 * OVL + 8 : 4 * OVL + 16, :] = cross[5 * OVL : 5 * OVL + 8, :]
-        out[4 * OVL + 16 : 4 * OVL + 24, :] = info
-
-
-def ready_kernel(offs, probe, counts, rolled, measured, wide):
+        xside[rows, :] = paired("col", jnp.where(right, east, west), 1)
+        dside[rows, :] = paired("col", jnp.where(right, west, east), 0)
+    xside[2 * cells : 2 * cells + 8, :] = paired("col", info, 1)
+    dside[2 * cells : 2 * cells + 8, :] = paired("col", info, 0)
+
+
+def corner_kernel(first, mine, inner, cross, side, out):
+    far = odd("row")
+    to_right = odd("col") if first else ~odd("col")
+    cells = (side.shape[0] - 8) // 2
+    border = side[2 * cells : 2 * cells + 1, :]
+    lane = lane_iota((HALF, LANES))
+    row = row_iota((HALF, LANES)).astype(F32)
+
+    def end(part, c, base):
+        def take(tile):
+            at = slice(tile * OVL + base, tile * OVL + base + HALF)
+            a, b = inner[at, :], cross[at, :]
+            return jnp.where(far, a, b) if part == 0 else jnp.where(far, b, a)
+
+        tail = take(4)
+        east = jnp.where(lane < HALF, turn(take(2 * c + 1)), turn(tail) if c == 0 else tail)
+        return paired("col", jnp.where(to_right, east, turn(take(2 * c))), first)
+
+    for c in range(2):
+        base = c * KEPT
+        out[base : base + HALF, :] = jnp.where(row < border, end(1, c, HALF), end(0, c, 0))
+        out[base + HALF : base + OVL, :] = end(0, c, HALF)
+        out[base + OVL : base + KEPT, :] = end(1, c, 0)
+    rows = 2 * KEPT
+    out[rows : rows + 8, :] = paired("col", inner[5 * OVL : 5 * OVL + 8, :], first)
+    out[rows + 8 : rows + 16, :] = paired("col", cross[5 * OVL : 5 * OVL + 8, :], first)
+    out[rows + 16 : rows + 24, :] = paired("col", mine[...], first)
+
+
+def ready_kernel(mine, probe, counts, rolled, measured, wide):
     size = probe.shape[-1]
     quarter = size // 4
-    u = offs[0]
-    v = offs[1]
+    u, v = [number(mine[...], i).astype(jnp.int32) for i in range(2)]
     for c in range(2):
         for t in range(4):
             cols = slice(t * quarter, (t + 1) * quarter)
@@ -213,10 +241,12 @@
         grads[0].append(ar * br + ai * bi)
         grads[1].append(ar * bi - ai * br)
     lane = lane_iota((STEP, LANES))
+    early = lane.astype(F32) < v
     for g in grads:
-        wout = turn(jnp.where(lane >= v, g[0], 0.0))
-        eout = turn(jnp.where(lane < HALF, jnp.where(lane < v, g[0], 0.0), g[3]))
-        yield g[1:], jnp.where(right, eout, wout), jnp.where(right, wout, eout)
+        wout = turn(jnp.where(early, 0.0, g[0]))
+        eout = turn(jnp.where(lane < HALF, jnp.where(early, g[0], 0.0), g[3]))
+        xout = paired("col", jnp.where(right, eout, wout), 1)
+        yield g[1:], xout, paired("col", jnp.where(right, wout, eout), 0)
 
 
 def right_product(hi, lo, rows, p, high, low, k):
@@ -229,11 +259,12 @@
     return dot(high[k], a) + dot(high[k], lo[at]) + dot(low[k], a)
 
 
-def fore_kernel(offs, obj, xside, dside, rolled, high, low, z, hi, lo):
+def fore_kernel(mine, obj, xside, dside, rolled, high, low, z, hi, lo):
     cells = obj.shape[1]
-    v = offs[1]
+    v = mine[1:2, :]
     right = odd("col")
     lane = lane_iota((STEP, LANES))
+    early = lane.astype(F32) < v
     for top in range(0, cells, cells // 2):
         for base in range(top, top + cells // 2, STEP):
             rows = slice(base, base + STEP)
@@ -241,11 +272,12 @@
             for c in range(2):
                 last = obj[c, rows, 256:cells]
                 last = jnp.concatenate([last, last], axis=1)
-                x, d = xside[c, rows, :], dside[c, rows, :]
+                at = slice(c * cells + base, c * cells + base + STEP)
+                x, d = xside[at, :], dside[at, :]
                 w, e = jnp.where(right, d, x), jnp.where(right, x, d)
                 tiles.append(
                     [
-                        jnp.where(lane < v, e, w),
+                        jnp.where(early, e, w),
                         obj[c, rows, 0:128],
                         obj[c, rows, 128:256],
                         jnp.where(lane < HALF, last, e),
@@ -258,38 +290,41 @@
 
 
 def main_kernel(
-    offs, inner, cross, xcorner, dcorner, rolled, measured, zown, high, low,
+    mine, inner, cross, xcorner, dcorner, rolled, measured, zown, high, low,
     own_hi, own_lo, nblock, sblock, xcorn, dcorn, ah, al, bh, bl, zh, tf,
 ):
     size = rolled.shape[-1]
     quarter = size // 4
     cells = zown.shape[1]
-    u = offs[0]
-    v = offs[1]
+    u = mine[0:1, :]
+    v = mine[1:2, :]
     right = odd("col")
     far = odd("row")
     lane = lane_iota((STEP, LANES))
-
-    def pieces(c, part, base):
-        def take(first, second, at, again):
-            a, b = first[at : at + STEP, :], second[again : again + STEP, :]
-            return jnp.where(far, a, b) if part == 0 else jnp.where(far, b, a)
-
-        tiles = [take(inner, cross, t * OVL + base, t * OVL + base) for t in (2 * c, 2 * c + 1, 4)]
+    early = lane.astype(F32) < v
+    step_row = row_iota((STEP, LANES)).astype(F32)
+
+    def patch(c, slot, base):
+        def halo(part, start):
+            tiles = []
+            for t in (2 * c, 2 * c + 1, 4):
+                at = slice(t * OVL + start, t * OVL + start + STEP)
+                a, b = inner[at, :], cross[at, :]
+                tiles.append(jnp.where(far, a, b) if part == 0 else jnp.where(far, b, a))
+            return tiles
+
+        if slot >= OVL:
+            tiles = halo(1, slot - OVL - cells)
+        else:
+            tiles = halo(0, slot)
+        if slot < HALF:
+            row = step_row + slot
+            tiles = [jnp.where(row < u, b, a) for a, b in zip(tiles, halo(1, slot + HALF))]
         last = turn(tiles[2]) if c == 1 else tiles[2]
-        x = take(xcorner, xcorner, c * OVL + base, (2 + c) * OVL + base)
-        d = take(dcorner, dcorner, c * OVL + base, (2 + c) * OVL + base)
+        at = slice(c * KEPT + base, c * KEPT + base + STEP)
+        x, d = xcorner[at, :], dcorner[at, :]
         w, e = jnp.where(right, d, x), jnp.where(right, x, d)
-        return [jnp.where(lane < v, e, w), tiles[0], tiles[1], jnp.where(lane < HALF, last, e)]
-
-    def patch(c, slot):
-        if slot >= OVL:
-            return pieces(c, 1, slot - OVL - cells)
-        above = pieces(c, 0, slot)
-        if slot >= HALF:
-            return above
-        row = row_iota((STEP, LANES)) + slot
-        return [jnp.where(row < u, y, x) for x, y in zip(above, pieces(c, 1, slot + HALF))]
+        return [jnp.where(early, e, w), tiles[0], tiles[1], jnp.where(lane < HALF, last, e)]
 
     block = 2 * quarter
     re, im = slice(0, quarter), slice(quarter, 2 * quarter)
@@ -298,7 +333,7 @@
 
     for base, slot in zip(range(0, count, STEP), slots):
         rows = slice(slot, slot + STEP)
-        enter([patch(c, slot) for c in range(2)], rolled, rows, ah, al, slice(base, base + STEP))
+        enter([patch(c, slot, base) for c in range(2)], rolled, rows, ah, al, slice(base, base + STEP))
     for p in range(4):
         zh[p] = right_product(ah, al, slice(0, count), p, high, low, p)
 
@@ -345,7 +380,7 @@
         zh[p] = right_product(ah, al, slice(0, count), p, high, low, 4 + p)
     for base, slot in zip(range(0, count, STEP), slots):
         at, rows = slice(base, base + STEP), slice(slot, slot + STEP)
-        row = row_iota((STEP, LANES)) + slot
+        row = step_row + slot
         sends = []
         if slot < OVL:
             sends.append((0, slot, row >= u if slot < HALF else None))
@@ -354,19 +389,19 @@
         if slot >= OVL:
             sends.append((1, slot - OVL - cells, None))
         for c, (g, xout, dout) in enumerate(leave(zh, at, rolled, rows, v, right)):
+            xcorn[c, at, :] = xout
+            dcorn[c, at, :] = dout
             for part, o, mask in sends:
                 to = slice(o, o + STEP)
                 put = (lambda x: x) if mask is None else (lambda x: jnp.where(mask, x, 0.0))
                 block = (nblock, sblock)[part]
                 for t in range(3):
                     block[c, to, 128 * t : 128 * t + 128] = put(g[t])
-                xcorn[part, c, to, :] = put(xout)
-                dcorn[part, c, to, :] = put(dout)
-
-
-def after_kernel(offs, hi, lo, rolled, high, low, own, xedge, dedge, z):
+
+
+def after_kernel(mine, hi, lo, rolled, high, low, own, xedge, dedge, z):
     cells = own.shape[1]
-    v = offs[1]
+    v = mine[1:2, :]
     right = odd("col")
     for top in range(0, cells, cells // 2):
         rows = slice(top, top + cells // 2)
@@ -382,28 +417,43 @@
                 dedge[c, at, :] = dout
 
 
-def send_kernel(nblock, sblock, xcorn, dcorn, inner, cross):
+def send_kernel(nblock, sblock, xcorn, dcorn, xcorner, dcorner, inner, cross):
     right = odd("col")
     far = odd("row")
-    first = lane_iota((OVL, LANES)) < HALF
-    tiles = []
-    for part, block in enumerate((nblock, sblock)):
-        last, out = [], []
-        for c in range(2):
-            x, d = xcorn[part, c], dcorn[part, c]
-            fw, fe = jnp.where(right, d, x), jnp.where(right, x, d)
-            out.append(block[c, :, 0:128] + fw)
-            out.append(block[c, :, 128:256] + jnp.where(first, 0.0, fe))
-            last.append(block[c, :, 256:384] + fe)
-        out.append(jnp.where(first, last[0], turn(last[1])))
-        tiles.append(out)
-    for t, (n, s) in enumerate(zip(*tiles)):
-        inner[t * OVL : t * OVL + OVL, :] = jnp.where(far, n, s)
-        cross[t * OVL : t * OVL + OVL, :] = jnp.where(far, s, n)
+    first = lane_iota((HALF, LANES)) < HALF
+    row = row_iota((HALF, LANES)).astype(F32)
+    at = 2 * KEPT + 16
+    borders = [ref[at : at + 1, :] for ref in (xcorner, dcorner)]
+
+    def corner(ref, border, c, part, base):
+        if part == 1 and base == 0:
+            return ref[c, OVL:KEPT, :]
+        if part == 0 and base == HALF:
+            return ref[c, HALF:OVL, :]
+        mixed = ref[c, 0:HALF, :]
+        return jnp.where((row < border) == (part == 1), mixed, 0.0)
+
+    for base in (0, HALF):
+        rows = slice(base, base + HALF)
+        tiles = []
+        for part, block in enumerate((nblock, sblock)):
+            last, out = [], []
+            for c in range(2):
+                x, d = [corner(*pair, c, part, base) for pair in zip((xcorn, dcorn), borders)]
+                fw, fe = jnp.where(right, d, x), jnp.where(right, x, d)
+                out.append(block[c, rows, 0:128] + fw)
+                out.append(block[c, rows, 128:256] + jnp.where(first, 0.0, fe))
+                last.append(block[c, rows, 256:384] + fe)
+            out.append(jnp.where(first, last[0], turn(last[1])))
+            tiles.append(out)
+        for t, (n, s) in enumerate(zip(*tiles)):
+            to = slice(t * OVL + base, t * OVL + base + HALF)
+            inner[to, :] = paired("row", jnp.where(far, n, s), 0)
+            cross[to, :] = paired("row", jnp.where(far, s, n), 1)
 
 
 def light_kernel(
-    offs, xcorner, dcorner, inner, cross, probe, weight, pad, acc
+    mine, xcorner, dcorner, inner, cross, probe, weight, pad, acc
 ):
     size = probe.shape[-1]
     cells = weight.shape[0]
@@ -417,28 +467,25 @@
     acc[...] = jnp.zeros(acc.shape, F32)
     first = lane_iota((HALF, LANES)) < HALF
     right = odd("col")
-    unit = row_iota((8, LANES)) == 0
-    lane = lane_iota((8, LANES))
     for di in (0, -1, 1):
         for dj in (0, -1, 1):
+
+            def take(first, second, at, again):
+                a, b = first[at : at + 8, :], second[again : again + 8, :]
+                return jnp.where(far, a, b) if di < 0 else jnp.where(far, b, a)
+
             if di == 0 and dj == 0:
-                u, v, there = offs[0], offs[1], 1.0
+                tile = mine[...]
+            elif dj == 0:
+                tile = take(inner, cross, 5 * OVL, 5 * OVL)
             else:
-
-                def take(first, second, at, again):
-                    a, b = first[at : at + 8, :], second[again : again + 8, :]
-                    return jnp.where(far, a, b) if di < 0 else jnp.where(far, b, a)
-
-                if dj == 0:
-                    tile = take(inner, cross, 5 * OVL, 5 * OVL)
+                if di == 0:
+                    x, d = [ref[2 * KEPT + 16 : 2 * KEPT + 24, :] for ref in (xcorner, dcorner)]
                 else:
-                    if di == 0:
-                        x, d = [ref[4 * OVL + 16 : 4 * OVL + 24, :] for ref in (xcorner, dcorner)]
-                    else:
-                        x, d = [take(ref, ref, 4 * OVL, 4 * OVL + 8) for ref in (xcorner, dcorner)]
-                    tile = jnp.where(right, d, x) if dj < 0 else jnp.where(right, x, d)
-                u, v, there = [jnp.sum(jnp.where(unit & (lane == i), tile, 0.0)) for i in range(3)]
-                u, v = u.astype(jnp.int32), v.astype(jnp.int32)
+                    x, d = [take(ref, ref, 2 * KEPT, 2 * KEPT + 8) for ref in (xcorner, dcorner)]
+                tile = jnp.where(right, d, x) if dj < 0 else jnp.where(right, x, d)
+            u, v, there = [number(tile, i) for i in range(3)]
+            u, v = u.astype(jnp.int32), v.astype(jnp.int32)
             start, count, put = {
                 0: (2 * OVL - u, cells, 0),
                 1: (OVL - u, OVL, cells - OVL),
@@ -501,49 +548,66 @@
                 updated[c, rows, cols] = obj[c, rows, cols] - x * weight[rows, cols]
 
 
-def swaps(axis):
-    count = lax.axis_size(axis)
-    return [
-        [pair for i in range(first, count - 1, 2) for pair in ((i, i + 1), (i + 1, i))]
-        for first in (1, 0)
-    ]
+def swap(count, first):
+    partner = list(range(count))
+    for i in range(first, count - 1, 2):
+        partner[i], partner[i + 1] = i + 1, i
+    return partner
+
+
+def routes():
+    rows, cols = lax.axis_size("row"), lax.axis_size("col")
+    odd_row, even_row = swap(rows, 1), swap(rows, 0)
+    odd_col, even_col = swap(cols, 1), swap(cols, 0)
+
+    def pairs(partner):
+        grid = [(r, c, *partner(r, c)) for r in range(rows) for c in range(cols)]
+        return [(r * cols + c, to_r * cols + to_c) for r, c, to_r, to_c in grid]
+
+    return (
+        pairs(lambda r, c: (odd_row[r], c if odd_row[r] != r else even_col[c])),
+        pairs(lambda r, c: (even_row[r], c)),
+        pairs(lambda r, c: (r, odd_col[c])),
+        pairs(lambda r, c: (r, even_col[c])),
+        pairs(lambda r, c: (r if odd_col[c] != c else even_row[r], odd_col[c])),
+    )
+
+
+def permute(x, pairs):
+    return lax.ppermute(x, ("row", "col"), pairs)
 
 
 def local(object_slab, probe_field, offsets, counts):
     cells = object_slab.shape[1]
     size = probe_field.shape[-1]
-    row_cross, row_inner = swaps("row")
-    col_cross, col_inner = swaps("col")
-    offs = offsets.reshape(2)
+    row_cross, row_inner, col_cross, col_inner, col_full = routes()
     table_high, table_low = tables(size)
     high, low = jnp.asarray(table_high), jnp.asarray(table_low)
 
-    to_inner, to_cross = pl.pallas_call(
+    to_inner, to_cross, mine = pl.pallas_call(
         row_kernel,
         name="rows",
-        out_shape=[pltpu.VMEM((5 * OVL + 8, LANES), F32) for _ in range(2)],
+        out_shape=[pltpu.VMEM((n, LANES), F32) for n in (5 * OVL + 8, 5 * OVL + 8, 8)],
         in_specs=[pl.BlockSpec(memory_space=pltpu.HBM) for _ in range(2)],
-        out_specs=[pl.BlockSpec(memory_space=pltpu.VMEM) for _ in range(2)],
+        out_specs=[pl.BlockSpec(memory_space=pltpu.VMEM) for _ in range(3)],
         scratch_shapes=[
             pltpu.VMEM((2, 2, OVL, cells), F32),
             pltpu.SMEM((1, 1, 1, 2), jnp.int32),
             pltpu.SemaphoreType.DMA((3,)),
         ],
         compiler_params=pltpu.CompilerParams(vmem_limit_bytes=8 * 1024 * 1024),
+        cost_estimate=pl.CostEstimate(flops=5_000_000_000, bytes_accessed=0, transcendentals=0),
     )(*[pltpu.with_memory_space_constraint(x, pltpu.HBM) for x in (offsets, object_slab)])
-    halo_inner = lax.ppermute(to_inner, "row", row_inner)
-    halo_cross = lax.ppermute(to_cross, "row", row_cross)
-    xside, dside = call(
-        side_kernel, [(2, cells, OVL), (2, cells, OVL)], [object_slab], flops=5_000_000_000
-    )
-    side_x = lax.ppermute(xside, "col", col_cross)
-    side_d = lax.ppermute(dside, "col", col_inner)
+    halo_inner = permute(to_inner, row_inner)
+    halo_cross = permute(to_cross, row_cross)
+    xside, dside = call(side_kernel, [(2 * cells + 8, OVL)] * 2, [mine, object_slab], flops=5_000_000_000)
+    side_x = permute(xside, col_cross)
+    side_d = permute(dside, col_inner)
 
     rolled, measured = call(
         ready_kernel,
         [(2, size, size), (size, size)],
-        [offs, probe_field, counts.reshape(size, size)],
-        smem=(0,),
+        [mine, probe_field, counts.reshape(size, size)],
         scratch=[pltpu.VMEM((2, 4, size + HALF, LANES), F32)],
         flops=5_000_000_000,
     )
@@ -551,31 +615,31 @@
     (zown,) = call(
         fore_kernel,
         [(4, cells, half)],
-        [offs, object_slab, side_x, side_d, rolled, high, low],
-        smem=(0,),
+        [mine, object_slab, side_x, side_d, rolled, high, low],
         scratch=[pltpu.VMEM((4, cells, half), BF16) for _ in range(2)],
         flops=2_000_000_000,
     )
-    xcorner, dcorner = call(
-        corner_kernel, [(4 * OVL + 24, OVL)] * 2, [offs, halo_inner, halo_cross], smem=(0,)
-    )
-    corner_x = lax.ppermute(xcorner, "col", col_cross)
-    corner_d = lax.ppermute(dcorner, "col", col_inner)
+    ends = []
+    for first, side in ((1, side_x), (0, side_d)):
+        kernel = functools.partial(corner_kernel, first)
+        operands = [mine, halo_inner, halo_cross, side]
+        ends += call(kernel, [(2 * KEPT + 24, OVL)], operands)
+    corner_x = permute(ends[0], col_full)
+    corner_d = permute(ends[1], col_inner)
     shapes = [
         ((4, cells, half), BF16),
         ((4, cells, half), BF16),
         ((2, OVL, 384), F32),
         ((2, OVL, 384), F32),
-        ((2, 2, OVL, OVL), F32),
-        ((2, 2, OVL, OVL), F32),
+        ((2, count, OVL), F32),
+        ((2, count, OVL), F32),
     ]
-    operands = [halo_inner, halo_cross, corner_x, corner_d, rolled, measured, zown, high, low]
+    operands = [mine, halo_inner, halo_cross, corner_x, corner_d, rolled, measured, zown, high, low]
     own_hi, own_lo, nblock, sblock, xcorn, dcorn = pl.pallas_call(
         main_kernel,
         name="main",
         out_shape=[pltpu.VMEM(s, d) for s, d in shapes],
-        in_specs=[pl.BlockSpec(memory_space=pltpu.SMEM)]
-        + [pl.BlockSpec(memory_space=pltpu.VMEM) for _ in operands],
+        in_specs=[pl.BlockSpec(memory_space=pltpu.VMEM) for _ in operands],
         out_specs=[pl.BlockSpec(memory_space=pltpu.VMEM) for _ in shapes],
         scratch_shapes=[
             pltpu.VMEM((4, count, half), BF16),
@@ -587,27 +651,25 @@
         ],
         compiler_params=pltpu.CompilerParams(vmem_limit_bytes=20 * 1024 * 1024),
         cost_estimate=pl.CostEstimate(flops=5_000_000_000, bytes_accessed=0, transcendentals=0),
-    )(offs, *[pltpu.with_memory_space_constraint(x, pltpu.VMEM) for x in operands])
-    fix_x = lax.ppermute(xcorn, "col", col_cross)
-    fix_d = lax.ppermute(dcorn, "col", col_inner)
+    )(*[pltpu.with_memory_space_constraint(x, pltpu.VMEM) for x in operands])
+    fix_x = permute(xcorn, col_full)
+    fix_d = permute(dcorn, col_inner)
     own, xedge, dedge = call(
         after_kernel,
         [(2, cells, cells), (2, cells, OVL), (2, cells, OVL)],
-        [offs, own_hi, own_lo, rolled, high, low],
-        smem=(0,),
+        [mine, own_hi, own_lo, rolled, high, low],
         scratch=[pltpu.VMEM((4, cells, half), F32)],
         flops=2_000_000_000,
     )
-    to_inner, to_cross = call(send_kernel, [(5 * OVL, LANES)] * 2, [nblock, sblock, fix_x, fix_d])
-    grad_inner = lax.ppermute(to_inner, "row", row_inner)
-    grad_cross = lax.ppermute(to_cross, "row", row_cross)
-    edge_x = lax.ppermute(xedge, "col", col_cross)
-    edge_d = lax.ppermute(dedge, "col", col_inner)
+    to_inner, to_cross = call(send_kernel, [(5 * OVL, LANES)] * 2, [nblock, sblock, fix_x, fix_d, corner_x, corner_d])
+    grad_inner = permute(to_inner, row_inner)
+    grad_cross = permute(to_cross, row_cross)
+    edge_x = permute(xedge, col_cross)
+    edge_d = permute(dedge, col_inner)
     (weight,) = call(
         light_kernel,
         [(cells, cells)],
-        [offs, corner_x, corner_d, halo_inner, halo_cross, probe_field],
-        smem=(0,),
+        [mine, corner_x, corner_d, halo_inner, halo_cross, probe_field],
         scratch=[pltpu.VMEM((6, size + 2 * OVL, LANES), F32), pltpu.VMEM((cells, 384), F32)],
         flops=10_000_000_000,
     )

time: 57.6 us -> 54.3 us (0.943)
  waiting for transfers between devices: 18.7 us -> 26.1 us
  starting transfers between devices: 20 us -> 13.4 us
  Pallas kernels: 17.2 us -> 14.3 us
  local copies, waits for them, and re-layouts: 1.22 us -> 0.12 us
    ppermute x12, waiting for transfers between devices: 18.7 us -> 26.1 us  [permute(): return lax.ppermute(x, ('row', 'col'), pairs)]
    ppermute x12, starting transfers between devices: 20 us -> 13.4 us  [permute(): return lax.ppermute(x, ('row', 'col'), pairs)]
    pallas_call x8 -> x9, Pallas kernels: 11.5 us -> 9.04 us  [call(): pl.pallas_call(kernel, out_shape=[jax.ShapeDtypeStruct(s, F32) if hbm_out...]
    unnamed x14 -> x10, local copies, waits for them, and re-layouts: 1.22 us -> 0.12 us
  transfers between devices with their start and end apart: 12 -> 12, of which waited for: 2 -> 3; matrix products, arithmetic and copies ran while one was open for 0% -> 0% of each run, Pallas kernels for 18% -> 13%
where the time goes in v5:
time: 54.3 us; the launch traced here: 54.1 us
  waiting for transfers between devices  26.1 us (48%)
  Pallas kernels  14.3 us (26%)
  starting transfers between devices  13.4 us (25%)
    ppermute x12, waiting for transfers between devices, permute(): return lax.ppermute(x, ('row', 'col'), pairs)  26.1 us
    ppermute x12, starting transfers between devices, permute(): return lax.ppermute(x, ('row', 'col'), pairs)  13.4 us
    pallas_call x9, Pallas kernels, call(): pl.pallas_call(kernel, out_shape=[jax.ShapeDtypeStruct(s, F32) if hbm_out...  9.04 us
    pallas_call x1, Pallas kernels, local(): pl.pallas_call(main_kernel, name='main', out_shape=[pltpu.VMEM(s, d) for...  3.95 us
    pallas_call x1, Pallas kernels, local(): pl.pallas_call(row_kernel, name='rows', out_shape=[pltpu.VMEM((n, LANES),...  1.32 us
  transfers between devices with their start and end apart: 12, of which 3 were waited for; matrix products, arithmetic and copies ran while one was open for 0% of the time, Pallas kernels for 13%

profile of v5, /device:TPU:0, one launch (start us, length us, event | category | flops | bytes accessed | tf_op | source)
XLA Modules:
  0.0 54.1 jit_solution(14199230187064494830)
XLA Ops:
  0.0 0.0 copy-start
  0.0 1.3 %rows.1 = (f32[648,128]{1,0:T(8,128)S(1)}, f32[648,128]{1,0:T(8,128)S(1)}, f32[8,128]{1,0:T(8,128)S(1)}) custom-call(s32[1,1,1,2]{3,2,1,0:T(1,128)} %offs.1, f32[2,320,320]{2,1,0:T(8,128)} %obj.7), custom_call_target="tpu_custom_call" | custom-call | flops 5000000000 | tf_op jit(solution)/shard_map/rows/pallas_call | solution.py:587
  1.3 0.1 copy-done
  1.4 0.0 copy-start.2
  1.4 0.7 %shard_map.64 = (f32[648,128]{1,0:T(8,128)S(1)}, f32[648,128]{1,0:T(8,128)S(1)}) custom-call(f32[8,128]{1,0:T(8,128)S(1)} %get-tuple-element.23.mine, f32[2,320,320]{2,1,0:T(8,128)S(1)} %copy-done), custom_call_target="tpu_custom_call" | custom-call | flops 5000000000 | tf_op jit(solution)/shard_map/pallas_call | solution.py:30
  2.1 0.0 copy-start.1
  2.1 0.6 %collective-permute-start.4 = (f32[648,128]{1,0:T(8,128)S(1)}, f32[648,128]{1,0:T(8,128)S(1)}, u32[]{:S(2)}, u32[]{:S(2)}) collective-permute-start(f32[648,128]{1,0:T(8,128)S(1)} %get-tuple-element.27), channel_id=1, source_target_pairs={{0,1},{1,0},{2,3},{3,2},{4,5},{5,4},{6,7},{7,6},{8,9},{9,8},{10,11... | collective-permute-start | bytes 995336 | tf_op jit(solution)/shard_map/ppermute | solution.py:577
  2.7 2.6 %collective-permute-start = (f32[648,128]{1,0:T(8,128)S(1)}, f32[648,128]{1,0:T(8,128)S(1)}, u32[]{:S(2)}, u32[]{:S(2)}) collective-permute-start(f32[648,128]{1,0:T(8,128)S(1)} %get-tuple-element.24), channel_id=1, source_target_pairs={{0,4},{1,5},{2,6},{3,7},{4,0},{5,1},{6,2},{7,3},{8,12},{9,13},{10,... | collective-permute-start | bytes 995336 | tf_op jit(solution)/shard_map/ppermute | solution.py:577
  5.3 0.2 collective-permute-start.1
  5.4 0.7 %collective-permute-start.2 = (f32[648,128]{1,0:T(8,128)S(1)}, f32[648,128]{1,0:T(8,128)S(1)}, u32[]{:S(2)}, u32[]{:S(2)}) collective-permute-start(f32[648,128]{1,0:T(8,128)S(1)} %get-tuple-element.26), channel_id=1, source_target_pairs={{0,0},{1,2},{2,1},{3,3},{4,4},{5,6},{6,5},{7,7},{8,8},{9,10},{10,9... | collective-permute-start | bytes 995336 | tf_op jit(solution)/shard_map/ppermute | solution.py:577
  6.1 0.0 collective-permute-done.4.side.dside
  6.1 13.9 %collective-permute-done.inner = f32[648,128]{1,0:T(8,128)S(1)} collective-permute-done((f32[648,128]{1,0:T(8,128)S(1)}, f32[648,128]{1,0:T(8,128)S(1)}, u32[]{:S(2)}, u32[]{:S(2)}) %collective-permute-start) | collective-permute-done | bytes 331808 | tf_op jit(solution)/shard_map/ppermute | solution.py:577
  20.0 0.0 collective-permute-done.1.cross
  20.0 0.3 shard_map.66
  20.3 0.1 collective-permute-start.5
  20.4 0.0 collective-permute-done.2.side.xside
  20.4 0.3 shard_map.65
  20.7 2.5 %collective-permute-start.3 = (f32[408,128]{1,0:T(8,128)S(1)}, f32[408,128]{1,0:T(8,128)S(1)}, u32[]{:S(2)}, u32[]{:S(2)}) collective-permute-start(f32[408,128]{1,0:T(8,128)S(1)} %shard_map.65), channel_id=1, source_target_pairs={{0,4},{1,2},{2,1},{3,7},{4,0},{5,6},{6,5},{7,3},{8,12},{9,10},{10,... | collective-permute-start | bytes 626696 | tf_op jit(solution)/shard_map/ppermute | solution.py:577
  23.2 0.0 copy-done.2
  23.2 0.0 copy-done.1
  23.2 0.0 copy-start.3
  23.2 0.0 copy-start.4
  23.2 1.8 %shard_map.67 = (f32[2,512,512]{2,1,0:T(8,128)S(1)}, f32[512,512]{1,0:T(8,128)S(1)}) custom-call(f32[8,128]{1,0:T(8,128)S(1)} %get-tuple-element.23.mine, f32[2,512,512]{2,1,0:T(8,128)S(1)} %copy-done.1, s32[512,512]{1,0:T(8,128)S(1)} %bitcast.1), custom_call_target="tpu_custom_call" | custom-call | flops 5000000000 | tf_op jit(solution)/shard_map/pallas_call | solution.py:30
  25.0 0.0 copy-done.3
  25.0 0.0 copy-done.4
  25.0 1.2 %shard_map.68.zown = f32[4,320,256]{2,1,0:T(8,128)S(1)} custom-call(f32[8,128]{1,0:T(8,128)S(1)} %get-tuple-element.23.mine, f32[2,320,320]{2,1,0:T(8,128)S(1)} %copy-done, f32[648,128]{1,0:T(8,128)S(1)} %collective-permute-done.2.side.xside, f32[648,128]{1,0:T(8,128)S(1)} %collective-permute-done.4.side.dside, f32[2,512,512]{2,1,0:T(8,128)S(1)} %get-tuple-element.28.rolled, ...), custom_call_target="tpu_custom_call" | custom-call | flops 2000000000 | tf_op jit(solution)/shard_map/pallas_call | solution.py:30
  26.2 0.0 collective-permute-done.5.dcorner
  26.2 0.8 %collective-permute-done.3.xcorner = f32[408,128]{1,0:T(8,128)S(1)} collective-permute-done((f32[408,128]{1,0:T(8,128)S(1)}, f32[408,128]{1,0:T(8,128)S(1)}, u32[]{:S(2)}, u32[]{:S(2)}) %collective-permute-start.3) | collective-permute-done | bytes 208928 | tf_op jit(solution)/shard_map/ppermute | solution.py:577
  27.0 4.0 %main.1 = (bf16[4,320,256]{2,1,0:T(8,128)(2,1)S(1)}, bf16[4,320,256]{2,1,0:T(8,128)(2,1)S(1)}, f32[2,128,384]{2,1,0:T(8,128)S(1)}, f32[2,128,384]{2,1,0:T(8,128)...) custom-call(f32[8,128]{1,0:T(8,128)S(1)} %get-tuple-element.23.mine, ...), custom_call_target="tpu_custom_call" | custom-call | flops 5000000000 | tf_op jit(solution)/shard_map/main/pallas_call | solution.py:638
  30.9 2.1 %collective-permute-start.8 = (f32[2,192,128]{2,1,0:T(8,128)S(1)}, f32[2,192,128]{2,1,0:T(8,128)S(1)}, u32[]{:S(2)}, u32[]{:S(2)}) collective-permute-start(f32[2,192,128]{2,1,0:T(8,128)S(1)} %get-tuple-element.37), channel_id=1, source_target_pairs={{0,4},{1,2},{2,1},{3,7},{4,0},{5,6},{6,5},{7,3},{8,12},{9,10},{10,... | collective-permute-start | bytes 589832 | tf_op jit(solution)/shard_map/ppermute | solution.py:577
  33.0 0.0 collective-permute-start.9
  33.0 1.0 %shard_map.69 = (f32[2,320,320]{2,1,0:T(8,128)S(1)}, f32[2,320,128]{2,1,0:T(8,128)S(1)}, f32[2,320,128]{2,1,0:T(8,128)S(1)}) custom-call(f32[8,128]{1,0:T(8,128)S(1)} %get-tuple-element.23.mine, bf16[4,320,256]{2,1,0:T(8,128)(2,1)S(1)} %get-tuple-element.30.hi, bf16[4,320,256]{2,1,0:T(8,128)(2,1)S(1)} %get-tuple-element.31.lo, ...), custom_call_target="tpu_custom_call" | custom-call | flops 2000000000 | tf_op jit(solution)/shard_map/pallas_call | solution.py:30
  34.0 0.7 %collective-permute-start.6 = (f32[2,320,128]{2,1,0:T(8,128)S(1)}, f32[2,320,128]{2,1,0:T(8,128)S(1)}, u32[]{:S(2)}, u32[]{:S(2)}) collective-permute-start(f32[2,320,128]{2,1,0:T(8,128)S(1)} %get-tuple-element.33), channel_id=1, source_target_pairs={{0,0},{1,2},{2,1},{3,3},{4,4},{5,6},{6,5},{7,7},{8,8},{9,10},{10,9... | collective-permute-start | bytes 983048 | tf_op jit(solution)/shard_map/ppermute | solution.py:577
  34.7 2.2 %collective-permute-start.7 = (f32[2,320,128]{2,1,0:T(8,128)S(1)}, f32[2,320,128]{2,1,0:T(8,128)S(1)}, u32[]{:S(2)}, u32[]{:S(2)}) collective-permute-start(f32[2,320,128]{2,1,0:T(8,128)S(1)} %get-tuple-element.34), channel_id=1, source_target_pairs={{0,1},{1,0},{2,3},{3,2},{4,5},{5,4},{6,7},{7,6},{8,9},{9,8},{10,11... | collective-permute-start | bytes 983048 | tf_op jit(solution)/shard_map/ppermute | solution.py:577
  36.9 0.0 collective-permute-done.8.xcorn
  36.9 0.0 collective-permute-done.9.dcorn
  36.9 0.1 shard_map.71
  37.0 1.9 %collective-permute-start.10 = (f32[640,128]{1,0:T(8,128)S(1)}, f32[640,128]{1,0:T(8,128)S(1)}, u32[]{:S(2)}, u32[]{:S(2)}) collective-permute-start(f32[640,128]{1,0:T(8,128)S(1)} %get-tuple-element.39), channel_id=1, source_target_pairs={{0,4},{1,5},{2,6},{3,7},{4,0},{5,1},{6,2},{7,3},{8,12},{9,13},{10,... | collective-permute-start | bytes 983048 | tf_op jit(solution)/shard_map/ppermute | solution.py:577
  38.9 0.0 collective-permute-start.11
  38.9 2.6 %shard_map.70.weight = f32[320,320]{1,0:T(8,128)S(1)} custom-call(f32[8,128]{1,0:T(8,128)S(1)} %get-tuple-element.23.mine, f32[408,128]{1,0:T(8,128)S(1)} %collective-permute-done.3.xcorner, f32[408,128]{1,0:T(8,128)S(1)} %collective-permute-done.5.dcorner, f32[648,128]{1,0:T(8,128)S(1)} %collective-permute-done.inner, ...), custom_call_target="tpu_custom_call" | custom-call | flops 10000000000 | tf_op jit(solution)/shard_map/pallas_call | solution.py:30
  41.5 0.0 collective-permute-done.6.xedge
  41.5 0.0 collective-permute-done.7.dedge
  41.5 11.4 %collective-permute-done.10.inner = f32[640,128]{1,0:T(8,128)S(1)} collective-permute-done((f32[640,128]{1,0:T(8,128)S(1)}, f32[640,128]{1,0:T(8,128)S(1)}, u32[]{:S(2)}, u32[]{:S(2)}) %collective-permute-start.10) | collective-permute-done | bytes 327712 | tf_op jit(solution)/shard_map/ppermute | solution.py:577
  52.9 0.0 collective-permute-done.11.cross
  52.9 1.2 %shard_map.72 = f32[2,320,320]{2,1,0:T(8,128)} custom-call(f32[2,320,320]{2,1,0:T(8,128)S(1)} %copy-done, f32[2,320,320]{2,1,0:T(8,128)S(1)} %get-tuple-element.32.own, f32[320,320]{1,0:T(8,128)S(1)} %shard_map.70.weight, f32[2,320,128]{2,1,0:T(8,128)S(1)} %collective-permute-done.6.xedge, f32[2,320,128]{2,1,0:T(8,128)S(1)} %collective-permute-done.7.dedge, ...), custom_call_target="tpu_custom_call" | custom-call | tf_op jit(solution)/shard_map/pallas_call | solution.py:30
Async XLA Ops:
  0.0 1.4 %copy-start = (f32[2,320,320]{2,1,0:T(8,128)S(1)}, f32[2,320,320]{2,1,0:T(8,128)}, u32[]{:S(2)}) copy-start(f32[2,320,320]{2,1,0:T(8,128)} %obj.7) | copy-start | bytes 2457604
  1.4 21.8 %copy-start.2 = (s32[1,1,1,512,512]{4,3,2,1,0:T(8,128)S(1)}, s32[1,1,1,512,512]{4,3,2,1,0:T(8,128)}, u32[]{:S(2)}) copy-start(s32[1,1,1,512,512]{4,3,2,1,0:T(8,128)} %param.9) | copy-start | bytes 3145732
  2.1 21.1 %copy-start.1 = (f32[2,512,512]{2,1,0:T(8,128)S(1)}, f32[2,512,512]{2,1,0:T(8,128)}, u32[]{:S(2)}) copy-start(f32[2,512,512]{2,1,0:T(8,128)} %probe.3) | copy-start | bytes 6291460
  2.1 4.0 %collective-permute-start.4 = (f32[648,128]{1,0:T(8,128)S(1)}, f32[648,128]{1,0:T(8,128)S(1)}, u32[]{:S(2)}, u32[]{:S(2)}) collective-permute-start(f32[648,128]{1,0:T(8,128)S(1)} %get-tuple-element.27), channel_id=1, source_target_pairs={{0,1},{1,0},{2,3},{3,2},{4,5},{5,4},{6,7},{7,6},{8,9},{9,8},{10,11... | collective-permute-start | bytes 995336 | tf_op jit(solution)/shard_map/ppermute | solution.py:577
  2.7 17.3 %collective-permute-start = (f32[648,128]{1,0:T(8,128)S(1)}, f32[648,128]{1,0:T(8,128)S(1)}, u32[]{:S(2)}, u32[]{:S(2)}) collective-permute-start(f32[648,128]{1,0:T(8,128)S(1)} %get-tuple-element.24), channel_id=1, source_target_pairs={{0,4},{1,5},{2,6},{3,7},{4,0},{5,1},{6,2},{7,3},{8,12},{9,13},{10,... | collective-permute-start | bytes 995336 | tf_op jit(solution)/shard_map/ppermute | solution.py:577
  5.3 14.8 %collective-permute-start.1 = (f32[648,128]{1,0:T(8,128)S(1)}, f32[648,128]{1,0:T(8,128)S(1)}, u32[]{:S(2)}, u32[]{:S(2)}) collective-permute-start(f32[648,128]{1,0:T(8,128)S(1)} %get-tuple-element.25), channel_id=1, source_target_pairs={{0,1},{1,0},{2,3},{3,2},{4,8},{5,9},{6,10},{7,11},{8,4},{9,5},{10,... | collective-permute-start | bytes 995336 | tf_op jit(solution)/shard_map/ppermute | solution.py:577
  5.4 15.0 %collective-permute-start.2 = (f32[648,128]{1,0:T(8,128)S(1)}, f32[648,128]{1,0:T(8,128)S(1)}, u32[]{:S(2)}, u32[]{:S(2)}) collective-permute-start(f32[648,128]{1,0:T(8,128)S(1)} %get-tuple-element.26), channel_id=1, source_target_pairs={{0,0},{1,2},{2,1},{3,3},{4,4},{5,6},{6,5},{7,7},{8,8},{9,10},{10,9... | collective-permute-start | bytes 995336 | tf_op jit(solution)/shard_map/ppermute | solution.py:577
  20.3 5.9 %collective-permute-start.5 = (f32[408,128]{1,0:T(8,128)S(1)}, f32[408,128]{1,0:T(8,128)S(1)}, u32[]{:S(2)}, u32[]{:S(2)}) collective-permute-start(f32[408,128]{1,0:T(8,128)S(1)} %shard_map.66), channel_id=1, source_target_pairs={{0,1},{1,0},{2,3},{3,2},{4,5},{5,4},{6,7},{7,6},{8,9},{9,8},{10,11... | collective-permute-start | bytes 626696 | tf_op jit(solution)/shard_map/ppermute | solution.py:577
  20.7 6.3 %collective-permute-start.3 = (f32[408,128]{1,0:T(8,128)S(1)}, f32[408,128]{1,0:T(8,128)S(1)}, u32[]{:S(2)}, u32[]{:S(2)}) collective-permute-start(f32[408,128]{1,0:T(8,128)S(1)} %shard_map.65), channel_id=1, source_target_pairs={{0,4},{1,2},{2,1},{3,7},{4,0},{5,6},{6,5},{7,3},{8,12},{9,10},{10,... | collective-permute-start | bytes 626696 | tf_op jit(solution)/shard_map/ppermute | solution.py:577
  23.2 1.8 %copy-start.3 = (bf16[8,256,256]{2,1,0:T(8,128)(2,1)S(1)}, bf16[8,256,256]{2,1,0:T(8,128)(2,1)}, u32[]{:S(2)}) copy-start(bf16[8,256,256]{2,1,0:T(8,128)(2,1)} %constant.4.clone.high) | copy-start | bytes 3145732
  23.2 1.8 %copy-start.4 = (bf16[8,256,256]{2,1,0:T(8,128)(2,1)S(1)}, bf16[8,256,256]{2,1,0:T(8,128)(2,1)}, u32[]{:S(2)}) copy-start(bf16[8,256,256]{2,1,0:T(8,128)(2,1)} %constant.5.clone.low) | copy-start | bytes 3145732
  30.9 5.9 %collective-permute-start.8 = (f32[2,192,128]{2,1,0:T(8,128)S(1)}, f32[2,192,128]{2,1,0:T(8,128)S(1)}, u32[]{:S(2)}, u32[]{:S(2)}) collective-permute-start(f32[2,192,128]{2,1,0:T(8,128)S(1)} %get-tuple-element.37), channel_id=1, source_target_pairs={{0,4},{1,2},{2,1},{3,7},{4,0},{5,6},{6,5},{7,3},{8,12},{9,10},{10,... | collective-permute-start | bytes 589832 | tf_op jit(solution)/shard_map/ppermute | solution.py:577
  33.0 3.8 %collective-permute-start.9 = (f32[2,192,128]{2,1,0:T(8,128)S(1)}, f32[2,192,128]{2,1,0:T(8,128)S(1)}, u32[]{:S(2)}, u32[]{:S(2)}) collective-permute-start(f32[2,192,128]{2,1,0:T(8,128)S(1)} %get-tuple-element.38), channel_id=1, source_target_pairs={{0,1},{1,0},{2,3},{3,2},{4,5},{5,4},{6,7},{7,6},{8,9},{9,8},{10,11... | collective-permute-start | bytes 589832 | tf_op jit(solution)/shard_map/ppermute | solution.py:577
  34.0 7.5 %collective-permute-start.6 = (f32[2,320,128]{2,1,0:T(8,128)S(1)}, f32[2,320,128]{2,1,0:T(8,128)S(1)}, u32[]{:S(2)}, u32[]{:S(2)}) collective-permute-start(f32[2,320,128]{2,1,0:T(8,128)S(1)} %get-tuple-element.33), channel_id=1, source_target_pairs={{0,0},{1,2},{2,1},{3,3},{4,4},{5,6},{6,5},{7,7},{8,8},{9,10},{10,9... | collective-permute-start | bytes 983048 | tf_op jit(solution)/shard_map/ppermute | solution.py:577
  34.7 6.8 %collective-permute-start.7 = (f32[2,320,128]{2,1,0:T(8,128)S(1)}, f32[2,320,128]{2,1,0:T(8,128)S(1)}, u32[]{:S(2)}, u32[]{:S(2)}) collective-permute-start(f32[2,320,128]{2,1,0:T(8,128)S(1)} %get-tuple-element.34), channel_id=1, source_target_pairs={{0,1},{1,0},{2,3},{3,2},{4,5},{5,4},{6,7},{7,6},{8,9},{9,8},{10,11... | collective-permute-start | bytes 983048 | tf_op jit(solution)/shard_map/ppermute | solution.py:577
  37.0 15.9 %collective-permute-start.10 = (f32[640,128]{1,0:T(8,128)S(1)}, f32[640,128]{1,0:T(8,128)S(1)}, u32[]{:S(2)}, u32[]{:S(2)}) collective-permute-start(f32[640,128]{1,0:T(8,128)S(1)} %get-tuple-element.39), channel_id=1, source_target_pairs={{0,4},{1,5},{2,6},{3,7},{4,0},{5,1},{6,2},{7,3},{8,12},{9,13},{10,... | collective-permute-start | bytes 983048 | tf_op jit(solution)/shard_map/ppermute | solution.py:577
  38.9 14.0 %collective-permute-start.11 = (f32[640,128]{1,0:T(8,128)S(1)}, f32[640,128]{1,0:T(8,128)S(1)}, u32[]{:S(2)}, u32[]{:S(2)}) collective-permute-start(f32[640,128]{1,0:T(8,128)S(1)} %get-tuple-element.40), channel_id=1, source_target_pairs={{0,1},{1,0},{2,3},{3,2},{4,8},{5,9},{6,10},{7,11},{8,4},{9,5},{10,... | collective-permute-start | bytes 983048 | tf_op jit(solution)/shard_map/ppermute | solution.py:577

commit v6 on v5

--- a/solution.py
+++ b/solution.py
@@ -33,7 +33,9 @@
             jax.ShapeDtypeStruct(s, F32) if hbm_out else pltpu.VMEM(s, F32) for s in out_shapes
         ],
         in_specs=specs,
-        out_specs=[pl.BlockSpec(memory_space=pltpu.VMEM) for _ in out_shapes],
+        out_specs=[
+            pl.BlockSpec(memory_space=pltpu.HBM if hbm_out else pltpu.VMEM) for _ in out_shapes
+        ],
         scratch_shapes=list(scratch),
         compiler_params=pltpu.CompilerParams(vmem_limit_bytes=limit * 1024 * 1024),
         cost_estimate=pl.CostEstimate(flops=flops, bytes_accessed=0, transcendentals=0)
@@ -119,28 +121,29 @@
     return jnp.sum(jnp.where(picked, tile, 0.0))
 
 
-def row_kernel(offs, obj, inner, cross, mine, held, numbers, sems):
+def row_kernel(first, source, obj, *refs):
     rows, cols = obj.shape[1:]
-    far = odd("row")
-    bases = jnp.where(far, 0, rows - OVL), jnp.where(far, rows - OVL, 0)
-    copies = [pltpu.make_async_copy(offs, numbers, sems.at[2])]
-    for t, base in enumerate(bases):
-        part = obj.at[:, pl.ds(pl.multiple_of(base, 8), OVL), :]
-        copies.append(pltpu.make_async_copy(part, held.at[t], sems.at[t]))
-    for copy in (copies[1], copies[0], copies[2]):
-        copy.start()
+    upward = odd("row") if first == 0 else ~odd("row")
+    base = pl.multiple_of(jnp.where(upward, 0, rows - OVL), 8)
+    out, *mine, held, numbers, sems = refs
+    copies = [pltpu.make_async_copy(obj.at[:, pl.ds(base, OVL), :], held, sems.at[0])]
+    copies[0].start()
+    if first == 0:
+        copies.append(pltpu.make_async_copy(source, numbers, sems.at[1]))
+        copies[1].start()
+        copies[1].wait()
+        info = offsets_tile(numbers[0, 0, 0, 0], numbers[0, 0, 0, 1])
+        mine[0][...] = info
+    else:
+        info = source[...]
+    out[5 * OVL : 5 * OVL + 8, :] = paired("row", info, first)
     copies[0].wait()
-    info = offsets_tile(numbers[0, 0, 0, 0], numbers[0, 0, 0, 1])
-    mine[...] = info
-    for t, out in enumerate((inner, cross)):
-        out[5 * OVL : 5 * OVL + 8, :] = paired("row", info, t)
-        copies[1 + t].wait()
-        for c in range(2):
-            for k in range(2):
-                at = (2 * c + k) * OVL
-                out[at : at + OVL, :] = paired("row", held[t, c, :, 128 * k : 128 * k + 128], t)
-            tail = paired("row", held[t, c, :, 256:cols], t)
-            out[4 * OVL : 5 * OVL, c * HALF : c * HALF + HALF] = tail
+    for c in range(2):
+        for k in range(2):
+            at = (2 * c + k) * OVL
+            out[at : at + OVL, :] = paired("row", held[c, :, 128 * k : 128 * k + 128], first)
+        tail = paired("row", held[c, :, 256:cols], first)
+        out[4 * OVL : 5 * OVL, c * HALF : c * HALF + HALF] = tail
 
 
 def side_kernel(mine, obj, xside, dside):
@@ -291,7 +294,7 @@
 
 def main_kernel(
     mine, inner, cross, xcorner, dcorner, rolled, measured, zown, high, low,
-    own_hi, own_lo, nblock, sblock, xcorn, dcorn, ah, al, bh, bl, zh, tf,
+    own_hi, own_lo, zback, xcorn, dcorn, ah, al, bh, bl, zh, tf,
 ):
     size = rolled.shape[-1]
     quarter = size // 4
@@ -356,6 +359,7 @@
                 for k, (yr, yi) in enumerate(mix_forward(quads)):
                     keep(bh, bl, (half, k, slice(r, r + STEP), cols), yr)
                     keep(bh, bl, (half, k, slice(quarter + r, quarter + r + STEP), cols), yi)
+    for half in range(2):
         for k in range(4):
             z = left_product(bh, bl, (half, k), high, low, 4 + k)
             zr, zi = z[re], z[im]
@@ -363,8 +367,11 @@
             factor = 1.0 - m * lax.rsqrt(zr * zr + zi * zi + EPSILON)
             keep(bh, bl, (half, k, re), factor * zr)
             keep(bh, bl, (half, k, im), factor * zi)
+    for half in range(2):
         for k in range(4):
             tf[half, k] = left_product(bh, bl, (half, k), high, low, k)
+    for half in range(2):
+        pair = (2 * half, 2 * half + 1)
         for t, p in enumerate(pair):
             cols = slice(t * quarter, (t + 1) * quarter)
             for r in range(0, quarter, STEP):
@@ -377,29 +384,15 @@
                     keep(hi, lo, (p, rows, im), yi)
 
     for p in range(4):
-        zh[p] = right_product(ah, al, slice(0, count), p, high, low, 4 + p)
+        zback[p] = right_product(ah, al, slice(0, count), p, high, low, 4 + p)
     for base, slot in zip(range(0, count, STEP), slots):
         at, rows = slice(base, base + STEP), slice(slot, slot + STEP)
-        row = step_row + slot
-        sends = []
-        if slot < OVL:
-            sends.append((0, slot, row >= u if slot < HALF else None))
-        if slot < HALF:
-            sends.append((1, slot + HALF, row < u))
-        if slot >= OVL:
-            sends.append((1, slot - OVL - cells, None))
-        for c, (g, xout, dout) in enumerate(leave(zh, at, rolled, rows, v, right)):
+        for c, (_, xout, dout) in enumerate(leave(zback, at, rolled, rows, v, right)):
             xcorn[c, at, :] = xout
             dcorn[c, at, :] = dout
-            for part, o, mask in sends:
-                to = slice(o, o + STEP)
-                put = (lambda x: x) if mask is None else (lambda x: jnp.where(mask, x, 0.0))
-                block = (nblock, sblock)[part]
-                for t in range(3):
-                    block[c, to, 128 * t : 128 * t + 128] = put(g[t])
-
-
-def after_kernel(mine, hi, lo, rolled, high, low, own, xedge, dedge, z):
+
+
+def after_kernel(mine, hi, lo, zback, rolled, high, low, own, xedge, dedge, nblock, sblock, z):
     cells = own.shape[1]
     v = mine[1:2, :]
     right = odd("col")
@@ -415,6 +408,23 @@
                 own[c, at, 256:cells] = g[2][:, : cells - 256]
                 xedge[c, at, :] = xout
                 dedge[c, at, :] = dout
+    u = mine[0:1, :]
+    for base in range(0, zback.shape[1], STEP):
+        slot = base if base < OVL else base + cells
+        row = row_iota((STEP, LANES)).astype(F32) + slot
+        sends = []
+        if slot < OVL:
+            sends.append((nblock, slot, row >= u if slot < HALF else None))
+        if slot < HALF:
+            sends.append((sblock, slot + HALF, row < u))
+        if slot >= OVL:
+            sends.append((sblock, slot - OVL - cells, None))
+        at, rows = slice(base, base + STEP), slice(slot, slot + STEP)
+        for c, (g, _, _) in enumerate(leave(zback, at, rolled, rows, v, right)):
+            for block, o, mask in sends:
+                for t, x in enumerate(g):
+                    put = x if mask is None else jnp.where(mask, x, 0.0)
+                    block[c, o : o + STEP, 128 * t : 128 * t + 128] = put
 
 
 def send_kernel(nblock, sblock, xcorn, dcorn, xcorner, dcorner, inner, cross):
@@ -513,11 +523,12 @@
         weight[rows, :] = STEP_SIZE / (acc[rows, 0:cells] + REGULAR)
 
 
-def final_kernel(obj, own, weight, xedge, dedge, inner, cross, updated):
+def final_kernel(obj, own, weight, xedge, dedge, inner, cross, updated, held, sems):
     cells = obj.shape[1]
     right = odd("col")
     far = odd("row")
     first = lane_iota((HALF, LANES)) < HALF
+    copies = []
     for r in range(0, cells, HALF):
         rows = slice(r, r + HALF)
         for c in range(2):
@@ -545,7 +556,12 @@
                 g[2] = g[2] + take(4, slice(c * HALF, c * HALF + HALF))
             for t, x in enumerate(g):
                 cols = slice(128 * t, min(128 * t + 128, cells))
-                updated[c, rows, cols] = obj[c, rows, cols] - x * weight[rows, cols]
+                held[c, rows, cols] = obj[c, rows, cols] - x * weight[rows, cols]
+        part = (slice(None), rows, slice(None))
+        copies.append(pltpu.make_async_copy(held.at[part], updated.at[part], sems.at[r // HALF]))
+        copies[-1].start()
+    for copy in copies:
+        copy.wait()
 
 
 def swap(count, first):
@@ -584,21 +600,29 @@
     table_high, table_low = tables(size)
     high, low = jnp.asarray(table_high), jnp.asarray(table_low)
 
-    to_inner, to_cross, mine = pl.pallas_call(
-        row_kernel,
-        name="rows",
-        out_shape=[pltpu.VMEM((n, LANES), F32) for n in (5 * OVL + 8, 5 * OVL + 8, 8)],
-        in_specs=[pl.BlockSpec(memory_space=pltpu.HBM) for _ in range(2)],
-        out_specs=[pl.BlockSpec(memory_space=pltpu.VMEM) for _ in range(3)],
-        scratch_shapes=[
-            pltpu.VMEM((2, 2, OVL, cells), F32),
-            pltpu.SMEM((1, 1, 1, 2), jnp.int32),
-            pltpu.SemaphoreType.DMA((3,)),
-        ],
-        compiler_params=pltpu.CompilerParams(vmem_limit_bytes=8 * 1024 * 1024),
-        cost_estimate=pl.CostEstimate(flops=5_000_000_000, bytes_accessed=0, transcendentals=0),
-    )(*[pltpu.with_memory_space_constraint(x, pltpu.HBM) for x in (offsets, object_slab)])
+    def rows_for(first, source, space):
+        shapes = [(5 * OVL + 8, LANES)] + [(8, LANES)] * (first == 0)
+        step = pl.pallas_call(
+            functools.partial(row_kernel, first),
+            out_shape=[pltpu.VMEM(n, F32) for n in shapes],
+            in_specs=[pl.BlockSpec(memory_space=space), pl.BlockSpec(memory_space=pltpu.HBM)],
+            out_specs=[pl.BlockSpec(memory_space=pltpu.VMEM) for _ in shapes],
+            scratch_shapes=[
+                pltpu.VMEM((2, OVL, cells), F32),
+                pltpu.SMEM((1, 1, 1, 2), jnp.int32),
+                pltpu.SemaphoreType.DMA((2,)),
+            ],
+            compiler_params=pltpu.CompilerParams(vmem_limit_bytes=8 * 1024 * 1024),
+            cost_estimate=pl.CostEstimate(flops=2_500_000_000, bytes_accessed=0, transcendentals=0),
+        )
+        return step(
+            pltpu.with_memory_space_constraint(source, space),
+            pltpu.with_memory_space_constraint(object_slab, pltpu.HBM),
+        )
+
+    to_inner, mine = rows_for(0, offsets, pltpu.HBM)
     halo_inner = permute(to_inner, row_inner)
+    (to_cross,) = rows_for(1, mine, pltpu.VMEM)
     halo_cross = permute(to_cross, row_cross)
     xside, dside = call(side_kernel, [(2 * cells + 8, OVL)] * 2, [mine, object_slab], flops=5_000_000_000)
     side_x = permute(xside, col_cross)
@@ -629,13 +653,12 @@
     shapes = [
         ((4, cells, half), BF16),
         ((4, cells, half), BF16),
-        ((2, OVL, 384), F32),
-        ((2, OVL, 384), F32),
+        ((4, count, half), F32),
         ((2, count, OVL), F32),
         ((2, count, OVL), F32),
     ]
     operands = [mine, halo_inner, halo_cross, corner_x, corner_d, rolled, measured, zown, high, low]
-    own_hi, own_lo, nblock, sblock, xcorn, dcorn = pl.pallas_call(
+    own_hi, own_lo, zback, xcorn, dcorn = pl.pallas_call(
         main_kernel,
         name="main",
         out_shape=[pltpu.VMEM(s, d) for s, d in shapes],
@@ -654,10 +677,10 @@
     )(*[pltpu.with_memory_space_constraint(x, pltpu.VMEM) for x in operands])
     fix_x = permute(xcorn, col_full)
     fix_d = permute(dcorn, col_inner)
-    own, xedge, dedge = call(
+    own, xedge, dedge, nblock, sblock = call(
         after_kernel,
-        [(2, cells, cells), (2, cells, OVL), (2, cells, OVL)],
-        [mine, own_hi, own_lo, rolled, high, low],
+        [(2, cells, cells)] + [(2, cells, OVL)] * 2 + [(2, OVL, 384)] * 2,
+        [mine, own_hi, own_lo, zback, rolled, high, low],
         scratch=[pltpu.VMEM((4, cells, half), F32)],
         flops=2_000_000_000,
     )
@@ -678,6 +701,10 @@
         [(2, cells, cells)],
         [object_slab, own, weight, edge_x, edge_d, grad_inner, grad_cross],
         hbm_out=True,
+        scratch=[
+            pltpu.VMEM((2, cells, cells), F32),
+            pltpu.SemaphoreType.DMA((cells // HALF,)),
+        ],
     )
     return updated
 

time: 54.3 us -> 56.1 us (1.033)
  starting transfers between devices: 13.4 us -> 14.8 us
  Pallas kernels: 14.3 us -> 15.1 us
    ppermute x12, starting transfers between devices: 13.4 us -> 14.8 us  [permute(): return lax.ppermute(x, ('row', 'col'), pairs)]
    pallas_call x1 -> x2, Pallas kernels: 1.32 us -> 2.4 us  [rows_for(): step(pltpu.with_memory_space_constraint(source, space), pltpu.with_memory...]
  transfers between devices with their start and end apart: 12 -> 12, of which waited for: 3 -> 3; matrix products, arithmetic and copies ran while one was open for 0% -> 0% of each run, Pallas kernels for 13% -> 15%
where the time goes in v6:
time: 56.1 us; the launch traced here: 55.9 us
  waiting for transfers between devices  25.7 us (46%)
  Pallas kernels  15.1 us (27%)
  starting transfers between devices  14.8 us (26%)
    ppermute x12, waiting for transfers between devices, permute(): return lax.ppermute(x, ('row', 'col'), pairs)  25.7 us
    ppermute x12, starting transfers between devices, permute(): return lax.ppermute(x, ('row', 'col'), pairs)  14.8 us
    pallas_call x9, Pallas kernels, call(): pl.pallas_call(kernel, out_shape=[jax.ShapeDtypeStruct(s, F32) if hbm_out...  8.96 us
    pallas_call x1, Pallas kernels, local(): pl.pallas_call(main_kernel, name='main', out_shape=[pltpu.VMEM(s, d) for...  3.78 us
    pallas_call x2, Pallas kernels, rows_for(): step(pltpu.with_memory_space_constraint(source, space), pltpu.with_memory...  2.4 us
  transfers between devices with their start and end apart: 12, of which 3 were waited for; matrix products, arithmetic and copies ran while one was open for 0% of the time, Pallas kernels for 15%

profile of v6, /device:TPU:0, one launch (start us, length us, event | category | flops | bytes accessed | tf_op | source)
XLA Modules:
  0.0 55.9 jit_solution(14664008402881489514)
XLA Ops:
  0.0 0.0 copy-start
  0.0 1.2 %shard_map.64 = (f32[648,128]{1,0:T(8,128)S(1)}, f32[8,128]{1,0:T(8,128)S(1)}) custom-call(s32[1,1,1,2]{3,2,1,0:T(1,128)} %source.1, f32[2,320,320]{2,1,0:T(8,128)} %obj.9), custom_call_target="tpu_custom_call" | custom-call | flops 2500000000 | tf_op jit(solution)/shard_map/pallas_call | solution.py:618
  1.2 0.1 copy-done
  1.3 0.7 %shard_map.66 = (f32[648,128]{1,0:T(8,128)S(1)}, f32[648,128]{1,0:T(8,128)S(1)}) custom-call(f32[8,128]{1,0:T(8,128)S(1)} %get-tuple-element.23.source.mine, f32[2,320,320]{2,1,0:T(8,128)S(1)} %copy-done), custom_call_target="tpu_custom_call" | custom-call | flops 5000000000 | tf_op jit(solution)/shard_map/pallas_call | solution.py:30
  2.0 0.6 collective-permute-start.4
  2.6 0.0 copy-start.3
  2.6 1.2 %shard_map.65 = f32[648,128]{1,0:T(8,128)S(1)} custom-call(f32[8,128]{1,0:T(8,128)S(1)} %get-tuple-element.23.source.mine, f32[2,320,320]{2,1,0:T(8,128)} %obj.9), custom_call_target="tpu_custom_call" | custom-call | flops 2500000000 | tf_op jit(solution)/shard_map/pallas_call | solution.py:618
  3.8 0.0 copy-start.2
  3.8 0.1 collective-permute-start.1
  3.9 4.0 %collective-permute-start = (f32[648,128]{1,0:T(8,128)S(1)}, f32[648,128]{1,0:T(8,128)S(1)}, u32[]{:S(2)}, u32[]{:S(2)}) collective-permute-start(f32[648,128]{1,0:T(8,128)S(1)} %get-tuple-element.24), channel_id=1, source_target_pairs={{0,4},{1,5},{2,6},{3,7},{4,0},{5,1},{6,2},{7,3},{8,12},{9,13},{10,... | collective-permute-start | bytes 995336 | tf_op jit(solution)/shard_map/ppermute | solution.py:593
  7.9 0.7 %collective-permute-start.2 = (f32[648,128]{1,0:T(8,128)S(1)}, f32[648,128]{1,0:T(8,128)S(1)}, u32[]{:S(2)}, u32[]{:S(2)}) collective-permute-start(f32[648,128]{1,0:T(8,128)S(1)} %get-tuple-element.25), channel_id=1, source_target_pairs={{0,0},{1,2},{2,1},{3,3},{4,4},{5,6},{6,5},{7,7},{8,8},{9,10},{10,9... | collective-permute-start | bytes 995336 | tf_op jit(solution)/shard_map/ppermute | solution.py:593
  8.6 0.0 collective-permute-done.4.side.dside
  8.6 0.0 collective-permute-done.1.cross
  8.6 13.5 %collective-permute-done.inner = f32[648,128]{1,0:T(8,128)S(1)} collective-permute-done((f32[648,128]{1,0:T(8,128)S(1)}, f32[648,128]{1,0:T(8,128)S(1)}, u32[]{:S(2)}, u32[]{:S(2)}) %collective-permute-start) | collective-permute-done | bytes 331808 | tf_op jit(solution)/shard_map/ppermute | solution.py:593
  22.1 0.3 shard_map.68
  22.4 0.1 collective-permute-start.5
  22.5 0.0 collective-permute-done.2.side.xside
  22.5 0.3 shard_map.67
  22.7 2.5 %collective-permute-start.3 = (f32[408,128]{1,0:T(8,128)S(1)}, f32[408,128]{1,0:T(8,128)S(1)}, u32[]{:S(2)}, u32[]{:S(2)}) collective-permute-start(f32[408,128]{1,0:T(8,128)S(1)} %shard_map.67), channel_id=1, source_target_pairs={{0,4},{1,2},{2,1},{3,7},{4,0},{5,6},{6,5},{7,3},{8,12},{9,10},{10,... | collective-permute-start | bytes 626696 | tf_op jit(solution)/shard_map/ppermute | solution.py:593
  25.3 0.0 copy-done.3
  25.3 0.0 copy-done.2
  25.3 0.0 copy-start.1
  25.3 0.0 copy-start.4
  25.3 0.0 copy-start.5
  25.3 1.8 %shard_map.69 = (f32[2,512,512]{2,1,0:T(8,128)S(1)}, f32[512,512]{1,0:T(8,128)S(1)}) custom-call(f32[8,128]{1,0:T(8,128)S(1)} %get-tuple-element.23.source.mine, f32[2,512,512]{2,1,0:T(8,128)S(1)} %copy-done.2, s32[512,512]{1,0:T(8,128)S(1)} %bitcast.1), custom_call_target="tpu_custom_call" | custom-call | flops 5000000000 | tf_op jit(solution)/shard_map/pallas_call | solution.py:30
  27.1 0.0 copy-done.1
  27.1 0.0 copy-done.4
  27.1 0.0 copy-done.5
  27.1 1.2 %shard_map.70.zown = f32[4,320,256]{2,1,0:T(8,128)S(1)} custom-call(f32[8,128]{1,0:T(8,128)S(1)} %get-tuple-element.23.source.mine, f32[2,320,320]{2,1,0:T(8,128)S(1)} %copy-done.1, f32[648,128]{1,0:T(8,128)S(1)} %collective-permute-done.2.side.xside, f32[648,128]{1,0:T(8,128)S(1)} %collective-permute-done.4.side.dside, ...), custom_call_target="tpu_custom_call" | custom-call | flops 2000000000 | tf_op jit(solution)/shard_map/pallas_call | solution.py:30
  28.3 0.0 collective-permute-done.5.dcorner
  28.3 0.7 %collective-permute-done.3.xcorner = f32[408,128]{1,0:T(8,128)S(1)} collective-permute-done((f32[408,128]{1,0:T(8,128)S(1)}, f32[408,128]{1,0:T(8,128)S(1)}, u32[]{:S(2)}, u32[]{:S(2)}) %collective-permute-start.3) | collective-permute-done | bytes 208928 | tf_op jit(solution)/shard_map/ppermute | solution.py:593
  29.1 3.8 %main.1 = (bf16[4,320,256]{2,1,0:T(8,128)(2,1)S(1)}, bf16[4,320,256]{2,1,0:T(8,128)(2,1)S(1)}, f32[4,192,256]{2,1,0:T(8,128)S(1)}, f32[2,192,128]{2,1,0:T(8,128)S(1)}, f32[2,192,128]{2,1,0:T(8,128)S(1)}) custom-call(f32[8,128]{1,0:T(8,128)S(1)} %get-tuple-element.23.source.mine, f32[648,128]{1,0:T(8,128)S(1)} %collective-permute-done.inner, ...), custom_call_target="tpu_custom_call" | custom-call | flops 5000000000 | tf_op jit(solution)/shard_map/main/pallas_call | solution.py:661
  32.9 2.1 %collective-permute-start.8 = (f32[2,192,128]{2,1,0:T(8,128)S(1)}, f32[2,192,128]{2,1,0:T(8,128)S(1)}, u32[]{:S(2)}, u32[]{:S(2)}) collective-permute-start(f32[2,192,128]{2,1,0:T(8,128)S(1)} %get-tuple-element.37), channel_id=1, source_target_pairs={{0,4},{1,2},{2,1},{3,7},{4,0},{5,6},{6,5},{7,3},{8,12},{9,10},{10,... | collective-permute-start | bytes 589832 | tf_op jit(solution)/shard_map/ppermute | solution.py:593
  34.9 0.0 collective-permute-start.9
  34.9 1.0 %shard_map.71 = (f32[2,320,320]{2,1,0:T(8,128)S(1)}, f32[2,320,128]{2,1,0:T(8,128)S(1)}, f32[2,320,128]{2,1,0:T(8,128)S(1)}, f32[2,128,384]{2,1,0:T(8,128)S(1)}, f32[2,128,384]{2,1,0:T(8,128)S(1)}) custom-call(f32[8,128]{1,0:T(8,128)S(1)} %get-tuple-element.23.source.mine, bf16[4,320,256]{2,1,0:T(8,128)(2,1)S(1)} %get-tuple-element.29.hi, ...), custom_call_target="tpu_custom_call" | custom-call | flops 2000000000 | tf_op jit(solution)/shard_map/pallas_call | solution.py:30
  36.0 0.7 %collective-permute-start.6 = (f32[2,320,128]{2,1,0:T(8,128)S(1)}, f32[2,320,128]{2,1,0:T(8,128)S(1)}, u32[]{:S(2)}, u32[]{:S(2)}) collective-permute-start(f32[2,320,128]{2,1,0:T(8,128)S(1)} %get-tuple-element.33), channel_id=1, source_target_pairs={{0,0},{1,2},{2,1},{3,3},{4,4},{5,6},{6,5},{7,7},{8,8},{9,10},{10,9... | collective-permute-start | bytes 983048 | tf_op jit(solution)/shard_map/ppermute | solution.py:593
  36.7 2.2 %collective-permute-start.7 = (f32[2,320,128]{2,1,0:T(8,128)S(1)}, f32[2,320,128]{2,1,0:T(8,128)S(1)}, u32[]{:S(2)}, u32[]{:S(2)}) collective-permute-start(f32[2,320,128]{2,1,0:T(8,128)S(1)} %get-tuple-element.34), channel_id=1, source_target_pairs={{0,1},{1,0},{2,3},{3,2},{4,5},{5,4},{6,7},{7,6},{8,9},{9,8},{10,11... | collective-permute-start | bytes 983048 | tf_op jit(solution)/shard_map/ppermute | solution.py:593
  38.8 0.0 collective-permute-done.8.xcorn
  38.8 0.0 collective-permute-done.9.dcorn
  38.8 0.1 shard_map.73
  39.0 1.8 %collective-permute-start.10 = (f32[640,128]{1,0:T(8,128)S(1)}, f32[640,128]{1,0:T(8,128)S(1)}, u32[]{:S(2)}, u32[]{:S(2)}) collective-permute-start(f32[640,128]{1,0:T(8,128)S(1)} %get-tuple-element.39), channel_id=1, source_target_pairs={{0,4},{1,5},{2,6},{3,7},{4,0},{5,1},{6,2},{7,3},{8,12},{9,13},{10,... | collective-permute-start | bytes 983048 | tf_op jit(solution)/shard_map/ppermute | solution.py:593
  40.8 0.0 collective-permute-start.11
  40.8 2.6 %shard_map.72.weight = f32[320,320]{1,0:T(8,128)S(1)} custom-call(f32[8,128]{1,0:T(8,128)S(1)} %get-tuple-element.23.source.mine, f32[408,128]{1,0:T(8,128)S(1)} %collective-permute-done.3.xcorner, f32[408,128]{1,0:T(8,128)S(1)} %collective-permute-done.5.dcorner, f32[648,128]{1,0:T(8,128)S(1)} %collective-permute-done.inner, ...), custom_call_target="tpu_custom_call" | custom-call | flops 10000000000 | tf_op jit(solution)/shard_map/pallas_call | solution.py:30
  43.4 0.0 collective-permute-done.6.xedge
  43.4 0.0 collective-permute-done.7.dedge
  43.4 11.4 %collective-permute-done.10.inner = f32[640,128]{1,0:T(8,128)S(1)} collective-permute-done((f32[640,128]{1,0:T(8,128)S(1)}, f32[640,128]{1,0:T(8,128)S(1)}, u32[]{:S(2)}, u32[]{:S(2)}) %collective-permute-start.10) | collective-permute-done | bytes 327712 | tf_op jit(solution)/shard_map/ppermute | solution.py:593
  54.8 0.0 collective-permute-done.11.cross
  54.8 1.1 %shard_map.74 = f32[2,320,320]{2,1,0:T(8,128)} custom-call(f32[2,320,320]{2,1,0:T(8,128)S(1)} %copy-done.1, f32[2,320,320]{2,1,0:T(8,128)S(1)} %get-tuple-element.32.own, f32[320,320]{1,0:T(8,128)S(1)} %shard_map.72.weight, f32[2,320,128]{2,1,0:T(8,128)S(1)} %collective-permute-done.6.xedge, f32[2,320,128]{2,1,0:T(8,128)S(1)} %collective-permute-done.7.dedge, ...), custom_call_target="tpu_custom_call" | custom-call | tf_op jit(solution)/shard_map/pallas_call | solution.py:30
Async XLA Ops:
  0.0 1.3 %copy-start = (f32[2,320,320]{2,1,0:T(8,128)S(1)}, f32[2,320,320]{2,1,0:T(8,128)}, u32[]{:S(2)}) copy-start(f32[2,320,320]{2,1,0:T(8,128)} %obj.9) | copy-start | bytes 2457604
  2.0 6.6 %collective-permute-start.4 = (f32[648,128]{1,0:T(8,128)S(1)}, f32[648,128]{1,0:T(8,128)S(1)}, u32[]{:S(2)}, u32[]{:S(2)}) collective-permute-start(f32[648,128]{1,0:T(8,128)S(1)} %get-tuple-element.26), channel_id=1, source_target_pairs={{0,1},{1,0},{2,3},{3,2},{4,5},{5,4},{6,7},{7,6},{8,9},{9,8},{10,11... | collective-permute-start | bytes 995336 | tf_op jit(solution)/shard_map/ppermute | solution.py:593
  2.6 22.7 %copy-start.3 = (s32[1,1,1,512,512]{4,3,2,1,0:T(8,128)S(1)}, s32[1,1,1,512,512]{4,3,2,1,0:T(8,128)}, u32[]{:S(2)}) copy-start(s32[1,1,1,512,512]{4,3,2,1,0:T(8,128)} %param.9) | copy-start | bytes 3145732
  3.8 21.5 %copy-start.2 = (f32[2,512,512]{2,1,0:T(8,128)S(1)}, f32[2,512,512]{2,1,0:T(8,128)}, u32[]{:S(2)}) copy-start(f32[2,512,512]{2,1,0:T(8,128)} %probe.3) | copy-start | bytes 6291460
  3.8 4.8 %collective-permute-start.1 = (f32[648,128]{1,0:T(8,128)S(1)}, f32[648,128]{1,0:T(8,128)S(1)}, u32[]{:S(2)}, u32[]{:S(2)}) collective-permute-start(f32[648,128]{1,0:T(8,128)S(1)} %shard_map.65), channel_id=1, source_target_pairs={{0,1},{1,0},{2,3},{3,2},{4,8},{5,9},{6,10},{7,11},{8,4},{9,5},{10,... | collective-permute-start | bytes 995336 | tf_op jit(solution)/shard_map/ppermute | solution.py:593
  3.9 18.2 %collective-permute-start = (f32[648,128]{1,0:T(8,128)S(1)}, f32[648,128]{1,0:T(8,128)S(1)}, u32[]{:S(2)}, u32[]{:S(2)}) collective-permute-start(f32[648,128]{1,0:T(8,128)S(1)} %get-tuple-element.24), channel_id=1, source_target_pairs={{0,4},{1,5},{2,6},{3,7},{4,0},{5,1},{6,2},{7,3},{8,12},{9,13},{10,... | collective-permute-start | bytes 995336 | tf_op jit(solution)/shard_map/ppermute | solution.py:593
  7.9 14.6 %collective-permute-start.2 = (f32[648,128]{1,0:T(8,128)S(1)}, f32[648,128]{1,0:T(8,128)S(1)}, u32[]{:S(2)}, u32[]{:S(2)}) collective-permute-start(f32[648,128]{1,0:T(8,128)S(1)} %get-tuple-element.25), channel_id=1, source_target_pairs={{0,0},{1,2},{2,1},{3,3},{4,4},{5,6},{6,5},{7,7},{8,8},{9,10},{10,9... | collective-permute-start | bytes 995336 | tf_op jit(solution)/shard_map/ppermute | solution.py:593
  22.4 5.9 %collective-permute-start.5 = (f32[408,128]{1,0:T(8,128)S(1)}, f32[408,128]{1,0:T(8,128)S(1)}, u32[]{:S(2)}, u32[]{:S(2)}) collective-permute-start(f32[408,128]{1,0:T(8,128)S(1)} %shard_map.68), channel_id=1, source_target_pairs={{0,1},{1,0},{2,3},{3,2},{4,5},{5,4},{6,7},{7,6},{8,9},{9,8},{10,11... | collective-permute-start | bytes 626696 | tf_op jit(solution)/shard_map/ppermute | solution.py:593
  22.7 6.3 %collective-permute-start.3 = (f32[408,128]{1,0:T(8,128)S(1)}, f32[408,128]{1,0:T(8,128)S(1)}, u32[]{:S(2)}, u32[]{:S(2)}) collective-permute-start(f32[408,128]{1,0:T(8,128)S(1)} %shard_map.67), channel_id=1, source_target_pairs={{0,4},{1,2},{2,1},{3,7},{4,0},{5,6},{6,5},{7,3},{8,12},{9,10},{10,... | collective-permute-start | bytes 626696 | tf_op jit(solution)/shard_map/ppermute | solution.py:593
  25.3 1.8 %copy-start.1 = (f32[2,320,320]{2,1,0:T(8,128)S(1)}, f32[2,320,320]{2,1,0:T(8,128)}, u32[]{:S(2)}) copy-start(f32[2,320,320]{2,1,0:T(8,128)} %obj.9) | copy-start | bytes 2457604
  25.3 1.8 %copy-start.4 = (bf16[8,256,256]{2,1,0:T(8,128)(2,1)S(1)}, bf16[8,256,256]{2,1,0:T(8,128)(2,1)}, u32[]{:S(2)}) copy-start(bf16[8,256,256]{2,1,0:T(8,128)(2,1)} %constant.4.clone.high) | copy-start | bytes 3145732
  25.3 1.8 %copy-start.5 = (bf16[8,256,256]{2,1,0:T(8,128)(2,1)S(1)}, bf16[8,256,256]{2,1,0:T(8,128)(2,1)}, u32[]{:S(2)}) copy-start(bf16[8,256,256]{2,1,0:T(8,128)(2,1)} %constant.5.clone.low) | copy-start | bytes 3145732
  32.9 6.0 %collective-permute-start.8 = (f32[2,192,128]{2,1,0:T(8,128)S(1)}, f32[2,192,128]{2,1,0:T(8,128)S(1)}, u32[]{:S(2)}, u32[]{:S(2)}) collective-permute-start(f32[2,192,128]{2,1,0:T(8,128)S(1)} %get-tuple-element.37), channel_id=1, source_target_pairs={{0,4},{1,2},{2,1},{3,7},{4,0},{5,6},{6,5},{7,3},{8,12},{9,10},{10,... | collective-permute-start | bytes 589832 | tf_op jit(solution)/shard_map/ppermute | solution.py:593
  34.9 3.9 %collective-permute-start.9 = (f32[2,192,128]{2,1,0:T(8,128)S(1)}, f32[2,192,128]{2,1,0:T(8,128)S(1)}, u32[]{:S(2)}, u32[]{:S(2)}) collective-permute-start(f32[2,192,128]{2,1,0:T(8,128)S(1)} %get-tuple-element.38), channel_id=1, source_target_pairs={{0,1},{1,0},{2,3},{3,2},{4,5},{5,4},{6,7},{7,6},{8,9},{9,8},{10,11... | collective-permute-start | bytes 589832 | tf_op jit(solution)/shard_map/ppermute | solution.py:593
  36.0 7.4 %collective-permute-start.6 = (f32[2,320,128]{2,1,0:T(8,128)S(1)}, f32[2,320,128]{2,1,0:T(8,128)S(1)}, u32[]{:S(2)}, u32[]{:S(2)}) collective-permute-start(f32[2,320,128]{2,1,0:T(8,128)S(1)} %get-tuple-element.33), channel_id=1, source_target_pairs={{0,0},{1,2},{2,1},{3,3},{4,4},{5,6},{6,5},{7,7},{8,8},{9,10},{10,9... | collective-permute-start | bytes 983048 | tf_op jit(solution)/shard_map/ppermute | solution.py:593
  36.7 6.7 %collective-permute-start.7 = (f32[2,320,128]{2,1,0:T(8,128)S(1)}, f32[2,320,128]{2,1,0:T(8,128)S(1)}, u32[]{:S(2)}, u32[]{:S(2)}) collective-permute-start(f32[2,320,128]{2,1,0:T(8,128)S(1)} %get-tuple-element.34), channel_id=1, source_target_pairs={{0,1},{1,0},{2,3},{3,2},{4,5},{5,4},{6,7},{7,6},{8,9},{9,8},{10,11... | collective-permute-start | bytes 983048 | tf_op jit(solution)/shard_map/ppermute | solution.py:593
  39.0 15.8 %collective-permute-start.10 = (f32[640,128]{1,0:T(8,128)S(1)}, f32[640,128]{1,0:T(8,128)S(1)}, u32[]{:S(2)}, u32[]{:S(2)}) collective-permute-start(f32[640,128]{1,0:T(8,128)S(1)} %get-tuple-element.39), channel_id=1, source_target_pairs={{0,4},{1,5},{2,6},{3,7},{4,0},{5,1},{6,2},{7,3},{8,12},{9,13},{10,... | collective-permute-start | bytes 983048 | tf_op jit(solution)/shard_map/ppermute | solution.py:593
  40.8 14.0 %collective-permute-start.11 = (f32[640,128]{1,0:T(8,128)S(1)}, f32[640,128]{1,0:T(8,128)S(1)}, u32[]{:S(2)}, u32[]{:S(2)}) collective-permute-start(f32[640,128]{1,0:T(8,128)S(1)} %get-tuple-element.40), channel_id=1, source_target_pairs={{0,1},{1,0},{2,3},{3,2},{4,8},{5,9},{6,10},{7,11},{8,4},{9,5},{10,... | collective-permute-start | bytes 983048 | tf_op jit(solution)/shard_map/ppermute | solution.py:593

commit v7 on v6

--- a/solution.py
+++ b/solution.py
@@ -125,7 +125,7 @@
     rows, cols = obj.shape[1:]
     upward = odd("row") if first == 0 else ~odd("row")
     base = pl.multiple_of(jnp.where(upward, 0, rows - OVL), 8)
-    out, *mine, held, numbers, sems = refs
+    out, middle, *mine, held, numbers, sems = refs
     copies = [pltpu.make_async_copy(obj.at[:, pl.ds(base, OVL), :], held, sems.at[0])]
     copies[0].start()
     if first == 0:
@@ -136,14 +136,13 @@
         mine[0][...] = info
     else:
         info = source[...]
-    out[5 * OVL : 5 * OVL + 8, :] = paired("row", info, first)
+    out[4 * OVL : 4 * OVL + 8, :] = paired("row", info, first)
     copies[0].wait()
     for c in range(2):
-        for k in range(2):
-            at = (2 * c + k) * OVL
-            out[at : at + OVL, :] = paired("row", held[c, :, 128 * k : 128 * k + 128], first)
-        tail = paired("row", held[c, :, 256:cols], first)
-        out[4 * OVL : 5 * OVL, c * HALF : c * HALF + HALF] = tail
+        at = 2 * c * OVL
+        out[at : at + OVL, :] = paired("row", held[c, :, 0:OVL], first)
+        out[at + OVL : at + 2 * OVL, :] = paired("row", held[c, :, cols - OVL : cols], first)
+        middle[:, c * HALF : c * HALF + HALF] = paired("row", held[c, :, OVL : cols - OVL], first)
 
 
 def side_kernel(mine, obj, xside, dside):
@@ -165,7 +164,6 @@
     to_right = odd("col") if first else ~odd("col")
     cells = (side.shape[0] - 8) // 2
     border = side[2 * cells : 2 * cells + 1, :]
-    lane = lane_iota((HALF, LANES))
     row = row_iota((HALF, LANES)).astype(F32)
 
     def end(part, c, base):
@@ -174,9 +172,7 @@
             a, b = inner[at, :], cross[at, :]
             return jnp.where(far, a, b) if part == 0 else jnp.where(far, b, a)
 
-        tail = take(4)
-        east = jnp.where(lane < HALF, turn(take(2 * c + 1)), turn(tail) if c == 0 else tail)
-        return paired("col", jnp.where(to_right, east, turn(take(2 * c))), first)
+        return paired("col", jnp.where(to_right, take(2 * c + 1), turn(take(2 * c))), first)
 
     for c in range(2):
         base = c * KEPT
@@ -184,8 +180,8 @@
         out[base + HALF : base + OVL, :] = end(0, c, HALF)
         out[base + OVL : base + KEPT, :] = end(1, c, 0)
     rows = 2 * KEPT
-    out[rows : rows + 8, :] = paired("col", inner[5 * OVL : 5 * OVL + 8, :], first)
-    out[rows + 8 : rows + 16, :] = paired("col", cross[5 * OVL : 5 * OVL + 8, :], first)
+    out[rows : rows + 8, :] = paired("col", inner[4 * OVL : 4 * OVL + 8, :], first)
+    out[rows + 8 : rows + 16, :] = paired("col", cross[4 * OVL : 4 * OVL + 8, :], first)
     out[rows + 16 : rows + 24, :] = paired("col", mine[...], first)
 
 
@@ -293,7 +289,7 @@
 
 
 def main_kernel(
-    mine, inner, cross, xcorner, dcorner, rolled, measured, zown, high, low,
+    mine, inner, cross, minner, mcross, xcorner, dcorner, rolled, measured, zown, high, low,
     own_hi, own_lo, zback, xcorn, dcorn, ah, al, bh, bl, zh, tf,
 ):
     size = rolled.shape[-1]
@@ -310,9 +306,9 @@
     def patch(c, slot, base):
         def halo(part, start):
             tiles = []
-            for t in (2 * c, 2 * c + 1, 4):
+            for first, second, t in ((inner, cross, 2 * c), (minner, mcross, 0), (inner, cross, 2 * c + 1)):
                 at = slice(t * OVL + start, t * OVL + start + STEP)
-                a, b = inner[at, :], cross[at, :]
+                a, b = first[at, :], second[at, :]
                 tiles.append(jnp.where(far, a, b) if part == 0 else jnp.where(far, b, a))
             return tiles
 
@@ -323,11 +319,12 @@
         if slot < HALF:
             row = step_row + slot
             tiles = [jnp.where(row < u, b, a) for a, b in zip(tiles, halo(1, slot + HALF))]
-        last = turn(tiles[2]) if c == 1 else tiles[2]
+        last = turn(tiles[2])
+        middle = jnp.where(lane < HALF, turn(tiles[1]) if c == 1 else tiles[1], last)
         at = slice(c * KEPT + base, c * KEPT + base + STEP)
         x, d = xcorner[at, :], dcorner[at, :]
         w, e = jnp.where(right, d, x), jnp.where(right, x, d)
-        return [jnp.where(early, e, w), tiles[0], tiles[1], jnp.where(lane < HALF, last, e)]
+        return [jnp.where(early, e, w), tiles[0], middle, jnp.where(lane < HALF, last, e)]
 
     block = 2 * quarter
     re, im = slice(0, quarter), slice(quarter, 2 * quarter)
@@ -392,7 +389,7 @@
             dcorn[c, at, :] = dout
 
 
-def after_kernel(mine, hi, lo, zback, rolled, high, low, own, xedge, dedge, nblock, sblock, z):
+def after_kernel(mine, hi, lo, rolled, high, low, own, xedge, dedge, z):
     cells = own.shape[1]
     v = mine[1:2, :]
     right = odd("col")
@@ -408,6 +405,12 @@
                 own[c, at, 256:cells] = g[2][:, : cells - 256]
                 xedge[c, at, :] = xout
                 dedge[c, at, :] = dout
+
+
+def block_kernel(mine, zback, rolled, nblock, sblock, minner, mcross):
+    cells = rolled.shape[-1] - zback.shape[1]
+    v = mine[1:2, :]
+    right = odd("col")
     u = mine[0:1, :]
     for base in range(0, zback.shape[1], STEP):
         slot = base if base < OVL else base + cells
@@ -425,6 +428,11 @@
                 for t, x in enumerate(g):
                     put = x if mask is None else jnp.where(mask, x, 0.0)
                     block[c, o : o + STEP, 128 * t : 128 * t + 128] = put
+    far = odd("row")
+    first = lane_iota((OVL, LANES)) < HALF
+    n, s = [jnp.where(first, b[0, :, 128:256], turn(b[1, :, 128:256])) for b in (nblock, sblock)]
+    minner[...] = paired("row", jnp.where(far, n, s), 0)
+    mcross[...] = paired("row", jnp.where(far, s, n), 1)
 
 
 def send_kernel(nblock, sblock, xcorn, dcorn, xcorner, dcorner, inner, cross):
@@ -447,14 +455,13 @@
         rows = slice(base, base + HALF)
         tiles = []
         for part, block in enumerate((nblock, sblock)):
-            last, out = [], []
+            out = []
             for c in range(2):
                 x, d = [corner(*pair, c, part, base) for pair in zip((xcorn, dcorn), borders)]
                 fw, fe = jnp.where(right, d, x), jnp.where(right, x, d)
                 out.append(block[c, rows, 0:128] + fw)
-                out.append(block[c, rows, 128:256] + jnp.where(first, 0.0, fe))
-                last.append(block[c, rows, 256:384] + fe)
-            out.append(jnp.where(first, last[0], turn(last[1])))
+                end = jnp.where(first, block[c, rows, 256:384], block[c, rows, 128:256])
+                out.append(turn(end + fe))
             tiles.append(out)
         for t, (n, s) in enumerate(zip(*tiles)):
             to = slice(t * OVL + base, t * OVL + base + HALF)
@@ -487,7 +494,7 @@
             if di == 0 and dj == 0:
                 tile = mine[...]
             elif dj == 0:
-                tile = take(inner, cross, 5 * OVL, 5 * OVL)
+                tile = take(inner, cross, 4 * OVL, 4 * OVL)
             else:
                 if di == 0:
                     x, d = [ref[2 * KEPT + 16 : 2 * KEPT + 24, :] for ref in (xcorner, dcorner)]
@@ -523,7 +530,9 @@
         weight[rows, :] = STEP_SIZE / (acc[rows, 0:cells] + REGULAR)
 
 
-def final_kernel(obj, own, weight, xedge, dedge, inner, cross, updated, held, sems):
+def final_kernel(
+    obj, own, weight, xedge, dedge, inner, cross, minner, mcross, updated, held, sems
+):
     cells = obj.shape[1]
     right = odd("col")
     far = odd("row")
@@ -546,14 +555,16 @@
                 adds.append((1, r - cells + OVL))
             for part, o in adds:
 
-                def take(tile, cols=slice(0, LANES)):
+                def take(first, second, tile):
                     src = slice(tile * OVL + o, tile * OVL + o + HALF)
-                    a, b = inner[src, cols], cross[src, cols]
+                    a, b = first[src, :], second[src, :]
                     return jnp.where(far, a, b) if part == 0 else jnp.where(far, b, a)
 
-                g[0] = g[0] + take(2 * c)
-                g[1] = g[1] + take(2 * c + 1)
-                g[2] = g[2] + take(4, slice(c * HALF, c * HALF + HALF))
+                end = turn(take(inner, cross, 2 * c + 1))
+                middle = take(minner, mcross, 0)
+                g[0] = g[0] + take(inner, cross, 2 * c)
+                g[1] = g[1] + jnp.where(first, turn(middle) if c == 1 else middle, end)
+                g[2] = g[2] + end[:, : cells - 256]
             for t, x in enumerate(g):
                 cols = slice(128 * t, min(128 * t + 128, cells))
                 held[c, rows, cols] = obj[c, rows, cols] - x * weight[rows, cols]
@@ -601,7 +612,7 @@
     high, low = jnp.asarray(table_high), jnp.asarray(table_low)
 
     def rows_for(first, source, space):
-        shapes = [(5 * OVL + 8, LANES)] + [(8, LANES)] * (first == 0)
+        shapes = [(4 * OVL + 8, LANES), (OVL, LANES)] + [(8, LANES)] * (first == 0)
         step = pl.pallas_call(
             functools.partial(row_kernel, first),
             out_shape=[pltpu.VMEM(n, F32) for n in shapes],
@@ -620,9 +631,9 @@
             pltpu.with_memory_space_constraint(object_slab, pltpu.HBM),
         )
 
-    to_inner, mine = rows_for(0, offsets, pltpu.HBM)
+    to_inner, middle_inner, mine = rows_for(0, offsets, pltpu.HBM)
     halo_inner = permute(to_inner, row_inner)
-    (to_cross,) = rows_for(1, mine, pltpu.VMEM)
+    to_cross, middle_cross = rows_for(1, mine, pltpu.VMEM)
     halo_cross = permute(to_cross, row_cross)
     xside, dside = call(side_kernel, [(2 * cells + 8, OVL)] * 2, [mine, object_slab], flops=5_000_000_000)
     side_x = permute(xside, col_cross)
@@ -643,6 +654,8 @@
         scratch=[pltpu.VMEM((4, cells, half), BF16) for _ in range(2)],
         flops=2_000_000_000,
     )
+    halo_mi = permute(middle_inner, row_inner)
+    halo_mc = permute(middle_cross, row_cross)
     ends = []
     for first, side in ((1, side_x), (0, side_d)):
         kernel = functools.partial(corner_kernel, first)
@@ -657,7 +670,8 @@
         ((2, count, OVL), F32),
         ((2, count, OVL), F32),
     ]
-    operands = [mine, halo_inner, halo_cross, corner_x, corner_d, rolled, measured, zown, high, low]
+    operands = [mine, halo_inner, halo_cross, halo_mi, halo_mc, corner_x, corner_d]
+    operands += [rolled, measured, zown, high, low]
     own_hi, own_lo, zback, xcorn, dcorn = pl.pallas_call(
         main_kernel,
         name="main",
@@ -677,16 +691,21 @@
     )(*[pltpu.with_memory_space_constraint(x, pltpu.VMEM) for x in operands])
     fix_x = permute(xcorn, col_full)
     fix_d = permute(dcorn, col_inner)
-    own, xedge, dedge, nblock, sblock = call(
+    nblock, sblock, middle_inner, middle_cross = call(
+        block_kernel, [(2, OVL, 384)] * 2 + [(OVL, LANES)] * 2, [mine, zback, rolled], flops=1_000_000_000
+    )
+    grad_mi = permute(middle_inner, row_inner)
+    grad_mc = permute(middle_cross, row_cross)
+    to_inner, to_cross = call(send_kernel, [(4 * OVL, LANES)] * 2, [nblock, sblock, fix_x, fix_d, corner_x, corner_d])
+    grad_inner = permute(to_inner, row_inner)
+    grad_cross = permute(to_cross, row_cross)
+    own, xedge, dedge = call(
         after_kernel,
-        [(2, cells, cells)] + [(2, cells, OVL)] * 2 + [(2, OVL, 384)] * 2,
-        [mine, own_hi, own_lo, zback, rolled, high, low],
+        [(2, cells, cells)] + [(2, cells, OVL)] * 2,
+        [mine, own_hi, own_lo, rolled, high, low],
         scratch=[pltpu.VMEM((4, cells, half), F32)],
         flops=2_000_000_000,
     )
-    to_inner, to_cross = call(send_kernel, [(5 * OVL, LANES)] * 2, [nblock, sblock, fix_x, fix_d, corner_x, corner_d])
-    grad_inner = permute(to_inner, row_inner)
-    grad_cross = permute(to_cross, row_cross)
     edge_x = permute(xedge, col_cross)
     edge_d = permute(dedge, col_inner)
     (weight,) = call(
@@ -699,7 +718,7 @@
     (updated,) = call(
         final_kernel,
         [(2, cells, cells)],
-        [object_slab, own, weight, edge_x, edge_d, grad_inner, grad_cross],
+        [object_slab, own, weight, edge_x, edge_d, grad_inner, grad_cross, grad_mi, grad_mc],
         hbm_out=True,
         scratch=[
             pltpu.VMEM((2, cells, cells), F32),

time: 56.1 us -> 57.7 us (1.029)
  starting transfers between devices: 14.8 us -> 25.6 us
  waiting for transfers between devices: 25.7 us -> 16.3 us
    ppermute x12 -> x16, starting transfers between devices: 14.8 us -> 25.6 us  [permute(): return lax.ppermute(x, ('row', 'col'), pairs)]
    ppermute x12 -> x16, waiting for transfers between devices: 25.7 us -> 16.3 us  [permute(): return lax.ppermute(x, ('row', 'col'), pairs)]
    pallas_call x9 -> x10, Pallas kernels: 8.96 us -> 8.98 us  [call(): pl.pallas_call(kernel, out_shape=[jax.ShapeDtypeStruct(s, F32) if hbm_out...]
  transfers between devices with their start and end apart: 12 -> 16, of which waited for: 3 -> 4; matrix products, arithmetic and copies ran while one was open for 0% -> 0% of each run, Pallas kernels for 15% -> 15%
where the time goes in v7:
time: 57.7 us; the launch traced here: 57.5 us
  starting transfers between devices  25.6 us (44%)
  waiting for transfers between devices  16.3 us (28%)
  Pallas kernels  15.2 us (26%)
    ppermute x16, starting transfers between devices, permute(): return lax.ppermute(x, ('row', 'col'), pairs)  25.6 us
    ppermute x16, waiting for transfers between devices, permute(): return lax.ppermute(x, ('row', 'col'), pairs)  16.3 us
    pallas_call x10, Pallas kernels, call(): pl.pallas_call(kernel, out_shape=[jax.ShapeDtypeStruct(s, F32) if hbm_out...  8.98 us
    pallas_call x1, Pallas kernels, local(): pl.pallas_call(main_kernel, name='main', out_shape=[pltpu.VMEM(s, d) for...  3.75 us
    pallas_call x2, Pallas kernels, rows_for(): step(pltpu.with_memory_space_constraint(source, space), pltpu.with_memory...  2.52 us
  transfers between devices with their start and end apart: 16, of which 4 were waited for; matrix products, arithmetic and copies ran while one was open for 0% of the time, Pallas kernels for 15%

profile of v7, /device:TPU:0, one launch (start us, length us, event | category | flops | bytes accessed | tf_op | source)
XLA Modules:
  0.0 57.5 jit_solution(12112782969956229797)
XLA Ops:
  0.0 0.0 copy-start
  0.0 1.3 %shard_map.64 = (f32[520,128]{1,0:T(8,128)S(1)}, f32[128,128]{1,0:T(8,128)S(1)}, f32[8,128]{1,0:T(8,128)S(1)}) custom-call(s32[1,1,1,2]{3,2,1,0:T(1,128)} %source.1, f32[2,320,320]{2,1,0:T(8,128)} %obj.9), custom_call_target="tpu_custom_call" | custom-call | flops 2500000000 | tf_op jit(solution)/shard_map/pallas_call | solution.py:629
  1.3 0.1 copy-done
  1.3 0.7 %shard_map.66 = (f32[648,128]{1,0:T(8,128)S(1)}, f32[648,128]{1,0:T(8,128)S(1)}) custom-call(f32[8,128]{1,0:T(8,128)S(1)} %get-tuple-element.28.source.mine, f32[2,320,320]{2,1,0:T(8,128)S(1)} %copy-done), custom_call_target="tpu_custom_call" | custom-call | flops 5000000000 | tf_op jit(solution)/shard_map/pallas_call | solution.py:30
  2.0 0.7 %collective-permute-start.4 = (f32[648,128]{1,0:T(8,128)S(1)}, f32[648,128]{1,0:T(8,128)S(1)}, u32[]{:S(2)}, u32[]{:S(2)}) collective-permute-start(f32[648,128]{1,0:T(8,128)S(1)} %get-tuple-element.33), channel_id=1, source_target_pairs={{0,0},{1,2},{2,1},{3,3},{4,4},{5,6},{6,5},{7,7},{8,8},{9,10},{10,9... | collective-permute-start | bytes 995336 | tf_op jit(solution)/shard_map/ppermute | solution.py:604
  2.7 4.4 %collective-permute-start.6 = (f32[648,128]{1,0:T(8,128)S(1)}, f32[648,128]{1,0:T(8,128)S(1)}, u32[]{:S(2)}, u32[]{:S(2)}) collective-permute-start(f32[648,128]{1,0:T(8,128)S(1)} %get-tuple-element.34), channel_id=1, source_target_pairs={{0,1},{1,0},{2,3},{3,2},{4,5},{5,4},{6,7},{7,6},{8,9},{9,8},{10,11... | collective-permute-start | bytes 995336 | tf_op jit(solution)/shard_map/ppermute | solution.py:604
  7.1 0.0 copy-start.3
  7.1 1.3 %shard_map.65 = (f32[520,128]{1,0:T(8,128)S(1)}, f32[128,128]{1,0:T(8,128)S(1)}) custom-call(f32[8,128]{1,0:T(8,128)S(1)} %get-tuple-element.28.source.mine, f32[2,320,320]{2,1,0:T(8,128)} %obj.9), custom_call_target="tpu_custom_call" | custom-call | flops 2500000000 | tf_op jit(solution)/shard_map/pallas_call | solution.py:629
  8.3 0.0 copy-start.2
  8.3 0.1 collective-permute-start.1
  8.4 3.0 %collective-permute-start = (f32[520,128]{1,0:T(8,128)S(1)}, f32[520,128]{1,0:T(8,128)S(1)}, u32[]{:S(2)}, u32[]{:S(2)}) collective-permute-start(f32[520,128]{1,0:T(8,128)S(1)} %get-tuple-element.29), channel_id=1, source_target_pairs={{0,4},{1,5},{2,6},{3,7},{4,0},{5,1},{6,2},{7,3},{8,12},{9,13},{10,... | collective-permute-start | bytes 798728 | tf_op jit(solution)/shard_map/ppermute | solution.py:604
  11.5 0.0 collective-permute-start.3
  11.5 0.0 collective-permute-done.1.cross
  11.5 8.5 %collective-permute-start.2 = (f32[128,128]{1,0:T(8,128)S(1)}, f32[128,128]{1,0:T(8,128)S(1)}, u32[]{:S(2)}, u32[]{:S(2)}) collective-permute-start(f32[128,128]{1,0:T(8,128)S(1)} %get-tuple-element.31), channel_id=1, source_target_pairs={{0,4},{1,5},{2,6},{3,7},{4,0},{5,1},{6,2},{7,3},{8,12},{9,13},{10,... | collective-permute-start | bytes 196616 | tf_op jit(solution)/shard_map/ppermute | solution.py:604
  20.0 3.9 %collective-permute-done.inner = f32[520,128]{1,0:T(8,128)S(1)} collective-permute-done((f32[520,128]{1,0:T(8,128)S(1)}, f32[520,128]{1,0:T(8,128)S(1)}, u32[]{:S(2)}, u32[]{:S(2)}) %collective-permute-start) | collective-permute-done | bytes 266272 | tf_op jit(solution)/shard_map/ppermute | solution.py:604
  23.9 0.0 collective-permute-done.6.side.dside
  23.9 0.1 shard_map.68
  24.0 0.1 collective-permute-start.7
  24.1 0.0 collective-permute-done.4.side.xside
  24.1 0.2 shard_map.67
  24.3 2.5 %collective-permute-start.5 = (f32[408,128]{1,0:T(8,128)S(1)}, f32[408,128]{1,0:T(8,128)S(1)}, u32[]{:S(2)}, u32[]{:S(2)}) collective-permute-start(f32[408,128]{1,0:T(8,128)S(1)} %shard_map.67), channel_id=1, source_target_pairs={{0,4},{1,2},{2,1},{3,7},{4,0},{5,6},{6,5},{7,3},{8,12},{9,10},{10,... | collective-permute-start | bytes 626696 | tf_op jit(solution)/shard_map/ppermute | solution.py:604
  26.8 0.0 copy-done.3
  26.8 0.0 copy-done.2
  26.8 0.0 copy-start.1
  26.8 0.0 copy-start.4
  26.9 0.0 copy-start.5
  26.9 1.8 %shard_map.69 = (f32[2,512,512]{2,1,0:T(8,128)S(1)}, f32[512,512]{1,0:T(8,128)S(1)}) custom-call(f32[8,128]{1,0:T(8,128)S(1)} %get-tuple-element.28.source.mine, f32[2,512,512]{2,1,0:T(8,128)S(1)} %copy-done.2, s32[512,512]{1,0:T(8,128)S(1)} %bitcast.1), custom_call_target="tpu_custom_call" | custom-call | flops 5000000000 | tf_op jit(solution)/shard_map/pallas_call | solution.py:30
  28.7 0.0 copy-done.1
  28.7 0.0 copy-done.4
  28.7 0.0 copy-done.5
  28.7 1.2 %shard_map.70.zown = f32[4,320,256]{2,1,0:T(8,128)S(1)} custom-call(f32[8,128]{1,0:T(8,128)S(1)} %get-tuple-element.28.source.mine, f32[2,320,320]{2,1,0:T(8,128)S(1)} %copy-done.1, f32[648,128]{1,0:T(8,128)S(1)} %collective-permute-done.4.side.xside, f32[648,128]{1,0:T(8,128)S(1)} %collective-permute-done.6.side.dside, ...), custom_call_target="tpu_custom_call" | custom-call | flops 2000000000 | tf_op jit(solution)/shard_map/pallas_call | solution.py:30
  29.9 0.0 collective-permute-done.3.mcross
  29.9 0.0 collective-permute-done.2.minner
  29.9 0.0 collective-permute-done.7.dcorner
  29.9 0.7 %collective-permute-done.5.xcorner = f32[408,128]{1,0:T(8,128)S(1)} collective-permute-done((f32[408,128]{1,0:T(8,128)S(1)}, f32[408,128]{1,0:T(8,128)S(1)}, u32[]{:S(2)}, u32[]{:S(2)}) %collective-permute-start.5) | collective-permute-done | bytes 208928 | tf_op jit(solution)/shard_map/ppermute | solution.py:604
  30.6 3.7 %main.1 = (bf16[4,320,256]{2,1,0:T(8,128)(2,1)S(1)}, bf16[4,320,256]{2,1,0:T(8,128)(2,1)S(1)}, f32[4,192,256]{2,1,0:T(8,128)S(1)}, f32[2,192,128]{2,1,0:T(8,128)S(1)}, f32[2,192,128]{2,1,0:T(8,128)S(1)}) custom-call(f32[8,128]{1,0:T(8,128)S(1)} %get-tuple-element.28.source.mine, f32[520,128]{1,0:T(8,128)S(1)} %collective-permute-done.inner, ...), custom_call_target="tpu_custom_call" | custom-call | flops 5000000000 | tf_op jit(solution)/shard_map/main/pallas_call | solution.py:675
  34.4 2.1 %collective-permute-start.10 = (f32[2,192,128]{2,1,0:T(8,128)S(1)}, f32[2,192,128]{2,1,0:T(8,128)S(1)}, u32[]{:S(2)}, u32[]{:S(2)}) collective-permute-start(f32[2,192,128]{2,1,0:T(8,128)S(1)} %get-tuple-element.45), channel_id=1, source_target_pairs={{0,4},{1,2},{2,1},{3,7},{4,0},{5,6},{6,5},{7,3},{8,12},{9,10},{10,... | collective-permute-start | bytes 589832 | tf_op jit(solution)/shard_map/ppermute | solution.py:604
  36.5 0.0 collective-permute-start.11
  36.5 0.2 shard_map.73
  36.7 0.3 collective-permute-start.14
  36.9 0.4 collective-permute-start.15
  37.3 1.0 %shard_map.71 = (f32[2,320,320]{2,1,0:T(8,128)S(1)}, f32[2,320,128]{2,1,0:T(8,128)S(1)}, f32[2,320,128]{2,1,0:T(8,128)S(1)}) custom-call(f32[8,128]{1,0:T(8,128)S(1)} %get-tuple-element.28.source.mine, bf16[4,320,256]{2,1,0:T(8,128)(2,1)S(1)} %get-tuple-element.37.hi, bf16[4,320,256]{2,1,0:T(8,128)(2,1)S(1)} %get-tuple-element.38.lo, ...), custom_call_target="tpu_custom_call" | custom-call | flops 2000000000 | tf_op jit(solution)/shard_map/pallas_call | solution.py:30
  38.3 0.7 %collective-permute-start.8 = (f32[2,320,128]{2,1,0:T(8,128)S(1)}, f32[2,320,128]{2,1,0:T(8,128)S(1)}, u32[]{:S(2)}, u32[]{:S(2)}) collective-permute-start(f32[2,320,128]{2,1,0:T(8,128)S(1)} %get-tuple-element.40), channel_id=1, source_target_pairs={{0,0},{1,2},{2,1},{3,3},{4,4},{5,6},{6,5},{7,7},{8,8},{9,10},{10,9... | collective-permute-start | bytes 983048 | tf_op jit(solution)/shard_map/ppermute | solution.py:604
  39.0 2.8 %collective-permute-done.10.xcorn = f32[2,192,128]{2,1,0:T(8,128)S(1)} collective-permute-done((f32[2,192,128]{2,1,0:T(8,128)S(1)}, f32[2,192,128]{2,1,0:T(8,128)S(1)}, u32[]{:S(2)}, u32[]{:S(2)}) %collective-permute-start.10) | collective-permute-done | bytes 196640 | tf_op jit(solution)/shard_map/ppermute | solution.py:604
  41.8 0.0 collective-permute-start.9
  41.8 0.0 collective-permute-done.11.dcorn
  41.8 0.2 shard_map.74
  42.0 2.9 %collective-permute-start.12 = (f32[512,128]{1,0:T(8,128)S(1)}, f32[512,128]{1,0:T(8,128)S(1)}, u32[]{:S(2)}, u32[]{:S(2)}) collective-permute-start(f32[512,128]{1,0:T(8,128)S(1)} %get-tuple-element.47), channel_id=1, source_target_pairs={{0,4},{1,5},{2,6},{3,7},{4,0},{5,1},{6,2},{7,3},{8,12},{9,13},{10,... | collective-permute-start | bytes 786440 | tf_op jit(solution)/shard_map/ppermute | solution.py:604
  44.9 0.0 collective-permute-done.14.minner
  44.9 0.0 collective-permute-start.13
  44.9 2.6 %shard_map.72.weight = f32[320,320]{1,0:T(8,128)S(1)} custom-call(f32[8,128]{1,0:T(8,128)S(1)} %get-tuple-element.28.source.mine, f32[408,128]{1,0:T(8,128)S(1)} %collective-permute-done.5.xcorner, f32[408,128]{1,0:T(8,128)S(1)} %collective-permute-done.7.dcorner, f32[520,128]{1,0:T(8,128)S(1)} %collective-permute-done.inner, ...), custom_call_target="tpu_custom_call" | custom-call | flops 10000000000 | tf_op jit(solution)/shard_map/pallas_call | solution.py:30
  47.4 0.0 collective-permute-done.15.mcross
  47.4 0.0 collective-permute-done.8.xedge
  47.4 0.0 collective-permute-done.9.dedge
  47.5 8.9 %collective-permute-done.12.inner = f32[512,128]{1,0:T(8,128)S(1)} collective-permute-done((f32[512,128]{1,0:T(8,128)S(1)}, f32[512,128]{1,0:T(8,128)S(1)}, u32[]{:S(2)}, u32[]{:S(2)}) %collective-permute-start.12) | collective-permute-done | bytes 262176 | tf_op jit(solution)/shard_map/ppermute | solution.py:604
  56.3 0.0 collective-permute-done.13.cross
  56.3 1.2 %shard_map.75 = f32[2,320,320]{2,1,0:T(8,128)} custom-call(f32[2,320,320]{2,1,0:T(8,128)S(1)} %copy-done.1, f32[2,320,320]{2,1,0:T(8,128)S(1)} %get-tuple-element.39.own, f32[320,320]{1,0:T(8,128)S(1)} %shard_map.72.weight, f32[2,320,128]{2,1,0:T(8,128)S(1)} %collective-permute-done.8.xedge, f32[2,320,128]{2,1,0:T(8,128)S(1)} %collective-permute-done.9.dedge, ...), custom_call_target="tpu_custom_call" | custom-call | tf_op jit(solution)/shard_map/pallas_call | solution.py:30
Async XLA Ops:
  0.0 1.3 %copy-start = (f32[2,320,320]{2,1,0:T(8,128)S(1)}, f32[2,320,320]{2,1,0:T(8,128)}, u32[]{:S(2)}) copy-start(f32[2,320,320]{2,1,0:T(8,128)} %obj.9) | copy-start | bytes 2457604
  2.0 22.1 %collective-permute-start.4 = (f32[648,128]{1,0:T(8,128)S(1)}, f32[648,128]{1,0:T(8,128)S(1)}, u32[]{:S(2)}, u32[]{:S(2)}) collective-permute-start(f32[648,128]{1,0:T(8,128)S(1)} %get-tuple-element.33), channel_id=1, source_target_pairs={{0,0},{1,2},{2,1},{3,3},{4,4},{5,6},{6,5},{7,7},{8,8},{9,10},{10,9... | collective-permute-start | bytes 995336 | tf_op jit(solution)/shard_map/ppermute | solution.py:604
  2.7 21.2 %collective-permute-start.6 = (f32[648,128]{1,0:T(8,128)S(1)}, f32[648,128]{1,0:T(8,128)S(1)}, u32[]{:S(2)}, u32[]{:S(2)}) collective-permute-start(f32[648,128]{1,0:T(8,128)S(1)} %get-tuple-element.34), channel_id=1, source_target_pairs={{0,1},{1,0},{2,3},{3,2},{4,5},{5,4},{6,7},{7,6},{8,9},{9,8},{10,11... | collective-permute-start | bytes 995336 | tf_op jit(solution)/shard_map/ppermute | solution.py:604
  7.1 19.8 %copy-start.3 = (s32[1,1,1,512,512]{4,3,2,1,0:T(8,128)S(1)}, s32[1,1,1,512,512]{4,3,2,1,0:T(8,128)}, u32[]{:S(2)}) copy-start(s32[1,1,1,512,512]{4,3,2,1,0:T(8,128)} %param.9) | copy-start | bytes 3145732
  8.3 18.5 %copy-start.2 = (f32[2,512,512]{2,1,0:T(8,128)S(1)}, f32[2,512,512]{2,1,0:T(8,128)}, u32[]{:S(2)}) copy-start(f32[2,512,512]{2,1,0:T(8,128)} %probe.3) | copy-start | bytes 6291460
  8.3 3.1 %collective-permute-start.1 = (f32[520,128]{1,0:T(8,128)S(1)}, f32[520,128]{1,0:T(8,128)S(1)}, u32[]{:S(2)}, u32[]{:S(2)}) collective-permute-start(f32[520,128]{1,0:T(8,128)S(1)} %get-tuple-element.30), channel_id=1, source_target_pairs={{0,1},{1,0},{2,3},{3,2},{4,8},{5,9},{6,10},{7,11},{8,4},{9,5},{10,... | collective-permute-start | bytes 798728 | tf_op jit(solution)/shard_map/ppermute | solution.py:604
  8.4 15.4 %collective-permute-start = (f32[520,128]{1,0:T(8,128)S(1)}, f32[520,128]{1,0:T(8,128)S(1)}, u32[]{:S(2)}, u32[]{:S(2)}) collective-permute-start(f32[520,128]{1,0:T(8,128)S(1)} %get-tuple-element.29), channel_id=1, source_target_pairs={{0,4},{1,5},{2,6},{3,7},{4,0},{5,1},{6,2},{7,3},{8,12},{9,13},{10,... | collective-permute-start | bytes 798728 | tf_op jit(solution)/shard_map/ppermute | solution.py:604
  11.5 18.4 %collective-permute-start.3 = (f32[128,128]{1,0:T(8,128)S(1)}, f32[128,128]{1,0:T(8,128)S(1)}, u32[]{:S(2)}, u32[]{:S(2)}) collective-permute-start(f32[128,128]{1,0:T(8,128)S(1)} %get-tuple-element.32), channel_id=1, source_target_pairs={{0,1},{1,0},{2,3},{3,2},{4,8},{5,9},{6,10},{7,11},{8,4},{9,5},{10,... | collective-permute-start | bytes 196616 | tf_op jit(solution)/shard_map/ppermute | solution.py:604
  11.5 18.4 %collective-permute-start.2 = (f32[128,128]{1,0:T(8,128)S(1)}, f32[128,128]{1,0:T(8,128)S(1)}, u32[]{:S(2)}, u32[]{:S(2)}) collective-permute-start(f32[128,128]{1,0:T(8,128)S(1)} %get-tuple-element.31), channel_id=1, source_target_pairs={{0,4},{1,5},{2,6},{3,7},{4,0},{5,1},{6,2},{7,3},{8,12},{9,13},{10,... | collective-permute-start | bytes 196616 | tf_op jit(solution)/shard_map/ppermute | solution.py:604
  24.0 5.8 %collective-permute-start.7 = (f32[408,128]{1,0:T(8,128)S(1)}, f32[408,128]{1,0:T(8,128)S(1)}, u32[]{:S(2)}, u32[]{:S(2)}) collective-permute-start(f32[408,128]{1,0:T(8,128)S(1)} %shard_map.68), channel_id=1, source_target_pairs={{0,1},{1,0},{2,3},{3,2},{4,5},{5,4},{6,7},{7,6},{8,9},{9,8},{10,11... | collective-permute-start | bytes 626696 | tf_op jit(solution)/shard_map/ppermute | solution.py:604
  24.3 6.3 %collective-permute-start.5 = (f32[408,128]{1,0:T(8,128)S(1)}, f32[408,128]{1,0:T(8,128)S(1)}, u32[]{:S(2)}, u32[]{:S(2)}) collective-permute-start(f32[408,128]{1,0:T(8,128)S(1)} %shard_map.67), channel_id=1, source_target_pairs={{0,4},{1,2},{2,1},{3,7},{4,0},{5,6},{6,5},{7,3},{8,12},{9,10},{10,... | collective-permute-start | bytes 626696 | tf_op jit(solution)/shard_map/ppermute | solution.py:604
  26.8 1.8 %copy-start.1 = (f32[2,320,320]{2,1,0:T(8,128)S(1)}, f32[2,320,320]{2,1,0:T(8,128)}, u32[]{:S(2)}) copy-start(f32[2,320,320]{2,1,0:T(8,128)} %obj.9) | copy-start | bytes 2457604
  26.8 1.8 %copy-start.4 = (bf16[8,256,256]{2,1,0:T(8,128)(2,1)S(1)}, bf16[8,256,256]{2,1,0:T(8,128)(2,1)}, u32[]{:S(2)}) copy-start(bf16[8,256,256]{2,1,0:T(8,128)(2,1)} %constant.4.clone.high) | copy-start | bytes 3145732
  26.9 1.8 %copy-start.5 = (bf16[8,256,256]{2,1,0:T(8,128)(2,1)S(1)}, bf16[8,256,256]{2,1,0:T(8,128)(2,1)}, u32[]{:S(2)}) copy-start(bf16[8,256,256]{2,1,0:T(8,128)(2,1)} %constant.5.clone.low) | copy-start | bytes 3145732
  34.4 7.4 %collective-permute-start.10 = (f32[2,192,128]{2,1,0:T(8,128)S(1)}, f32[2,192,128]{2,1,0:T(8,128)S(1)}, u32[]{:S(2)}, u32[]{:S(2)}) collective-permute-start(f32[2,192,128]{2,1,0:T(8,128)S(1)} %get-tuple-element.45), channel_id=1, source_target_pairs={{0,4},{1,2},{2,1},{3,7},{4,0},{5,6},{6,5},{7,3},{8,12},{9,10},{10,... | collective-permute-start | bytes 589832 | tf_op jit(solution)/shard_map/ppermute | solution.py:604
  36.5 5.3 %collective-permute-start.11 = (f32[2,192,128]{2,1,0:T(8,128)S(1)}, f32[2,192,128]{2,1,0:T(8,128)S(1)}, u32[]{:S(2)}, u32[]{:S(2)}) collective-permute-start(f32[2,192,128]{2,1,0:T(8,128)S(1)} %get-tuple-element.46), channel_id=1, source_target_pairs={{0,1},{1,0},{2,3},{3,2},{4,5},{5,4},{6,7},{7,6},{8,9},{9,8},{10,11... | collective-permute-start | bytes 589832 | tf_op jit(solution)/shard_map/ppermute | solution.py:604
  36.7 8.2 %collective-permute-start.14 = (f32[128,128]{1,0:T(8,128)S(1)}, f32[128,128]{1,0:T(8,128)S(1)}, u32[]{:S(2)}, u32[]{:S(2)}) collective-permute-start(f32[128,128]{1,0:T(8,128)S(1)} %get-tuple-element.49), channel_id=1, source_target_pairs={{0,4},{1,5},{2,6},{3,7},{4,0},{5,1},{6,2},{7,3},{8,12},{9,13},{10,... | collective-permute-start | bytes 196616 | tf_op jit(solution)/shard_map/ppermute | solution.py:604
  36.9 10.5 %collective-permute-start.15 = (f32[128,128]{1,0:T(8,128)S(1)}, f32[128,128]{1,0:T(8,128)S(1)}, u32[]{:S(2)}, u32[]{:S(2)}) collective-permute-start(f32[128,128]{1,0:T(8,128)S(1)} %get-tuple-element.50), channel_id=1, source_target_pairs={{0,1},{1,0},{2,3},{3,2},{4,8},{5,9},{6,10},{7,11},{8,4},{9,5},{10,... | collective-permute-start | bytes 196616 | tf_op jit(solution)/shard_map/ppermute | solution.py:604
  38.3 9.1 %collective-permute-start.8 = (f32[2,320,128]{2,1,0:T(8,128)S(1)}, f32[2,320,128]{2,1,0:T(8,128)S(1)}, u32[]{:S(2)}, u32[]{:S(2)}) collective-permute-start(f32[2,320,128]{2,1,0:T(8,128)S(1)} %get-tuple-element.40), channel_id=1, source_target_pairs={{0,0},{1,2},{2,1},{3,3},{4,4},{5,6},{6,5},{7,7},{8,8},{9,10},{10,9... | collective-permute-start | bytes 983048 | tf_op jit(solution)/shard_map/ppermute | solution.py:604
  41.8 5.7 %collective-permute-start.9 = (f32[2,320,128]{2,1,0:T(8,128)S(1)}, f32[2,320,128]{2,1,0:T(8,128)S(1)}, u32[]{:S(2)}, u32[]{:S(2)}) collective-permute-start(f32[2,320,128]{2,1,0:T(8,128)S(1)} %get-tuple-element.41), channel_id=1, source_target_pairs={{0,1},{1,0},{2,3},{3,2},{4,5},{5,4},{6,7},{7,6},{8,9},{9,8},{10,11... | collective-permute-start | bytes 983048 | tf_op jit(solution)/shard_map/ppermute | solution.py:604
  42.0 14.4 %collective-permute-start.12 = (f32[512,128]{1,0:T(8,128)S(1)}, f32[512,128]{1,0:T(8,128)S(1)}, u32[]{:S(2)}, u32[]{:S(2)}) collective-permute-start(f32[512,128]{1,0:T(8,128)S(1)} %get-tuple-element.47), channel_id=1, source_target_pairs={{0,4},{1,5},{2,6},{3,7},{4,0},{5,1},{6,2},{7,3},{8,12},{9,13},{10,... | collective-permute-start | bytes 786440 | tf_op jit(solution)/shard_map/ppermute | solution.py:604
  44.9 11.5 %collective-permute-start.13 = (f32[512,128]{1,0:T(8,128)S(1)}, f32[512,128]{1,0:T(8,128)S(1)}, u32[]{:S(2)}, u32[]{:S(2)}) collective-permute-start(f32[512,128]{1,0:T(8,128)S(1)} %get-tuple-element.48), channel_id=1, source_target_pairs={{0,1},{1,0},{2,3},{3,2},{4,8},{5,9},{6,10},{7,11},{8,4},{9,5},{10,... | collective-permute-start | bytes 786440 | tf_op jit(solution)/shard_map/ppermute | solution.py:604

commit v8 on v7

--- a/solution.py
+++ b/solution.py
@@ -9,6 +9,7 @@
 from jax.experimental import pallas as pl
 from jax.experimental.pallas import tpu as pltpu
 from jax.sharding import PartitionSpec as P
+
 
 OVL = 128
 HALF = 64
@@ -575,16 +576,17 @@
         copy.wait()
 
 
-def swap(count, first):
+def swap(count, first, gap=1):
     partner = list(range(count))
-    for i in range(first, count - 1, 2):
-        partner[i], partner[i + 1] = i + 1, i
+    for i in range(first, count - gap):
+        if (i - first) // gap % 2 == 0:
+            partner[i], partner[i + gap] = i + gap, i
     return partner
 
 
 def routes():
     rows, cols = lax.axis_size("row"), lax.axis_size("col")
-    odd_row, even_row = swap(rows, 1), swap(rows, 0)
+    odd_row, even_row, far_row = swap(rows, 1), swap(rows, 0), swap(rows, 0, 2)
     odd_col, even_col = swap(cols, 1), swap(cols, 0)
 
     def pairs(partner):
@@ -596,7 +598,7 @@
         pairs(lambda r, c: (even_row[r], c)),
         pairs(lambda r, c: (r, odd_col[c])),
         pairs(lambda r, c: (r, even_col[c])),
-        pairs(lambda r, c: (r if odd_col[c] != c else even_row[r], odd_col[c])),
+        pairs(lambda r, c: (r if odd_col[c] != c else far_row[r], odd_col[c])),
     )
 
 

time: 57.7 us -> 57.6 us (level)
  waiting for transfers between devices: 16.3 us -> 13.5 us
  starting transfers between devices: 25.6 us -> 28.4 us
    ppermute x16, waiting for transfers between devices: 16.3 us -> 13.5 us  [permute(): return lax.ppermute(x, ('row', 'col'), pairs)]
    ppermute x16, starting transfers between devices: 25.6 us -> 28.4 us  [permute(): return lax.ppermute(x, ('row', 'col'), pairs)]
  transfers between devices with their start and end apart: 16 -> 16, of which waited for: 4 -> 3; matrix products, arithmetic and copies ran while one was open for 0% -> 0% of each run, Pallas kernels for 15% -> 15%
where the time goes in v8:
time: 57.6 us; the launch traced here: 57.4 us
  starting transfers between devices  28.4 us (49%)
  Pallas kernels  15.2 us (26%)
  waiting for transfers between devices  13.5 us (23%)
    ppermute x16, starting transfers between devices, permute(): return lax.ppermute(x, ('row', 'col'), pairs)  28.4 us
    ppermute x16, waiting for transfers between devices, permute(): return lax.ppermute(x, ('row', 'col'), pairs)  13.5 us
    pallas_call x10, Pallas kernels, call(): pl.pallas_call(kernel, out_shape=[jax.ShapeDtypeStruct(s, F32) if hbm_out...  8.97 us
    pallas_call x1, Pallas kernels, local(): pl.pallas_call(main_kernel, name='main', out_shape=[pltpu.VMEM(s, d) for...  3.75 us
    pallas_call x2, Pallas kernels, rows_for(): step(pltpu.with_memory_space_constraint(source, space), pltpu.with_memory...  2.52 us
  transfers between devices with their start and end apart: 16, of which 3 were waited for; matrix products, arithmetic and copies ran while one was open for 0% of the time, Pallas kernels for 15%

profile of v8, /device:TPU:0, one launch (start us, length us, event | category | flops | bytes accessed | tf_op | source)
XLA Modules:
  0.0 57.4 jit_solution(4585424804224417411)
XLA Ops:
  0.0 0.0 copy-start
  0.0 1.3 %shard_map.64 = (f32[520,128]{1,0:T(8,128)S(1)}, f32[128,128]{1,0:T(8,128)S(1)}, f32[8,128]{1,0:T(8,128)S(1)}) custom-call(s32[1,1,1,2]{3,2,1,0:T(1,128)} %source.1, f32[2,320,320]{2,1,0:T(8,128)} %obj.9), custom_call_target="tpu_custom_call" | custom-call | flops 2500000000 | tf_op jit(solution)/shard_map/pallas_call | solution.py:631
  1.3 0.1 copy-done
  1.3 0.7 %shard_map.66 = (f32[648,128]{1,0:T(8,128)S(1)}, f32[648,128]{1,0:T(8,128)S(1)}) custom-call(f32[8,128]{1,0:T(8,128)S(1)} %get-tuple-element.28.source.mine, f32[2,320,320]{2,1,0:T(8,128)S(1)} %copy-done), custom_call_target="tpu_custom_call" | custom-call | flops 5000000000 | tf_op jit(solution)/shard_map/pallas_call | solution.py:31
  2.0 0.7 %collective-permute-start.4 = (f32[648,128]{1,0:T(8,128)S(1)}, f32[648,128]{1,0:T(8,128)S(1)}, u32[]{:S(2)}, u32[]{:S(2)}) collective-permute-start(f32[648,128]{1,0:T(8,128)S(1)} %get-tuple-element.33), channel_id=1, source_target_pairs={{0,0},{1,2},{2,1},{3,3},{4,4},{5,6},{6,5},{7,7},{8,8},{9,10},{10,9... | collective-permute-start | bytes 995336 | tf_op jit(solution)/shard_map/ppermute | solution.py:606
  2.7 4.4 %collective-permute-start.6 = (f32[648,128]{1,0:T(8,128)S(1)}, f32[648,128]{1,0:T(8,128)S(1)}, u32[]{:S(2)}, u32[]{:S(2)}) collective-permute-start(f32[648,128]{1,0:T(8,128)S(1)} %get-tuple-element.34), channel_id=1, source_target_pairs={{0,1},{1,0},{2,3},{3,2},{4,5},{5,4},{6,7},{7,6},{8,9},{9,8},{10,11... | collective-permute-start | bytes 995336 | tf_op jit(solution)/shard_map/ppermute | solution.py:606
  7.1 0.0 copy-start.3
  7.1 1.3 %shard_map.65 = (f32[520,128]{1,0:T(8,128)S(1)}, f32[128,128]{1,0:T(8,128)S(1)}) custom-call(f32[8,128]{1,0:T(8,128)S(1)} %get-tuple-element.28.source.mine, f32[2,320,320]{2,1,0:T(8,128)} %obj.9), custom_call_target="tpu_custom_call" | custom-call | flops 2500000000 | tf_op jit(solution)/shard_map/pallas_call | solution.py:631
  8.3 0.0 copy-start.2
  8.3 0.1 collective-permute-start.1
  8.4 3.0 %collective-permute-start = (f32[520,128]{1,0:T(8,128)S(1)}, f32[520,128]{1,0:T(8,128)S(1)}, u32[]{:S(2)}, u32[]{:S(2)}) collective-permute-start(f32[520,128]{1,0:T(8,128)S(1)} %get-tuple-element.29), channel_id=1, source_target_pairs={{0,4},{1,5},{2,6},{3,7},{4,0},{5,1},{6,2},{7,3},{8,12},{9,13},{10,... | collective-permute-start | bytes 798728 | tf_op jit(solution)/shard_map/ppermute | solution.py:606
  11.5 0.0 collective-permute-start.3
  11.5 0.0 collective-permute-done.1.cross
  11.5 8.5 %collective-permute-start.2 = (f32[128,128]{1,0:T(8,128)S(1)}, f32[128,128]{1,0:T(8,128)S(1)}, u32[]{:S(2)}, u32[]{:S(2)}) collective-permute-start(f32[128,128]{1,0:T(8,128)S(1)} %get-tuple-element.31), channel_id=1, source_target_pairs={{0,4},{1,5},{2,6},{3,7},{4,0},{5,1},{6,2},{7,3},{8,12},{9,13},{10,... | collective-permute-start | bytes 196616 | tf_op jit(solution)/shard_map/ppermute | solution.py:606
  20.0 3.9 %collective-permute-done.inner = f32[520,128]{1,0:T(8,128)S(1)} collective-permute-done((f32[520,128]{1,0:T(8,128)S(1)}, f32[520,128]{1,0:T(8,128)S(1)}, u32[]{:S(2)}, u32[]{:S(2)}) %collective-permute-start) | collective-permute-done | bytes 266272 | tf_op jit(solution)/shard_map/ppermute | solution.py:606
  23.9 0.0 collective-permute-done.6.side.dside
  23.9 0.1 shard_map.68
  24.0 0.1 collective-permute-start.7
  24.1 0.0 collective-permute-done.4.side.xside
  24.1 0.2 shard_map.67
  24.3 2.6 %collective-permute-start.5 = (f32[408,128]{1,0:T(8,128)S(1)}, f32[408,128]{1,0:T(8,128)S(1)}, u32[]{:S(2)}, u32[]{:S(2)}) collective-permute-start(f32[408,128]{1,0:T(8,128)S(1)} %shard_map.67), channel_id=1, source_target_pairs={{0,8},{1,2},{2,1},{3,11},{4,12},{5,6},{6,5},{7,15},{8,0},{9,10},{1... | collective-permute-start | bytes 626696 | tf_op jit(solution)/shard_map/ppermute | solution.py:606
  26.9 0.0 copy-done.3
  26.9 0.0 copy-done.2
  26.9 0.0 copy-start.1
  26.9 0.0 copy-start.4
  26.9 0.0 copy-start.5
  26.9 1.8 %shard_map.69 = (f32[2,512,512]{2,1,0:T(8,128)S(1)}, f32[512,512]{1,0:T(8,128)S(1)}) custom-call(f32[8,128]{1,0:T(8,128)S(1)} %get-tuple-element.28.source.mine, f32[2,512,512]{2,1,0:T(8,128)S(1)} %copy-done.2, s32[512,512]{1,0:T(8,128)S(1)} %bitcast.1), custom_call_target="tpu_custom_call" | custom-call | flops 5000000000 | tf_op jit(solution)/shard_map/pallas_call | solution.py:31
  28.7 0.0 copy-done.1
  28.7 0.0 copy-done.4
  28.7 0.0 copy-done.5
  28.7 1.1 %shard_map.70.zown = f32[4,320,256]{2,1,0:T(8,128)S(1)} custom-call(f32[8,128]{1,0:T(8,128)S(1)} %get-tuple-element.28.source.mine, f32[2,320,320]{2,1,0:T(8,128)S(1)} %copy-done.1, f32[648,128]{1,0:T(8,128)S(1)} %collective-permute-done.4.side.xside, f32[648,128]{1,0:T(8,128)S(1)} %collective-permute-done.6.side.dside, ...), custom_call_target="tpu_custom_call" | custom-call | flops 2000000000 | tf_op jit(solution)/shard_map/pallas_call | solution.py:31
  29.9 0.0 collective-permute-done.3.mcross
  29.9 0.0 collective-permute-done.2.minner
  29.9 0.0 collective-permute-done.7.dcorner
  29.9 0.7 %collective-permute-done.5.xcorner = f32[408,128]{1,0:T(8,128)S(1)} collective-permute-done((f32[408,128]{1,0:T(8,128)S(1)}, f32[408,128]{1,0:T(8,128)S(1)}, u32[]{:S(2)}, u32[]{:S(2)}) %collective-permute-start.5) | collective-permute-done | bytes 208928 | tf_op jit(solution)/shard_map/ppermute | solution.py:606
  30.7 3.8 %main.1 = (bf16[4,320,256]{2,1,0:T(8,128)(2,1)S(1)}, bf16[4,320,256]{2,1,0:T(8,128)(2,1)S(1)}, f32[4,192,256]{2,1,0:T(8,128)S(1)}, f32[2,192,128]{2,1,0:T(8,128)S(1)}, f32[2,192,128]{2,1,0:T(8,128)S(1)}) custom-call(f32[8,128]{1,0:T(8,128)S(1)} %get-tuple-element.28.source.mine, f32[520,128]{1,0:T(8,128)S(1)} %collective-permute-done.inner, ...), custom_call_target="tpu_custom_call" | custom-call | flops 5000000000 | tf_op jit(solution)/shard_map/main/pallas_call | solution.py:677
  34.4 2.1 %collective-permute-start.10 = (f32[2,192,128]{2,1,0:T(8,128)S(1)}, f32[2,192,128]{2,1,0:T(8,128)S(1)}, u32[]{:S(2)}, u32[]{:S(2)}) collective-permute-start(f32[2,192,128]{2,1,0:T(8,128)S(1)} %get-tuple-element.45), channel_id=1, source_target_pairs={{0,8},{1,2},{2,1},{3,11},{4,12},{5,6},{6,5},{7,15},{8,0},{9,10},{1... | collective-permute-start | bytes 589832 | tf_op jit(solution)/shard_map/ppermute | solution.py:606
  36.5 0.0 collective-permute-start.11
  36.5 0.2 shard_map.73
  36.7 1.6 %collective-permute-start.14 = (f32[128,128]{1,0:T(8,128)S(1)}, f32[128,128]{1,0:T(8,128)S(1)}, u32[]{:S(2)}, u32[]{:S(2)}) collective-permute-start(f32[128,128]{1,0:T(8,128)S(1)} %get-tuple-element.49), channel_id=1, source_target_pairs={{0,4},{1,5},{2,6},{3,7},{4,0},{5,1},{6,2},{7,3},{8,12},{9,13},{10,... | collective-permute-start | bytes 196616 | tf_op jit(solution)/shard_map/ppermute | solution.py:606
  38.3 0.2 collective-permute-start.15
  38.5 1.0 %shard_map.71 = (f32[2,320,320]{2,1,0:T(8,128)S(1)}, f32[2,320,128]{2,1,0:T(8,128)S(1)}, f32[2,320,128]{2,1,0:T(8,128)S(1)}) custom-call(f32[8,128]{1,0:T(8,128)S(1)} %get-tuple-element.28.source.mine, bf16[4,320,256]{2,1,0:T(8,128)(2,1)S(1)} %get-tuple-element.37.hi, bf16[4,320,256]{2,1,0:T(8,128)(2,1)S(1)} %get-tuple-element.38.lo, ...), custom_call_target="tpu_custom_call" | custom-call | flops 2000000000 | tf_op jit(solution)/shard_map/pallas_call | solution.py:31
  39.5 0.7 %collective-permute-start.8 = (f32[2,320,128]{2,1,0:T(8,128)S(1)}, f32[2,320,128]{2,1,0:T(8,128)S(1)}, u32[]{:S(2)}, u32[]{:S(2)}) collective-permute-start(f32[2,320,128]{2,1,0:T(8,128)S(1)} %get-tuple-element.40), channel_id=1, source_target_pairs={{0,0},{1,2},{2,1},{3,3},{4,4},{5,6},{6,5},{7,7},{8,8},{9,10},{10,9... | collective-permute-start | bytes 983048 | tf_op jit(solution)/shard_map/ppermute | solution.py:606
  40.2 0.0 collective-permute-done.10.xcorn
  40.2 1.6 %collective-permute-start.9 = (f32[2,320,128]{2,1,0:T(8,128)S(1)}, f32[2,320,128]{2,1,0:T(8,128)S(1)}, u32[]{:S(2)}, u32[]{:S(2)}) collective-permute-start(f32[2,320,128]{2,1,0:T(8,128)S(1)} %get-tuple-element.41), channel_id=1, source_target_pairs={{0,1},{1,0},{2,3},{3,2},{4,5},{5,4},{6,7},{7,6},{8,9},{9,8},{10,11... | collective-permute-start | bytes 983048 | tf_op jit(solution)/shard_map/ppermute | solution.py:606
  41.8 0.0 collective-permute-done.11.dcorn
  41.8 0.2 shard_map.74
  42.0 2.9 %collective-permute-start.12 = (f32[512,128]{1,0:T(8,128)S(1)}, f32[512,128]{1,0:T(8,128)S(1)}, u32[]{:S(2)}, u32[]{:S(2)}) collective-permute-start(f32[512,128]{1,0:T(8,128)S(1)} %get-tuple-element.47), channel_id=1, source_target_pairs={{0,4},{1,5},{2,6},{3,7},{4,0},{5,1},{6,2},{7,3},{8,12},{9,13},{10,... | collective-permute-start | bytes 786440 | tf_op jit(solution)/shard_map/ppermute | solution.py:606
  44.9 0.0 collective-permute-done.14.minner
  44.9 0.0 collective-permute-start.13
  44.9 2.6 %shard_map.72.weight = f32[320,320]{1,0:T(8,128)S(1)} custom-call(f32[8,128]{1,0:T(8,128)S(1)} %get-tuple-element.28.source.mine, f32[408,128]{1,0:T(8,128)S(1)} %collective-permute-done.5.xcorner, f32[408,128]{1,0:T(8,128)S(1)} %collective-permute-done.7.dcorner, f32[520,128]{1,0:T(8,128)S(1)} %collective-permute-done.inner, ...), custom_call_target="tpu_custom_call" | custom-call | flops 10000000000 | tf_op jit(solution)/shard_map/pallas_call | solution.py:31
  47.4 0.0 collective-permute-done.15.mcross
  47.4 0.0 collective-permute-done.8.xedge
  47.4 0.0 collective-permute-done.9.dedge
  47.5 8.8 %collective-permute-done.12.inner = f32[512,128]{1,0:T(8,128)S(1)} collective-permute-done((f32[512,128]{1,0:T(8,128)S(1)}, f32[512,128]{1,0:T(8,128)S(1)}, u32[]{:S(2)}, u32[]{:S(2)}) %collective-permute-start.12) | collective-permute-done | bytes 262176 | tf_op jit(solution)/shard_map/ppermute | solution.py:606
  56.2 0.0 collective-permute-done.13.cross
  56.2 1.2 %shard_map.75 = f32[2,320,320]{2,1,0:T(8,128)} custom-call(f32[2,320,320]{2,1,0:T(8,128)S(1)} %copy-done.1, f32[2,320,320]{2,1,0:T(8,128)S(1)} %get-tuple-element.39.own, f32[320,320]{1,0:T(8,128)S(1)} %shard_map.72.weight, f32[2,320,128]{2,1,0:T(8,128)S(1)} %collective-permute-done.8.xedge, f32[2,320,128]{2,1,0:T(8,128)S(1)} %collective-permute-done.9.dedge, ...), custom_call_target="tpu_custom_call" | custom-call | tf_op jit(solution)/shard_map/pallas_call | solution.py:31
Async XLA Ops:
  0.0 1.3 %copy-start = (f32[2,320,320]{2,1,0:T(8,128)S(1)}, f32[2,320,320]{2,1,0:T(8,128)}, u32[]{:S(2)}) copy-start(f32[2,320,320]{2,1,0:T(8,128)} %obj.9) | copy-start | bytes 2457604
  2.0 22.1 %collective-permute-start.4 = (f32[648,128]{1,0:T(8,128)S(1)}, f32[648,128]{1,0:T(8,128)S(1)}, u32[]{:S(2)}, u32[]{:S(2)}) collective-permute-start(f32[648,128]{1,0:T(8,128)S(1)} %get-tuple-element.33), channel_id=1, source_target_pairs={{0,0},{1,2},{2,1},{3,3},{4,4},{5,6},{6,5},{7,7},{8,8},{9,10},{10,9... | collective-permute-start | bytes 995336 | tf_op jit(solution)/shard_map/ppermute | solution.py:606
  2.7 21.2 %collective-permute-start.6 = (f32[648,128]{1,0:T(8,128)S(1)}, f32[648,128]{1,0:T(8,128)S(1)}, u32[]{:S(2)}, u32[]{:S(2)}) collective-permute-start(f32[648,128]{1,0:T(8,128)S(1)} %get-tuple-element.34), channel_id=1, source_target_pairs={{0,1},{1,0},{2,3},{3,2},{4,5},{5,4},{6,7},{7,6},{8,9},{9,8},{10,11... | collective-permute-start | bytes 995336 | tf_op jit(solution)/shard_map/ppermute | solution.py:606
  7.1 19.8 %copy-start.3 = (s32[1,1,1,512,512]{4,3,2,1,0:T(8,128)S(1)}, s32[1,1,1,512,512]{4,3,2,1,0:T(8,128)}, u32[]{:S(2)}) copy-start(s32[1,1,1,512,512]{4,3,2,1,0:T(8,128)} %param.9) | copy-start | bytes 3145732
  8.3 18.6 %copy-start.2 = (f32[2,512,512]{2,1,0:T(8,128)S(1)}, f32[2,512,512]{2,1,0:T(8,128)}, u32[]{:S(2)}) copy-start(f32[2,512,512]{2,1,0:T(8,128)} %probe.3) | copy-start | bytes 6291460
  8.3 3.1 %collective-permute-start.1 = (f32[520,128]{1,0:T(8,128)S(1)}, f32[520,128]{1,0:T(8,128)S(1)}, u32[]{:S(2)}, u32[]{:S(2)}) collective-permute-start(f32[520,128]{1,0:T(8,128)S(1)} %get-tuple-element.30), channel_id=1, source_target_pairs={{0,1},{1,0},{2,3},{3,2},{4,8},{5,9},{6,10},{7,11},{8,4},{9,5},{10,... | collective-permute-start | bytes 798728 | tf_op jit(solution)/shard_map/ppermute | solution.py:606
  8.4 15.4 %collective-permute-start = (f32[520,128]{1,0:T(8,128)S(1)}, f32[520,128]{1,0:T(8,128)S(1)}, u32[]{:S(2)}, u32[]{:S(2)}) collective-permute-start(f32[520,128]{1,0:T(8,128)S(1)} %get-tuple-element.29), channel_id=1, source_target_pairs={{0,4},{1,5},{2,6},{3,7},{4,0},{5,1},{6,2},{7,3},{8,12},{9,13},{10,... | collective-permute-start | bytes 798728 | tf_op jit(solution)/shard_map/ppermute | solution.py:606
  11.5 18.5 %collective-permute-start.3 = (f32[128,128]{1,0:T(8,128)S(1)}, f32[128,128]{1,0:T(8,128)S(1)}, u32[]{:S(2)}, u32[]{:S(2)}) collective-permute-start(f32[128,128]{1,0:T(8,128)S(1)} %get-tuple-element.32), channel_id=1, source_target_pairs={{0,1},{1,0},{2,3},{3,2},{4,8},{5,9},{6,10},{7,11},{8,4},{9,5},{10,... | collective-permute-start | bytes 196616 | tf_op jit(solution)/shard_map/ppermute | solution.py:606
  11.5 18.5 %collective-permute-start.2 = (f32[128,128]{1,0:T(8,128)S(1)}, f32[128,128]{1,0:T(8,128)S(1)}, u32[]{:S(2)}, u32[]{:S(2)}) collective-permute-start(f32[128,128]{1,0:T(8,128)S(1)} %get-tuple-element.31), channel_id=1, source_target_pairs={{0,4},{1,5},{2,6},{3,7},{4,0},{5,1},{6,2},{7,3},{8,12},{9,13},{10,... | collective-permute-start | bytes 196616 | tf_op jit(solution)/shard_map/ppermute | solution.py:606
  24.0 5.9 %collective-permute-start.7 = (f32[408,128]{1,0:T(8,128)S(1)}, f32[408,128]{1,0:T(8,128)S(1)}, u32[]{:S(2)}, u32[]{:S(2)}) collective-permute-start(f32[408,128]{1,0:T(8,128)S(1)} %shard_map.68), channel_id=1, source_target_pairs={{0,1},{1,0},{2,3},{3,2},{4,5},{5,4},{6,7},{7,6},{8,9},{9,8},{10,11... | collective-permute-start | bytes 626696 | tf_op jit(solution)/shard_map/ppermute | solution.py:606
  24.3 6.4 %collective-permute-start.5 = (f32[408,128]{1,0:T(8,128)S(1)}, f32[408,128]{1,0:T(8,128)S(1)}, u32[]{:S(2)}, u32[]{:S(2)}) collective-permute-start(f32[408,128]{1,0:T(8,128)S(1)} %shard_map.67), channel_id=1, source_target_pairs={{0,8},{1,2},{2,1},{3,11},{4,12},{5,6},{6,5},{7,15},{8,0},{9,10},{1... | collective-permute-start | bytes 626696 | tf_op jit(solution)/shard_map/ppermute | solution.py:606
  26.9 1.8 %copy-start.1 = (f32[2,320,320]{2,1,0:T(8,128)S(1)}, f32[2,320,320]{2,1,0:T(8,128)}, u32[]{:S(2)}) copy-start(f32[2,320,320]{2,1,0:T(8,128)} %obj.9) | copy-start | bytes 2457604
  26.9 1.8 %copy-start.4 = (bf16[8,256,256]{2,1,0:T(8,128)(2,1)S(1)}, bf16[8,256,256]{2,1,0:T(8,128)(2,1)}, u32[]{:S(2)}) copy-start(bf16[8,256,256]{2,1,0:T(8,128)(2,1)} %constant.4.clone.high) | copy-start | bytes 3145732
  26.9 1.8 %copy-start.5 = (bf16[8,256,256]{2,1,0:T(8,128)(2,1)S(1)}, bf16[8,256,256]{2,1,0:T(8,128)(2,1)}, u32[]{:S(2)}) copy-start(bf16[8,256,256]{2,1,0:T(8,128)(2,1)} %constant.5.clone.low) | copy-start | bytes 3145732
  34.4 5.8 %collective-permute-start.10 = (f32[2,192,128]{2,1,0:T(8,128)S(1)}, f32[2,192,128]{2,1,0:T(8,128)S(1)}, u32[]{:S(2)}, u32[]{:S(2)}) collective-permute-start(f32[2,192,128]{2,1,0:T(8,128)S(1)} %get-tuple-element.45), channel_id=1, source_target_pairs={{0,8},{1,2},{2,1},{3,11},{4,12},{5,6},{6,5},{7,15},{8,0},{9,10},{1... | collective-permute-start | bytes 589832 | tf_op jit(solution)/shard_map/ppermute | solution.py:606
  36.5 5.3 %collective-permute-start.11 = (f32[2,192,128]{2,1,0:T(8,128)S(1)}, f32[2,192,128]{2,1,0:T(8,128)S(1)}, u32[]{:S(2)}, u32[]{:S(2)}) collective-permute-start(f32[2,192,128]{2,1,0:T(8,128)S(1)} %get-tuple-element.46), channel_id=1, source_target_pairs={{0,1},{1,0},{2,3},{3,2},{4,5},{5,4},{6,7},{7,6},{8,9},{9,8},{10,11... | collective-permute-start | bytes 589832 | tf_op jit(solution)/shard_map/ppermute | solution.py:606
  36.7 8.1 %collective-permute-start.14 = (f32[128,128]{1,0:T(8,128)S(1)}, f32[128,128]{1,0:T(8,128)S(1)}, u32[]{:S(2)}, u32[]{:S(2)}) collective-permute-start(f32[128,128]{1,0:T(8,128)S(1)} %get-tuple-element.49), channel_id=1, source_target_pairs={{0,4},{1,5},{2,6},{3,7},{4,0},{5,1},{6,2},{7,3},{8,12},{9,13},{10,... | collective-permute-start | bytes 196616 | tf_op jit(solution)/shard_map/ppermute | solution.py:606
  38.3 9.1 %collective-permute-start.15 = (f32[128,128]{1,0:T(8,128)S(1)}, f32[128,128]{1,0:T(8,128)S(1)}, u32[]{:S(2)}, u32[]{:S(2)}) collective-permute-start(f32[128,128]{1,0:T(8,128)S(1)} %get-tuple-element.50), channel_id=1, source_target_pairs={{0,1},{1,0},{2,3},{3,2},{4,8},{5,9},{6,10},{7,11},{8,4},{9,5},{10,... | collective-permute-start | bytes 196616 | tf_op jit(solution)/shard_map/ppermute | solution.py:606
  39.5 7.9 %collective-permute-start.8 = (f32[2,320,128]{2,1,0:T(8,128)S(1)}, f32[2,320,128]{2,1,0:T(8,128)S(1)}, u32[]{:S(2)}, u32[]{:S(2)}) collective-permute-start(f32[2,320,128]{2,1,0:T(8,128)S(1)} %get-tuple-element.40), channel_id=1, source_target_pairs={{0,0},{1,2},{2,1},{3,3},{4,4},{5,6},{6,5},{7,7},{8,8},{9,10},{10,9... | collective-permute-start | bytes 983048 | tf_op jit(solution)/shard_map/ppermute | solution.py:606
  40.2 7.2 %collective-permute-start.9 = (f32[2,320,128]{2,1,0:T(8,128)S(1)}, f32[2,320,128]{2,1,0:T(8,128)S(1)}, u32[]{:S(2)}, u32[]{:S(2)}) collective-permute-start(f32[2,320,128]{2,1,0:T(8,128)S(1)} %get-tuple-element.41), channel_id=1, source_target_pairs={{0,1},{1,0},{2,3},{3,2},{4,5},{5,4},{6,7},{7,6},{8,9},{9,8},{10,11... | collective-permute-start | bytes 983048 | tf_op jit(solution)/shard_map/ppermute | solution.py:606
  42.0 14.2 %collective-permute-start.12 = (f32[512,128]{1,0:T(8,128)S(1)}, f32[512,128]{1,0:T(8,128)S(1)}, u32[]{:S(2)}, u32[]{:S(2)}) collective-permute-start(f32[512,128]{1,0:T(8,128)S(1)} %get-tuple-element.47), channel_id=1, source_target_pairs={{0,4},{1,5},{2,6},{3,7},{4,0},{5,1},{6,2},{7,3},{8,12},{9,13},{10,... | collective-permute-start | bytes 786440 | tf_op jit(solution)/shard_map/ppermute | solution.py:606
  44.9 11.4 %collective-permute-start.13 = (f32[512,128]{1,0:T(8,128)S(1)}, f32[512,128]{1,0:T(8,128)S(1)}, u32[]{:S(2)}, u32[]{:S(2)}) collective-permute-start(f32[512,128]{1,0:T(8,128)S(1)} %get-tuple-element.48), channel_id=1, source_target_pairs={{0,1},{1,0},{2,3},{3,2},{4,8},{5,9},{6,10},{7,11},{8,4},{9,5},{10,... | collective-permute-start | bytes 786440 | tf_op jit(solution)/shard_map/ppermute | solution.py:606
